TPU v7x, 32 devices: a whole 2x2x4 slice. The times are simulated.
32 devices in a mesh: sub: 32 (over z, y, x, core).
Axes of the slice: x: 2, y: 2, z: 4, core: 2. Of those that a mesh axis runs over, the one named last changes fastest.
Arguments:
- right_side: float32 [128, 128, 512], P('sub'), may hold values from -8 to 8
- sigma: float32 [128, 128, 512], P('sub'), may hold values from 0.25 to 2
- wind: float32 [128, 128, 512], P('sub'), may hold values from -0.8 to 0.8
- local_inverse: float32 [32, 512, 512], P('sub'), may hold values from -1 to 2, as said below
- basis_y: float32 [128, 32], replicated, may hold values from -0.5 to 0.5
- basis_z: float32 [512, 64], replicated, may hold values from -0.25 to 0.25
- gamma: float32 [5, 32, 64], replicated, may hold values from 0.3 to 3
Outputs:
- solution_field: float32 [128, 128, 512], P('sub')
- residual: float32 [128, 128, 512], P('sub')
Inputs may be any that keep to these rules, and one draw needn't show every extreme that they name: `local_inverse`: each block is the identity plus a perturbation whose entries lie within 2/sqrt(512) of zero; each row of the perturbation has norm about one half.
All inputs are finite; a program needn't handle non-finite values.
Results may differ from a plain program's by a relative error of at most 0.00022.
Values sent between devices are 32-bit elements; how exact they have to be, the bound alone decides.
No kernel may reach another device: no remote copies, remote signals or barrier semaphores. Data moves between devices by JAX's collectives and lax.ppermute only.
A program may use at most 64 MiB of HBM per device.

v0:
```python
import jax
import jax.numpy as jnp
from jax import lax
from jax.sharding import PartitionSpec as P

HIGH = lax.Precision.HIGHEST


def extended(cells, sides, width):
    for axis, dim in sides:
        count = lax.axis_size(axis)
        ends = count - 1
        head = lax.slice_in_dim(cells, 0, width, axis=dim)
        tail = lax.slice_in_dim(cells, cells.shape[dim] - width, cells.shape[dim], axis=dim)
        cells = jnp.concatenate(
            [
                lax.ppermute(tail, axis, [(i, (i + 1) % count) for i in range(ends)]),
                cells,
                lax.ppermute(head, axis, [((i + 1) % count, i) for i in range(ends)]),
            ],
            axis=dim,
        )
    return cells


def swapped(block, axis, apart):
    count = lax.axis_size(axis)
    route = []
    for low in range(count):
        high = low | 1 << apart
        if high != low and high < count:
            route += [(low, high), (high, low)]
    return lax.ppermute(block, axis, route)


def apply_operator(field, sigma, wind):
    padded_x = extended(field, (("sub", 0),), 1)
    upper = padded_x[2:]
    lower = padded_x[:-2]
    padded_y = jnp.pad(field, ((0, 0), (1, 1), (0, 0)))
    padded_z = jnp.pad(field, ((0, 0), (0, 0), (1, 1)))
    beside = (
        upper
        + lower
        + padded_y[:, 2:]
        + padded_y[:, :-2]
        + padded_z[:, :, 2:]
        + padded_z[:, :, :-2]
    )
    return (6.0 + sigma) * field - beside + wind * (upper - lower)


def precondition(field, local_inverse, basis_y, basis_z, gamma):
    layers, rows, depth = field.shape
    local = jnp.dot(field.reshape(layers * rows, depth), local_inverse[0], precision=HIGH).reshape(
        layers, rows, depth
    )
    summed = jnp.sum(field, axis=0)
    proj = jnp.dot(basis_y.T, jnp.dot(summed, basis_z, precision=HIGH), precision=HIGH)
    levels = lax.axis_size("sub").bit_length() - 1
    coarse = jnp.zeros_like(proj)
    for level in range(levels):
        partial_sum = proj
        for which in range(level + 1):
            partial_sum = partial_sum + swapped(partial_sum, "sub", which)
        coarse = coarse + gamma[level] * partial_sum / jnp.sqrt(
            jnp.float32(layers * 2 ** (level + 1))
        )
    spread = jnp.dot(basis_y, jnp.dot(coarse, basis_z.T, precision=HIGH), precision=HIGH)
    return local + spread[None]


def orthogonal_step(image, vectors):
    products = [jnp.sum(vector * image) for vector in vectors]
    sums = lax.psum(jnp.stack(products + [jnp.sum(image * image)]), "sub")
    squares = sums[len(vectors)]
    for index in range(len(vectors)):
        image = image - sums[index] * vectors[index]
        squares = squares - sums[index] * sums[index]
    length = jnp.sqrt(squares)
    return (sums, image, length)


def on_device(right_side, sigma, wind, local_inverse, basis_y, basis_z, gamma):
    beta = jnp.sqrt(lax.psum(jnp.sum(right_side * right_side), "sub"))
    first = right_side / beta
    z_one = precondition(first, local_inverse, basis_y, basis_z, gamma)
    image = apply_operator(z_one, sigma, wind)
    sums, image, h21 = orthogonal_step(image, [first])
    h11 = sums[0]
    second = image / h21
    z_two = precondition(second, local_inverse, basis_y, basis_z, gamma)
    image = apply_operator(z_two, sigma, wind)
    sums, image, h32 = orthogonal_step(image, [first, second])
    h12 = sums[0]
    h22 = sums[1]
    m11 = h11 * h11 + h21 * h21
    m12 = h11 * h12 + h21 * h22
    m22 = h12 * h12 + h22 * h22 + h32 * h32
    q_one = h11 * beta
    q_two = h12 * beta
    determ = m11 * m22 - m12 * m12
    y_one = (m22 * q_one - m12 * q_two) / determ
    y_two = (m11 * q_two - m12 * q_one) / determ
    solution_field = y_one * z_one + y_two * z_two
    residual = right_side - apply_operator(solution_field, sigma, wind)
    return (solution_field, residual)


def solution(mesh):
    placed = (
        P("sub", None, None),
        P("sub", None, None),
        P("sub", None, None),
        P("sub", None, None),
        P(),
        P(),
        P(),
    )
    return jax.shard_map(
        on_device,
        mesh=mesh,
        in_specs=placed,
        out_specs=(P("sub", None, None), P("sub", None, None)),
        check_vma=False,
    )
```

profile of v0, /device:TPU:8, one launch (start us, length us, event | category | flops | bytes accessed | tf_op | source)
XLA Modules:
  0.0 225.6 jit_solution(12309424426258021769)
XLA Ops:
  0.7 2.2 multiply_reduce_fusion.5
  2.9 40.6 %psum.21 = f32[]{:T(128)} all-reduce(f32[]{:T(128)} %multiply_reduce_fusion.5), channel_id=1, replica_groups=mesh['sub'=32] {'sub'}, use_global_device_ids=true, to_apply=%region_1.0 | all-reduce | flops 1 | bytes 8 | tf_op jit(solution)/shard_map/psum | solution.py:85
  45.0 1.2 collective-permute-done
  46.2 2.3 %collective-permute-start.1 = (f32[32,64]{1,0:T(8,128)S(1)}, f32[32,64]{1,0:T(8,128)S(1)}, u32[]{:S(2)}, u32[]{:S(2)}) collective-permute-start(f32[32,64]{1,0:T(8,128)S(1)} %add.183), channel_id=1, source_target_pairs={{0,2},{2,0},{1,3},{3,1},{4,6},{6,4},{5,7},{7,5},{8,10},{10,8},{9,1... | collective-permute-start | bytes 24584 | tf_op jit(solution)/shard_map/ppermute | solution.py:33
  48.5 1.7 collective-permute-done.1
  50.2 2.2 collective-permute-start.2
  52.4 1.7 collective-permute-done.2
  54.6 3.2 %collective-permute-done.3 = f32[32,64]{1,0:T(8,128)S(1)} collective-permute-done((f32[32,64]{1,0:T(8,128)S(1)}, f32[32,64]{1,0:T(8,128)S(1)}, u32[]{:S(2)}, u32[]{:S(2)}) %collective-permute-start.3) | collective-permute-done | bytes 8224 | tf_op jit(solution)/shard_map/ppermute | solution.py:33
  57.8 1.3 collective-permute-start.4
  59.1 3.4 %collective-permute-done.4 = f32[32,64]{1,0:T(8,128)S(1)} collective-permute-done((f32[32,64]{1,0:T(8,128)S(1)}, f32[32,64]{1,0:T(8,128)S(1)}, u32[]{:S(2)}, u32[]{:S(2)}) %collective-permute-start.4) | collective-permute-done | bytes 8224 | tf_op jit(solution)/shard_map/ppermute | solution.py:33
  62.5 1.0 fusion.23
  63.5 0.6 convolution_bitcast_fusion.1
  64.2 1.9 convolution_add_fusion.1
  66.2 2.1 collective-permute-start.5
  68.3 2.4 %collective-permute-start.6 = (f32[1,128,512]{2,1,0:T(8,128)S(1)}, f32[1,128,512]{2,1,0:T(8,128)S(1)}, u32[]{:S(2)}, u32[]{:S(2)}) collective-permute-start(f32[1,128,512]{2,1,0:T(8,128)S(1)} %get-tuple-element.15), channel_id=1, source_target_pairs={{0,1},{1,2},{2,3},{3,4},{4,5},{5,6},{6,7},{7,8},{8,9},{9,10},{10,1... | collective-permute-start | bytes 786440 | tf_op jit(solution)/shard_map/ppermute | solution.py:17
  70.7 1.5 collective-permute-done.5
  72.1 5.6 %collective-permute-done.6 = f32[1,128,512]{2,1,0:T(8,128)S(1)} collective-permute-done((f32[1,128,512]{2,1,0:T(8,128)S(1)}, f32[1,128,512]{2,1,0:T(8,128)S(1)}, u32[]{:S(2)}, u32[]{:S(2)}) %collective-permute-start.6) | collective-permute-done | bytes 262176 | tf_op jit(solution)/shard_map/ppermute | solution.py:17
  77.8 1.5 multiply_reduce_fusion.4
  79.3 1.4 pad_maximum_fusion.6
  80.7 38.1 %psum.22 = f32[2]{0:T(128)S(1)} all-reduce(f32[2]{0:T(128)S(1)} %pad_maximum_fusion.6), channel_id=1, replica_groups=mesh['sub'=32] {'sub'}, use_global_device_ids=true, to_apply=%region_5.6 | all-reduce | flops 2 | bytes 16 | tf_op jit(solution)/shard_map/psum | solution.py:75
  121.3 1.9 fusion.84
  123.8 1.2 collective-permute-done.7
  125.0 2.3 %collective-permute-start.8 = (f32[32,64]{1,0:T(8,128)S(1)}, f32[32,64]{1,0:T(8,128)S(1)}, u32[]{:S(2)}, u32[]{:S(2)}) collective-permute-start(f32[32,64]{1,0:T(8,128)S(1)} %add.200), channel_id=1, source_target_pairs={{0,2},{2,0},{1,3},{3,1},{4,6},{6,4},{5,7},{7,5},{8,10},{10,8},{9,1... | collective-permute-start | bytes 24584 | tf_op jit(solution)/shard_map/ppermute | solution.py:33
  127.2 1.7 collective-permute-done.8
  129.0 2.0 collective-permute-start.9
  131.0 1.7 collective-permute-done.9
  132.7 1.6 collective-permute-start.10
  134.3 2.1 collective-permute-done.10
  136.4 2.4 %collective-permute-start.11 = (f32[32,64]{1,0:T(8,128)S(1)}, f32[32,64]{1,0:T(8,128)S(1)}, u32[]{:S(2)}, u32[]{:S(2)}) collective-permute-start(f32[32,64]{1,0:T(8,128)S(1)} %add.205), channel_id=1, source_target_pairs={{0,16},{16,0},{1,17},{17,1},{2,18},{18,2},{3,19},{19,3},{4,20},{20... | collective-permute-start | bytes 24584 | tf_op jit(solution)/shard_map/ppermute | solution.py:33
  138.9 2.2 collective-permute-done.11
  141.1 1.0 fusion.27
  142.1 0.6 convolution_bitcast_fusion
  142.8 3.1 %convolution_add_fusion = f32[4,128,512]{2,1,0:T(8,128)S(1)} fusion(f32[4,128,512]{2,1,0:T(8,128)} %get-tuple-element.8, f32[1,512,512]{2,1,0:T(8,128)S(1)} %copy-done, f32[128,512]{1,0:T(8,128)S(1)} %copy.10), kind=kOutput, calls=%fused_computation | convolution fusion | flops 1610874880 | bytes 3407872 | tf_op jit(solution)/shard_map/dot_general | solution.py:55
  145.9 0.7 fusion.87
  146.6 1.9 collective-permute-start.12
  148.5 2.4 %collective-permute-start.13 = (f32[1,128,512]{2,1,0:T(8,128)S(1)}, f32[1,128,512]{2,1,0:T(8,128)}, u32[]{:S(2)}, u32[]{:S(2)}) collective-permute-start(f32[1,128,512]{2,1,0:T(8,128)S(1)} %get-tuple-element.12), channel_id=1, source_target_pairs={{0,1},{1,2},{2,3},{3,4},{4,5},{5,6},{6,7},{7,8},{8,9},{9,10},{10,1... | collective-permute-start | bytes 786440 | tf_op jit(solution)/shard_map/ppermute | solution.py:17
  151.6 1.1 collective-permute-done.12
  152.7 5.9 %collective-permute-done.13 = f32[1,128,512]{2,1,0:T(8,128)} collective-permute-done((f32[1,128,512]{2,1,0:T(8,128)S(1)}, f32[1,128,512]{2,1,0:T(8,128)}, u32[]{:S(2)}, u32[]{:S(2)}) %collective-permute-start.13) | collective-permute-done | bytes 262176 | tf_op jit(solution)/shard_map/ppermute | solution.py:17
  158.6 3.5 %multiply_reduce_fusion.2 = (f32[]{:T(128)}, f32[]{:T(128)}, f32[]{:T(128)}) fusion(f32[4,128,512]{2,1,0:T(8,128)S(1)} %copy-done.1, f32[]{:T(128)S(6)} %sqrt.9, f32[4,128,512]{2,1,0:T(8,128)} %get-tuple-element.8, f32[4,128,512]{2,1,0:T(8,128)} %param.9, f32[4,128,512]{2,1,0:T(8,128)S(1)} %convolution_add_fusion, ...), kind=kLoop, calls=%fused_computation.48 | loop fusion | flops 5242877 | bytes 5767184 | tf_op jit(solution)/shard_map/reduce_sum | solution.py:74
  162.1 1.9 pad_maximum_fusion.7
  164.0 39.0 %psum.23 = f32[3]{0:T(128)S(1)} all-reduce(f32[3]{0:T(128)S(1)} %pad_maximum_fusion.7), channel_id=1, replica_groups=mesh['sub'=32] {'sub'}, use_global_device_ids=true, to_apply=%region_10.11 | all-reduce | flops 3 | bytes 24 | tf_op jit(solution)/shard_map/psum | solution.py:75
  203.0 0.6 fusion.89
  209.5 1.5 multiply_add_fusion
  211.1 3.1 %collective-permute-start.14 = (f32[1,128,512]{2,1,0:T(8,128)S(1)}, f32[1,128,512]{2,1,0:T(8,128)S(1)}, u32[]{:S(2)}, u32[]{:S(2)}) collective-permute-start(f32[1,128,512]{2,1,0:T(8,128)S(1)} %get-tuple-element.11), channel_id=1, source_target_pairs={{1,0},{2,1},{3,2},{4,3},{5,4},{6,5},{7,6},{8,7},{9,8},{10,9},{11,1... | collective-permute-start | bytes 786440 | tf_op jit(solution)/shard_map/ppermute | solution.py:19
  214.2 1.9 collective-permute-start.15
  216.1 1.9 collective-permute-done.14
  218.0 5.6 %collective-permute-done.15 = f32[1,128,512]{2,1,0:T(8,128)S(1)} collective-permute-done((f32[1,128,512]{2,1,0:T(8,128)S(1)}, f32[1,128,512]{2,1,0:T(8,128)S(1)}, u32[]{:S(2)}, u32[]{:S(2)}) %collective-permute-start.15) | collective-permute-done | bytes 262176 | tf_op jit(solution)/shard_map/ppermute | solution.py:17
  223.7 1.9 fusion.18
  (41 shorter events, 2.8 us)
Async XLA Ops:
  0.6 63.6 %copy-start = (f32[1,512,512]{2,1,0:T(8,128)S(1)}, f32[1,512,512]{2,1,0:T(8,128)}, u32[]{:S(2)}) copy-start(f32[1,512,512]{2,1,0:T(8,128)} %param.10) | copy-start | bytes 3145732
  0.6 43.6 %copy-start.1 = (f32[4,128,512]{2,1,0:T(8,128)S(1)}, f32[4,128,512]{2,1,0:T(8,128)}, u32[]{:S(2)}) copy-start(f32[4,128,512]{2,1,0:T(8,128)} %param.7) | copy-start | bytes 3145732
  0.7 43.7 %copy-start.8 = (f32[512,64]{0,1:T(8,128)S(1)}, f32[512,64]{0,1:T(8,128)}, u32[]{:S(2)}) copy-start(f32[512,64]{0,1:T(8,128)} %param.12) | copy-start | bytes 393220
  2.9 41.8 %copy-start.9 = (f32[128,32]{0,1:T(8,128)S(1)}, f32[128,32]{0,1:T(8,128)}, u32[]{:S(2)}) copy-start(f32[128,32]{0,1:T(8,128)} %param.11) | copy-start | bytes 49156
  44.9 1.2 collective-permute-start
  46.2 4.0 %collective-permute-start.1 = (f32[32,64]{1,0:T(8,128)S(1)}, f32[32,64]{1,0:T(8,128)S(1)}, u32[]{:S(2)}, u32[]{:S(2)}) collective-permute-start(f32[32,64]{1,0:T(8,128)S(1)} %add.183), channel_id=1, source_target_pairs={{0,2},{2,0},{1,3},{3,1},{4,6},{6,4},{5,7},{7,5},{8,10},{10,8},{9,1... | collective-permute-start | bytes 24584 | tf_op jit(solution)/shard_map/ppermute | solution.py:33
  50.2 3.9 %collective-permute-start.2 = (f32[32,64]{1,0:T(8,128)S(1)}, f32[32,64]{1,0:T(8,128)S(1)}, u32[]{:S(2)}, u32[]{:S(2)}) collective-permute-start(f32[32,64]{1,0:T(8,128)S(1)} %add.184), channel_id=1, source_target_pairs={{0,4},{4,0},{1,5},{5,1},{2,6},{6,2},{3,7},{7,3},{8,12},{12,8},{9,1... | collective-permute-start | bytes 24584 | tf_op jit(solution)/shard_map/ppermute | solution.py:33
  54.1 3.7 %collective-permute-start.3 = (f32[32,64]{1,0:T(8,128)S(1)}, f32[32,64]{1,0:T(8,128)S(1)}, u32[]{:S(2)}, u32[]{:S(2)}) collective-permute-start(f32[32,64]{1,0:T(8,128)S(1)} %add.186), channel_id=1, source_target_pairs={{0,8},{8,0},{1,9},{9,1},{2,10},{10,2},{3,11},{11,3},{4,12},{12,4},... | collective-permute-start | bytes 24584 | tf_op jit(solution)/shard_map/ppermute | solution.py:33
  57.8 4.6 %collective-permute-start.4 = (f32[32,64]{1,0:T(8,128)S(1)}, f32[32,64]{1,0:T(8,128)S(1)}, u32[]{:S(2)}, u32[]{:S(2)}) collective-permute-start(f32[32,64]{1,0:T(8,128)S(1)} %add.188), channel_id=1, source_target_pairs={{0,16},{16,0},{1,17},{17,1},{2,18},{18,2},{3,19},{19,3},{4,20},{20... | collective-permute-start | bytes 24584 | tf_op jit(solution)/shard_map/ppermute | solution.py:33
  64.2 13.5 %copy-start.4 = (f32[4,128,512]{2,1,0:T(8,128)S(1)}, f32[4,128,512]{2,1,0:T(8,128)}, u32[]{:S(2)}) copy-start(f32[4,128,512]{2,1,0:T(8,128)} %param.8) | copy-start | bytes 3145732
  66.1 13.2 %copy-start.6 = (f32[4,128,512]{2,1,0:T(8,128)}, f32[4,128,512]{2,1,0:T(8,128)S(1)}, u32[]{:S(2)}) copy-start(f32[4,128,512]{2,1,0:T(8,128)S(1)} %convolution_add_fusion.1) | copy-start | bytes 3145732
  66.2 11.6 %copy-start.2 = (f32[4,128,512]{2,1,0:T(8,128)S(1)}, f32[4,128,512]{2,1,0:T(8,128)}, u32[]{:S(2)}) copy-start(f32[4,128,512]{2,1,0:T(8,128)} %param.9) | copy-start | bytes 3145732
  66.2 5.9 %collective-permute-start.5 = (f32[1,128,512]{2,1,0:T(8,128)S(1)}, f32[1,128,512]{2,1,0:T(8,128)S(1)}, u32[]{:S(2)}, u32[]{:S(2)}) collective-permute-start(f32[1,128,512]{2,1,0:T(8,128)S(1)} %get-tuple-element.14), channel_id=1, source_target_pairs={{1,0},{2,1},{3,2},{4,3},{5,4},{6,5},{7,6},{8,7},{9,8},{10,9},{11,1... | collective-permute-start | bytes 786440 | tf_op jit(solution)/shard_map/ppermute | solution.py:19
  68.3 9.5 %collective-permute-start.6 = (f32[1,128,512]{2,1,0:T(8,128)S(1)}, f32[1,128,512]{2,1,0:T(8,128)S(1)}, u32[]{:S(2)}, u32[]{:S(2)}) collective-permute-start(f32[1,128,512]{2,1,0:T(8,128)S(1)} %get-tuple-element.15), channel_id=1, source_target_pairs={{0,1},{1,2},{2,3},{3,4},{4,5},{5,6},{6,7},{7,8},{8,9},{9,10},{10,1... | collective-permute-start | bytes 786440 | tf_op jit(solution)/shard_map/ppermute | solution.py:17
  123.7 1.2 collective-permute-start.7
  125.0 4.0 %collective-permute-start.8 = (f32[32,64]{1,0:T(8,128)S(1)}, f32[32,64]{1,0:T(8,128)S(1)}, u32[]{:S(2)}, u32[]{:S(2)}) collective-permute-start(f32[32,64]{1,0:T(8,128)S(1)} %add.200), channel_id=1, source_target_pairs={{0,2},{2,0},{1,3},{3,1},{4,6},{6,4},{5,7},{7,5},{8,10},{10,8},{9,1... | collective-permute-start | bytes 24584 | tf_op jit(solution)/shard_map/ppermute | solution.py:33
  129.0 3.7 %collective-permute-start.9 = (f32[32,64]{1,0:T(8,128)S(1)}, f32[32,64]{1,0:T(8,128)S(1)}, u32[]{:S(2)}, u32[]{:S(2)}) collective-permute-start(f32[32,64]{1,0:T(8,128)S(1)} %add.201), channel_id=1, source_target_pairs={{0,4},{4,0},{1,5},{5,1},{2,6},{6,2},{3,7},{7,3},{8,12},{12,8},{9,1... | collective-permute-start | bytes 24584 | tf_op jit(solution)/shard_map/ppermute | solution.py:33
  132.7 3.7 %collective-permute-start.10 = (f32[32,64]{1,0:T(8,128)S(1)}, f32[32,64]{1,0:T(8,128)S(1)}, u32[]{:S(2)}, u32[]{:S(2)}) collective-permute-start(f32[32,64]{1,0:T(8,128)S(1)} %add.203), channel_id=1, source_target_pairs={{0,8},{8,0},{1,9},{9,1},{2,10},{10,2},{3,11},{11,3},{4,12},{12,4},... | collective-permute-start | bytes 24584 | tf_op jit(solution)/shard_map/ppermute | solution.py:33
  136.4 4.6 %collective-permute-start.11 = (f32[32,64]{1,0:T(8,128)S(1)}, f32[32,64]{1,0:T(8,128)S(1)}, u32[]{:S(2)}, u32[]{:S(2)}) collective-permute-start(f32[32,64]{1,0:T(8,128)S(1)} %add.205), channel_id=1, source_target_pairs={{0,16},{16,0},{1,17},{17,1},{2,18},{18,2},{3,19},{19,3},{4,20},{20... | collective-permute-start | bytes 24584 | tf_op jit(solution)/shard_map/ppermute | solution.py:33
  146.6 6.1 %collective-permute-start.12 = (f32[1,128,512]{2,1,0:T(8,128)}, f32[1,128,512]{2,1,0:T(8,128)}, u32[]{:S(2)}, u32[]{:S(2)}) collective-permute-start(f32[1,128,512]{2,1,0:T(8,128)} %get-tuple-element.13), channel_id=1, source_target_pairs={{1,0},{2,1},{3,2},{4,3},{5,4},{6,5},{7,6},{8,7},{9,8},{10,9},{11,1... | collective-permute-start | bytes 786440 | tf_op jit(solution)/shard_map/ppermute | solution.py:19
  148.5 10.0 %collective-permute-start.13 = (f32[1,128,512]{2,1,0:T(8,128)S(1)}, f32[1,128,512]{2,1,0:T(8,128)}, u32[]{:S(2)}, u32[]{:S(2)}) collective-permute-start(f32[1,128,512]{2,1,0:T(8,128)S(1)} %get-tuple-element.12), channel_id=1, source_target_pairs={{0,1},{1,2},{2,3},{3,4},{4,5},{5,6},{6,7},{7,8},{8,9},{9,10},{10,1... | collective-permute-start | bytes 786440 | tf_op jit(solution)/shard_map/ppermute | solution.py:17
  209.5 14.2 %copy-start.5 = (f32[4,128,512]{2,1,0:T(8,128)S(1)}, f32[4,128,512]{2,1,0:T(8,128)}, u32[]{:S(2)}) copy-start(f32[4,128,512]{2,1,0:T(8,128)} %param.8) | copy-start | bytes 3145732
  211.0 14.5 %copy-start.7 = (f32[4,128,512]{2,1,0:T(8,128)}, f32[4,128,512]{2,1,0:T(8,128)S(1)}, u32[]{:S(2)}) copy-start(f32[4,128,512]{2,1,0:T(8,128)S(1)} %multiply_add_fusion) | copy-start | bytes 3145732
  211.0 12.6 %copy-start.3 = (f32[4,128,512]{2,1,0:T(8,128)S(1)}, f32[4,128,512]{2,1,0:T(8,128)}, u32[]{:S(2)}) copy-start(f32[4,128,512]{2,1,0:T(8,128)} %param.9) | copy-start | bytes 3145732
  211.1 7.0 %collective-permute-start.14 = (f32[1,128,512]{2,1,0:T(8,128)S(1)}, f32[1,128,512]{2,1,0:T(8,128)S(1)}, u32[]{:S(2)}, u32[]{:S(2)}) collective-permute-start(f32[1,128,512]{2,1,0:T(8,128)S(1)} %get-tuple-element.11), channel_id=1, source_target_pairs={{1,0},{2,1},{3,2},{4,3},{5,4},{6,5},{7,6},{8,7},{9,8},{10,9},{11,1... | collective-permute-start | bytes 786440 | tf_op jit(solution)/shard_map/ppermute | solution.py:19
  214.2 9.5 %collective-permute-start.15 = (f32[1,128,512]{2,1,0:T(8,128)S(1)}, f32[1,128,512]{2,1,0:T(8,128)S(1)}, u32[]{:S(2)}, u32[]{:S(2)}) collective-permute-start(f32[1,128,512]{2,1,0:T(8,128)S(1)} %get-tuple-element.10), channel_id=1, source_target_pairs={{0,1},{1,2},{2,3},{3,4},{4,5},{5,6},{6,7},{7,8},{8,9},{9,10},{10,1... | collective-permute-start | bytes 786440 | tf_op jit(solution)/shard_map/ppermute | solution.py:17
where the time goes:
time: 227 us; the launch traced here: 226 us
  blocking collectives  118 us (52%)
  waiting for transfers between devices  41.8 us (18%)
  starting transfers between devices  28.5 us (13%)
  other arithmetic  16 us (7%)
  between operations  10.1 us (4%)
  matrix products  9.18 us (4%)
  local copies, waits for them, and re-layouts  2.34 us (1%)
    psum x2, blocking collectives, orthogonal_step(): sums = lax.psum(jnp.stack(products + [jnp.sum(image * image)]), 'sub')  77 us
    psum x1, blocking collectives, on_device(): beta = jnp.sqrt(lax.psum(jnp.sum(right_side * right_side), 'sub'))  40.6 us
    ppermute x10, waiting for transfers between devices, swapped(): return lax.ppermute(block, axis, route)  20.1 us
    ppermute x3, waiting for transfers between devices, extended(): lax.ppermute(tail, axis, [(i, (i + 1) % count) for i in range(ends)])  17.1 us
    ppermute x10, starting transfers between devices, swapped(): return lax.ppermute(block, axis, route)  14.7 us
    ppermute x3, starting transfers between devices, extended(): lax.ppermute(head, axis, [((i + 1) % count, i) for i in range(ends)])  7.05 us
    ppermute x3, starting transfers between devices, extended(): lax.ppermute(tail, axis, [(i, (i + 1) % count) for i in range(ends)])  6.73 us
    reduce_sum x2, other arithmetic, orthogonal_step(): products = [jnp.sum(vector * image) for vector in vectors]  5.06 us
  transfers between devices with their start and end apart: 16, of which 16 were waited for; matrix products, arithmetic and copies ran while one was open for 0% of the time, Pallas kernels for 0%

commit v1 on v0

v1 whole, which is shorter than its diff:
```python
import functools
import jax
import jax.numpy as jnp
from jax import lax
from jax.experimental import pallas as pl
from jax.experimental.pallas import tpu as pltpu
from jax.sharding import PartitionSpec as P

F32 = jnp.float32
BF16 = jnp.bfloat16
AXIS = "sub"
LANES = 128
NN = (((1,), (0,)), ((), ()))
NT = (((1,), (1,)), ((), ()))
TN = (((0,), (0,)), ((), ()))


def halves(x):
    high = x.astype(BF16)
    return high, (x - high.astype(F32)).astype(BF16)


def dot3(left, right, dims=NN):
    lh, ll = left
    rh, rl = right
    mul = functools.partial(lax.dot_general, dimension_numbers=dims, preferred_element_type=F32)
    return mul(lh, rh) + (mul(lh, rl) + mul(ll, rh))


def fold_of(ky, kz):
    fold = max(1, LANES // kz)
    while ky % fold:
        fold //= 2
    return fold


def pack(block, fold):
    rows = block.shape[0] // fold
    return jnp.concatenate([block[i * rows : (i + 1) * rows] for i in range(fold)], axis=1)


def unpack(block, fold):
    cols = block.shape[1] // fold
    return jnp.concatenate([block[:, i * cols : (i + 1) * cols] for i in range(fold)], axis=0)


def project(summed, by, bz, fold):
    half = dot3(halves(summed), halves(bz))
    return pack(dot3(halves(by), halves(half), TN), fold)


def coarse_of(gath_ref, gamma_ref, tree_ref, rows, layers, fold, levels, count):
    below = None
    base = 0
    offsets = []
    for level in range(levels):
        size = count >> (level + 1)
        offsets.append(base)
        if level == 0:
            pairs = gath_ref[:, :rows, :].reshape(size, 2, rows, -1)
        else:
            pairs = below.reshape(size, 2, rows, -1)
        below = pairs[:, 0] + pairs[:, 1]
        tree_ref[pl.ds(base, size)] = below
        base += size
    scaled = [
        pack(gamma_ref[level], fold) * (1.0 / (layers * 2.0 ** (level + 1)) ** 0.5)
        for level in range(levels)
    ]
    me = lax.axis_index(AXIS)
    out = []
    for shift in (-1, 0, 1):
        who = jnp.clip(me + shift, 0, count - 1)
        total = scaled[0] * tree_ref[offsets[0] + (who >> 1)]
        for level in range(1, levels):
            total = total + scaled[level] * tree_ref[offsets[level] + (who >> (level + 1))]
        if shift:
            inside = (me + shift == who).astype(F32)
            total = total * inside
        out.append(unpack(total, fold))
    return out


def spreads(coarse, by, bz):
    ky = by.shape[1]
    back = dot3(halves(jnp.concatenate(coarse, axis=0)), halves(bz), NT)
    by_parts = halves(by)
    return [dot3(by_parts, halves(back[i * ky : (i + 1) * ky])) for i in range(len(coarse))]


def stencil(prev, here, after, sigma, wind):
    rows, depth = here.shape
    row = lax.broadcasted_iota(jnp.int32, here.shape, 0)
    col = lax.broadcasted_iota(jnp.int32, here.shape, 1)
    beside = (
        after
        + prev
        + jnp.where(row == rows - 1, 0.0, pltpu.roll(here, rows - 1, 0))
        + jnp.where(row == 0, 0.0, pltpu.roll(here, 1, 0))
        + jnp.where(col == depth - 1, 0.0, pltpu.roll(here, depth - 1, 1))
        + jnp.where(col == 0, 0.0, pltpu.roll(here, 1, 1))
    )
    return (6.0 + sigma) * here - beside + wind * (after - prev)


def lane_sum(x):
    total = jnp.sum(x, axis=0, keepdims=True)
    out = total[:, :LANES]
    for i in range(1, x.shape[1] // LANES):
        out = out + total[:, i * LANES : (i + 1) * LANES]
    return out


def full_sum(x):
    return jnp.sum(x, axis=(0, 1), keepdims=True)


def even_here():
    return lax.rem(lax.axis_index(AXIS), 2) == 0


def first_kernel(r_ref, by_ref, bz_ref, out_ref, *, fold):
    layers = r_ref.shape[0]
    summed = r_ref[0]
    for x in range(1, layers):
        summed = summed + r_ref[x]
    packed = project(summed, by_ref[...], bz_ref[...], fold)
    out_ref[...] = jnp.broadcast_to(packed[None], out_ref.shape)


def local_kernel(f_ref, inv_ref, local_ref, even_ref, odd_ref):
    layers, rows, depth = f_ref.shape
    inverse = halves(inv_ref[0])
    for x in range(layers):
        local_ref[x] = dot3(halves(f_ref[x]), inverse)
    even = even_here()
    even_ref[0] = local_ref[jnp.where(even, layers - 1, 0)]
    odd_ref[0] = local_ref[jnp.where(even, 0, layers - 1)]


def middle_kernel(
    gath_ref, local_ref, even_ref, odd_ref, r_ref, sigma_ref, wind_ref, by_ref, bz_ref, gamma_ref,
    z_ref, edge_ref, w_ref, out_ref, tree_ref, *, fold, levels, count, rows,
):
    layers = r_ref.shape[0]
    bz = bz_ref[...]
    by = by_ref[...]
    coarse = coarse_of(gath_ref, gamma_ref, tree_ref, rows, layers, fold, levels, count)
    before, own, after = spreads(coarse, by, bz)
    even = even_here().astype(F32)
    from_pair = even_ref[0]
    from_other = odd_ref[0]
    edge_ref[0] = before + (from_other * even + from_pair * (1.0 - even))
    edge_ref[1] = after + (from_pair * even + from_other * (1.0 - even))
    for x in range(layers):
        z_ref[x] = local_ref[x] + own
    rr = rw = ww = summed = None
    for x in range(layers):
        prev = edge_ref[0] if x == 0 else z_ref[x - 1]
        nxt = edge_ref[1] if x == layers - 1 else z_ref[x + 1]
        w = stencil(prev, z_ref[x], nxt, sigma_ref[x], wind_ref[x])
        w_ref[x] = w
        r = r_ref[x]
        parts = (lane_sum(r * r), lane_sum(r * w), lane_sum(w * w))
        if x == 0:
            rr, rw, ww = parts
            summed = w
        else:
            rr, rw, ww = rr + parts[0], rw + parts[1], ww + parts[2]
            summed = summed + w
    packed = project(summed, by, bz, fold)
    scalars = jnp.concatenate([rr, rw, ww, jnp.zeros((5, LANES), F32)], axis=0)
    out_ref[:, :rows, :] = jnp.broadcast_to(packed[None], (count,) + packed.shape)
    out_ref[:, rows:, :] = jnp.broadcast_to(scalars[None], (count,) + scalars.shape)


def first_scalars(gath_ref, rows):
    sums = jnp.sum(gath_ref[:, rows:, :], axis=0)
    rr = full_sum(sums[0:1])
    rw = full_sum(sums[1:2])
    ww = full_sum(sums[2:3])
    inv_rr = 1.0 / rr
    beta = jnp.sqrt(rr)
    h11 = rw * inv_rr
    h21 = jnp.sqrt(ww * inv_rr - h11 * h11)
    return beta, h11, h21


def last_kernel(
    gath_ref, local_ref, even_ref, odd_ref, r_ref, z_ref, edge_ref, w_ref, sigma_ref, wind_ref,
    by_ref, bz_ref, gamma_ref,
    z2_ref, u_ref, out_ref, tree_ref, edge2_ref, *, fold, levels, count, rows,
):
    layers = r_ref.shape[0]
    beta, h11, h21 = first_scalars(gath_ref, rows)
    scale = 1.0 / (h21 * beta)
    coarse = coarse_of(gath_ref, gamma_ref, tree_ref, rows, layers, fold, levels, count)
    before, own, after = spreads(coarse, by_ref[...], bz_ref[...])
    even = even_here().astype(F32)
    from_pair = even_ref[0]
    from_other = odd_ref[0]
    edge2_ref[0] = scale * (
        before + (from_other * even + from_pair * (1.0 - even)) - h11 * edge_ref[0]
    )
    edge2_ref[1] = scale * (
        after + (from_pair * even + from_other * (1.0 - even)) - h11 * edge_ref[1]
    )
    for x in range(layers):
        z2_ref[x] = scale * (local_ref[x] + own - h11 * z_ref[x])
    a = b = c = None
    for x in range(layers):
        prev = edge2_ref[0] if x == 0 else z2_ref[x - 1]
        nxt = edge2_ref[1] if x == layers - 1 else z2_ref[x + 1]
        u = stencil(prev, z2_ref[x], nxt, sigma_ref[x], wind_ref[x])
        u_ref[x] = u
        r = r_ref[x]
        v2 = scale * (w_ref[x] - h11 * r)
        parts = (lane_sum(r * u), lane_sum(v2 * u), lane_sum(u * u))
        a, b, c = parts if x == 0 else (a + parts[0], b + parts[1], c + parts[2])
    lane = lax.broadcasted_iota(jnp.int32, (1, LANES), 1)
    row = jnp.where(
        lane == 0, full_sum(a), jnp.where(lane == 1, full_sum(b), jnp.where(lane == 2, full_sum(c), 0.0))
    )
    out_ref[...] = jnp.broadcast_to(row, out_ref.shape)


def finish_kernel(
    sums_ref, gath_ref, r_ref, z_ref, w_ref, z2_ref, u_ref, sol_ref, res_ref, *, rows
):
    beta, h11, h21 = first_scalars(gath_ref, rows)
    sums = jnp.sum(sums_ref[...], axis=0, keepdims=True)
    lane = lax.broadcasted_iota(jnp.int32, sums.shape, 1)
    h12 = full_sum(jnp.where(lane == 0, sums, 0.0)) / beta
    h22 = full_sum(jnp.where(lane == 1, sums, 0.0))
    h32 = jnp.sqrt(full_sum(jnp.where(lane == 2, sums, 0.0)) - h12 * h12 - h22 * h22)
    m11 = h11 * h11 + h21 * h21
    m12 = h11 * h12 + h21 * h22
    m22 = h12 * h12 + h22 * h22 + h32 * h32
    q_one = h11 * beta
    q_two = h12 * beta
    determ = m11 * m22 - m12 * m12
    y_one = (m22 * q_one - m12 * q_two) / determ / beta
    y_two = (m11 * q_two - m12 * q_one) / determ
    for x in range(r_ref.shape[0]):
        sol_ref[x] = y_one * z_ref[x] + y_two * z2_ref[x]
        res_ref[x] = r_ref[x] - (y_one * w_ref[x] + y_two * u_ref[x])


def call(kernel, name, outs, args, scratch=(), flops=0):
    vmem = pl.BlockSpec(memory_space=pltpu.VMEM)
    return pl.pallas_call(
        kernel,
        name=name,
        out_shape=[jax.ShapeDtypeStruct(s, F32) for s in outs],
        in_specs=[vmem] * len(args),
        out_specs=[vmem] * len(outs),
        scratch_shapes=[pltpu.VMEM(s, F32) for s in scratch],
        compiler_params=pltpu.CompilerParams(vmem_limit_bytes=24 << 20),
        cost_estimate=pl.CostEstimate(flops=flops, bytes_accessed=0, transcendentals=0),
    )(*args)


def exchange(block):
    return lax.all_to_all(block, AXIS, 0, 0, tiled=True)


def on_device(right_side, sigma, wind, local_inverse, basis_y, basis_z, gamma):
    count = lax.axis_size(AXIS)
    levels = count.bit_length() - 1
    layers, ny, nz = right_side.shape
    ky, kz = basis_y.shape[1], basis_z.shape[1]
    fold = fold_of(ky, kz)
    rows, width = ky // fold, kz * fold
    field = (layers, ny, nz)
    edge = (1, ny, nz)
    pairs = [(i, i ^ 1) for i in range(count)]
    others = [(i, i + 1) for i in range(1, count - 1, 2)]
    others = others + [(j, i) for i, j in others]
    matmul = 6 * layers * ny * nz * nz
    sizes = dict(fold=fold, levels=levels, count=count, rows=rows)

    def local_of(f):
        local, even, odd = call(local_kernel, "local", [field, edge, edge], (f, local_inverse), flops=matmul)
        return local, lax.ppermute(even, AXIS, pairs), lax.ppermute(odd, AXIS, others)

    (sent,) = call(
        functools.partial(first_kernel, fold=fold), "first", [(count, rows, width)],
        (right_side, basis_y, basis_z), flops=matmul // 8,
    )
    gathered = exchange(sent)
    local, even, odd = local_of(right_side)
    tree = (count, rows, width)
    z, edges, w, sent = call(
        functools.partial(middle_kernel, **sizes), "middle",
        [field, (2, ny, nz), field, (count, rows + 8, width)],
        (gathered, local, even, odd, right_side, sigma, wind, basis_y, basis_z, gamma),
        [tree], flops=matmul,
    )
    gathered = exchange(sent)
    local, even, odd = local_of(w)
    z2, u, sent = call(
        functools.partial(last_kernel, **sizes), "last",
        [field, field, (count, LANES)],
        (gathered, local, even, odd, right_side, z, edges, w, sigma, wind, basis_y, basis_z, gamma),
        [tree, (2, ny, nz)], flops=matmul,
    )
    sums = exchange(sent)
    return call(
        functools.partial(finish_kernel, rows=rows), "finish", [field, field],
        (sums, gathered, right_side, z, w, z2, u), flops=matmul // 8,
    )


def solution(mesh):
    placed = (P(AXIS, None, None),) * 4 + (P(),) * 3
    return jax.shard_map(
        lambda *args: tuple(on_device(*args)),
        mesh=mesh,
        in_specs=placed,
        out_specs=(P(AXIS, None, None), P(AXIS, None, None)),
        check_vma=False,
    )
```

time: 227 us -> 84.3 us (0.37)
  the two profiles are of different devices: /device:TPU:8 before, /device:TPU:0 now
where the time goes in v1:
time: 84.3 us; the launch traced here: 83.3 us
  local copies, waits for them, and re-layouts  24.7 us (29%)
  starting transfers between devices  18.7 us (22%)
  blocking collectives  14.9 us (18%)
  Pallas kernels  12.7 us (15%)
  waiting for transfers between devices  11.5 us (14%)
    unnamed x58, local copies, waits for them, and re-layouts  24.7 us
    all_to_all x2, starting transfers between devices, exchange(): return lax.all_to_all(block, AXIS, 0, 0, tiled=True)  17 us
    all_to_all x1, blocking collectives, exchange(): return lax.all_to_all(block, AXIS, 0, 0, tiled=True)  14.9 us
    pallas_call x6, Pallas kernels, call(): pl.pallas_call(kernel, name=name, out_shape=[jax.ShapeDtypeStruct(s, F32)...  12.7 us
    all_to_all x2, waiting for transfers between devices, exchange(): return lax.all_to_all(block, AXIS, 0, 0, tiled=True)  10.1 us
  transfers between devices with their start and end apart: 6, of which 4 were waited for; matrix products, arithmetic and copies ran while one was open for 0% of the time, Pallas kernels for 3%

profile of v1, /device:TPU:0, one launch (start us, length us, event | category | flops | bytes accessed | tf_op | source)
XLA Modules:
  0.0 83.3 jit_solution(16285464429805252788)
XLA Ops:
  0.6 0.8 copy.15.by_ref
  1.4 1.0 %copy.16.bz_ref = f32[512,64]{1,0:T(8,128)S(1)} copy(f32[512,64]{0,1:T(8,128)} %param.12) | data formatting | bytes 262144 | tf_op args[5]
  2.5 0.0 copy-start
  2.5 1.2 %copy-done = f32[4,128,512]{2,1,0:T(8,128)S(1)} copy-done((f32[4,128,512]{2,1,0:T(8,128)S(1)}, f32[4,128,512]{2,1,0:T(8,128)}, u32[]{:S(2)}) %copy-start) | copy-done | bytes 1048600
  3.7 1.2 %first.1 = f32[32,16,128]{2,1,0:T(8,128)} custom-call(f32[4,128,512]{2,1,0:T(8,128)S(1)} %copy-done, f32[128,32]{1,0:T(8,128)S(1)} %copy.15.by_ref, f32[512,64]{1,0:T(8,128)S(1)} %copy.16.bz_ref), custom_call_target="tpu_custom_call" | custom-call | flops 100663296 | tf_op jit(solution)/shard_map/first/pallas_call | solution.py:251
  4.9 7.5 %all-to-all-start = ((f32[32,16,128]{2,1,0:T(8,128)}), f32[32,16,128]{2,1,0:T(8,128)}, u32[]{:S(2)}, u32[]{:S(2)}) async-start(f32[32,16,128]{2,1,0:T(8,128)} %first.1), calls=%async_computation | async-start | bytes 524288 | tf_op jit(solution)/shard_map/all_to_all | solution.py:264
  12.4 0.0 copy-start.26
  12.4 1.2 %copy-done.26 = f32[1,512,512]{2,1,0:T(8,128)S(1)} copy-done((f32[1,512,512]{2,1,0:T(8,128)S(1)}, f32[1,512,512]{2,1,0:T(8,128)}, u32[]{:S(2)}) %copy-start.26) | copy-done | bytes 1048600
  13.6 1.1 %local.2 = (f32[4,128,512]{2,1,0:T(8,128)S(1)}, f32[1,128,512]{2,1,0:T(8,128)S(1)}, f32[1,128,512]{2,1,0:T(8,128)S(1)}) custom-call(f32[4,128,512]{2,1,0:T(8,128)S(1)} %copy-done.1, f32[1,512,512]{2,1,0:T(8,128)S(1)} %copy-done.26), custom_call_target="tpu_custom_call" | custom-call | flops 805306368 | tf_op jit(solution)/shard_map/local/pallas_call | solution.py:251
  14.7 0.0 copy-start.10
  14.7 1.0 %copy-done.10 = f32[4,128,512]{2,1,0:T(8,128)} copy-done((f32[4,128,512]{2,1,0:T(8,128)}, f32[4,128,512]{2,1,0:T(8,128)S(1)}, u32[]{:S(2)}) %copy-start.10) | copy-done | bytes 1048600
  15.7 0.2 collective-permute-start
  15.9 0.7 collective-permute-start.1
  16.5 0.7 collective-permute-done.even_ref
  17.2 0.7 copy-done.22
  17.9 0.7 copy-done.24
  18.6 4.3 %all-to-all-done.gath_ref = f32[32,16,128]{2,1,0:T(8,128)} async-done(((f32[32,16,128]{2,1,0:T(8,128)}), f32[32,16,128]{2,1,0:T(8,128)}, u32[]{:S(2)}, u32[]{:S(2)}) %all-to-all-start) | async-done | bytes 262176 | tf_op jit(solution)/shard_map/all_to_all | solution.py:264
  23.0 0.0 copy-start.11
  23.0 1.2 %copy-done.11 = f32[4,128,512]{2,1,0:T(8,128)S(1)} copy-done((f32[4,128,512]{2,1,0:T(8,128)S(1)}, f32[4,128,512]{2,1,0:T(8,128)}, u32[]{:S(2)}) %copy-start.11) | copy-done | bytes 1048600
  24.2 0.9 %copy-done.23 = f32[1,128,512]{2,1,0:T(8,128)S(1)} copy-done((f32[1,128,512]{2,1,0:T(8,128)S(1)}, f32[1,128,512]{2,1,0:T(8,128)}, u32[]{:S(2)}) %copy-start.23) | copy-done | bytes 262168
  25.1 0.9 %copy-done.25 = f32[1,128,512]{2,1,0:T(8,128)S(1)} copy-done((f32[1,128,512]{2,1,0:T(8,128)S(1)}, f32[1,128,512]{2,1,0:T(8,128)}, u32[]{:S(2)}) %copy-start.25) | copy-done | bytes 262168
  26.1 3.3 %middle.1 = (f32[4,128,512]{2,1,0:T(8,128)S(1)}, f32[2,128,512]{2,1,0:T(8,128)S(1)}, f32[4,128,512]{2,1,0:T(8,128)S(1)}, f32[32,24,128]{2,1,0:T(8,128)S(1)}) custom-call(f32[32,16,128]{2,1,0:T(8,128)} %all-to-all-done.gath_ref, f32[4,128,512]{2,1,0:T(8,128)S(1)} %copy-done.11, f32[1,128,512]{2,1,0:T(8,128)S(1)} %copy-done.23, f32[1,128,512]{2,1,0:T(8,128)S(1)} %copy-done.25, ...), custom_call_target="tpu_custom_call" | custom-call | flops 805306368 | tf_op jit(solution)/shard_map/middle/pallas_call | solution.py:251
  29.4 1.0 %copy-done.4 = f32[4,128,512]{2,1,0:T(8,128)} copy-done((f32[4,128,512]{2,1,0:T(8,128)}, f32[4,128,512]{2,1,0:T(8,128)S(1)}, u32[]{:S(2)}) %copy-start.4) | copy-done | bytes 1048600
  30.4 1.0 %copy-done.6 = f32[4,128,512]{2,1,0:T(8,128)} copy-done((f32[4,128,512]{2,1,0:T(8,128)}, f32[4,128,512]{2,1,0:T(8,128)S(1)}, u32[]{:S(2)}) %copy-start.6) | copy-done | bytes 1048600
  31.3 0.8 copy-done.14
  32.1 0.7 copy-done.16
  32.9 9.5 %all-to-all-start.1 = ((f32[32,24,128]{2,1,0:T(8,128)}), f32[32,24,128]{2,1,0:T(8,128)}, u32[]{:S(2)}, u32[]{:S(2)}) async-start(f32[32,24,128]{2,1,0:T(8,128)} %copy-done.16), calls=%async_computation.1 | async-start | bytes 786432 | tf_op jit(solution)/shard_map/all_to_all | solution.py:264
  42.4 0.0 copy-start.7
  42.4 1.2 %copy-done.7 = f32[4,128,512]{2,1,0:T(8,128)S(1)} copy-done((f32[4,128,512]{2,1,0:T(8,128)S(1)}, f32[4,128,512]{2,1,0:T(8,128)}, u32[]{:S(2)}) %copy-start.7) | copy-done | bytes 1048600
  43.6 1.2 %copy-done.27 = f32[1,512,512]{2,1,0:T(8,128)S(1)} copy-done((f32[1,512,512]{2,1,0:T(8,128)S(1)}, f32[1,512,512]{2,1,0:T(8,128)}, u32[]{:S(2)}) %copy-start.27) | copy-done | bytes 1048600
  44.9 1.1 %local.3 = (f32[4,128,512]{2,1,0:T(8,128)S(1)}, f32[1,128,512]{2,1,0:T(8,128)S(1)}, f32[1,128,512]{2,1,0:T(8,128)S(1)}) custom-call(f32[4,128,512]{2,1,0:T(8,128)S(1)} %copy-done.7, f32[1,512,512]{2,1,0:T(8,128)S(1)} %copy-done.27), custom_call_target="tpu_custom_call" | custom-call | flops 805306368 | tf_op jit(solution)/shard_map/local/pallas_call | solution.py:251
  45.9 0.0 copy-start.12
  45.9 1.0 %copy-done.12 = f32[4,128,512]{2,1,0:T(8,128)} copy-done((f32[4,128,512]{2,1,0:T(8,128)}, f32[4,128,512]{2,1,0:T(8,128)S(1)}, u32[]{:S(2)}) %copy-start.12) | copy-done | bytes 1048600
  46.9 0.2 collective-permute-start.2
  47.1 0.7 collective-permute-start.3
  47.8 0.7 collective-permute-done.2.even_ref
  48.4 0.7 copy-done.18
  49.2 0.7 copy-done.20
  49.9 5.8 %all-to-all-done.1.gath_ref = f32[32,24,128]{2,1,0:T(8,128)} async-done(((f32[32,24,128]{2,1,0:T(8,128)}), f32[32,24,128]{2,1,0:T(8,128)}, u32[]{:S(2)}, u32[]{:S(2)}) %all-to-all-start.1) | async-done | bytes 393248 | tf_op jit(solution)/shard_map/all_to_all | solution.py:264
  55.7 1.2 %copy-done.5 = f32[4,128,512]{2,1,0:T(8,128)S(1)} copy-done((f32[4,128,512]{2,1,0:T(8,128)S(1)}, f32[4,128,512]{2,1,0:T(8,128)}, u32[]{:S(2)}) %copy-start.5) | copy-done | bytes 1048600
  56.9 1.2 %copy-done.8 = f32[4,128,512]{2,1,0:T(8,128)S(1)} copy-done((f32[4,128,512]{2,1,0:T(8,128)S(1)}, f32[4,128,512]{2,1,0:T(8,128)}, u32[]{:S(2)}) %copy-start.8) | copy-done | bytes 1048600
  58.1 1.2 %copy-done.13 = f32[4,128,512]{2,1,0:T(8,128)S(1)} copy-done((f32[4,128,512]{2,1,0:T(8,128)S(1)}, f32[4,128,512]{2,1,0:T(8,128)}, u32[]{:S(2)}) %copy-start.13) | copy-done | bytes 1048600
  59.3 1.0 %copy-done.15 = f32[2,128,512]{2,1,0:T(8,128)S(1)} copy-done((f32[2,128,512]{2,1,0:T(8,128)S(1)}, f32[2,128,512]{2,1,0:T(8,128)}, u32[]{:S(2)}) %copy-start.15) | copy-done | bytes 524312
  60.4 0.9 %copy-done.19 = f32[1,128,512]{2,1,0:T(8,128)S(1)} copy-done((f32[1,128,512]{2,1,0:T(8,128)S(1)}, f32[1,128,512]{2,1,0:T(8,128)}, u32[]{:S(2)}) %copy-start.19) | copy-done | bytes 262168
  61.3 0.9 %copy-done.21 = f32[1,128,512]{2,1,0:T(8,128)S(1)} copy-done((f32[1,128,512]{2,1,0:T(8,128)S(1)}, f32[1,128,512]{2,1,0:T(8,128)}, u32[]{:S(2)}) %copy-start.21) | copy-done | bytes 262168
  62.3 3.2 %last.1 = (f32[4,128,512]{2,1,0:T(8,128)S(1)}, f32[4,128,512]{2,1,0:T(8,128)S(1)}, f32[32,128]{1,0:T(8,128)S(1)}) custom-call(f32[32,24,128]{2,1,0:T(8,128)} %all-to-all-done.1.gath_ref, f32[4,128,512]{2,1,0:T(8,128)S(1)} %copy-done.13, f32[1,128,512]{2,1,0:T(8,128)S(1)} %copy-done.19, f32[1,128,512]{2,1,0:T(8,128)S(1)} %copy-done.21, ...), custom_call_target="tpu_custom_call" | custom-call | flops 805306368 | tf_op jit(solution)/shard_map/last/pallas_call | solution.py:251
  65.5 14.9 %all_to_all.21 = f32[32,1,128]{2,1,0:T(1,128)S(1)} all-to-all(f32[32,1,128]{2,1,0:T(1,128)S(1)} %bitcast.5), channel_id=1, replica_groups=mesh['sub'=32] {'sub'}, dimensions={0} | all-to-all | bytes 32768 | tf_op jit(solution)/shard_map/all_to_all | solution.py:264
  80.5 2.9 %finish.1 = (f32[4,128,512]{2,1,0:T(8,128)}, f32[4,128,512]{2,1,0:T(8,128)}) custom-call(f32[32,128]{1,0:T(8,128)S(1)} %bitcast.4, f32[32,24,128]{2,1,0:T(8,128)} %all-to-all-done.1.gath_ref, f32[4,128,512]{2,1,0:T(8,128)S(1)} %copy-done.1, f32[4,128,512]{2,1,0:T(8,128)S(1)} %copy-done.5, f32[4,128,512]{2,1,0:T(8,128)S(1)} %copy-done.9, ...), custom_call_target="tpu_custom_call" | custom-call | flops 100663296 | tf_op jit(solution)/shard_map/finish/pallas_call | solution.py:251
  (29 shorter events, 0.1 us)
Async XLA Ops:
  2.5 1.2 %copy-start = (f32[4,128,512]{2,1,0:T(8,128)S(1)}, f32[4,128,512]{2,1,0:T(8,128)}, u32[]{:S(2)}) copy-start(f32[4,128,512]{2,1,0:T(8,128)} %r_ref.7) | copy-start | bytes 3145732
  3.7 8.7 %copy-start.1 = (f32[4,128,512]{2,1,0:T(8,128)S(1)}, f32[4,128,512]{2,1,0:T(8,128)}, u32[]{:S(2)}) copy-start(f32[4,128,512]{2,1,0:T(8,128)} %r_ref.7) | copy-start | bytes 3145732
  4.9 18.0 %all-to-all-start = ((f32[32,16,128]{2,1,0:T(8,128)}), f32[32,16,128]{2,1,0:T(8,128)}, u32[]{:S(2)}, u32[]{:S(2)}) async-start(f32[32,16,128]{2,1,0:T(8,128)} %first.1), calls=%async_computation | async-start | bytes 524288 | tf_op jit(solution)/shard_map/all_to_all | solution.py:264
  12.4 1.2 %copy-start.26 = (f32[1,512,512]{2,1,0:T(8,128)S(1)}, f32[1,512,512]{2,1,0:T(8,128)}, u32[]{:S(2)}) copy-start(f32[1,512,512]{2,1,0:T(8,128)} %inv_ref.3) | copy-start | bytes 3145732
  13.6 9.3 %copy-start.2 = (f32[4,128,512]{2,1,0:T(8,128)S(1)}, f32[4,128,512]{2,1,0:T(8,128)}, u32[]{:S(2)}) copy-start(f32[4,128,512]{2,1,0:T(8,128)} %sigma_ref.3) | copy-start | bytes 3145732
  13.6 9.3 %copy-start.3 = (f32[4,128,512]{2,1,0:T(8,128)S(1)}, f32[4,128,512]{2,1,0:T(8,128)}, u32[]{:S(2)}) copy-start(f32[4,128,512]{2,1,0:T(8,128)} %wind_ref.3) | copy-start | bytes 3145732
  13.6 9.3 %copy-start.17 = (f32[5,32,64]{2,1,0:T(8,128)S(1)}, f32[5,32,64]{2,1,0:T(8,128)}, u32[]{:S(2)}) copy-start(f32[5,32,64]{2,1,0:T(8,128)} %gamma_ref.3) | copy-start | bytes 122884
  14.7 1.0 %copy-start.10 = (f32[4,128,512]{2,1,0:T(8,128)}, f32[4,128,512]{2,1,0:T(8,128)S(1)}, u32[]{:S(2)}) copy-start(f32[4,128,512]{2,1,0:T(8,128)S(1)} %get-tuple-element.15.local_ref) | copy-start | bytes 3145732
  15.7 1.5 %collective-permute-start = (f32[1,128,512]{2,1,0:T(8,128)S(1)}, f32[1,128,512]{2,1,0:T(8,128)S(1)}, u32[]{:S(2)}, u32[]{:S(2)}) collective-permute-start(f32[1,128,512]{2,1,0:T(8,128)S(1)} %get-tuple-element.16), channel_id=1, source_target_pairs={{0,1},{1,0},{2,3},{3,2},{4,5},{5,4},{6,7},{7,6},{8,9},{9,8},{10,11... | collective-permute-start | bytes 786440 | tf_op jit(solution)/shard_map/ppermute | solution.py:284
  15.9 2.1 %collective-permute-start.1 = (f32[1,128,512]{2,1,0:T(8,128)S(1)}, f32[1,128,512]{2,1,0:T(8,128)S(1)}, u32[]{:S(2)}, u32[]{:S(2)}) collective-permute-start(f32[1,128,512]{2,1,0:T(8,128)S(1)} %get-tuple-element.17), channel_id=1, source_target_pairs={{1,2},{3,4},{5,6},{7,8},{9,10},{11,12},{13,14},{15,16},{17,18},{19... | collective-permute-start | bytes 786440 | tf_op jit(solution)/shard_map/ppermute | solution.py:284
  17.2 0.7 copy-start.22
  17.9 0.7 copy-start.24
  23.0 1.2 %copy-start.11 = (f32[4,128,512]{2,1,0:T(8,128)S(1)}, f32[4,128,512]{2,1,0:T(8,128)}, u32[]{:S(2)}) copy-start(f32[4,128,512]{2,1,0:T(8,128)} %copy-done.10) | copy-start | bytes 3145732
  24.2 0.9 %copy-start.23 = (f32[1,128,512]{2,1,0:T(8,128)S(1)}, f32[1,128,512]{2,1,0:T(8,128)}, u32[]{:S(2)}) copy-start(f32[1,128,512]{2,1,0:T(8,128)} %copy-done.22) | copy-start | bytes 786436
  25.1 0.9 %copy-start.25 = (f32[1,128,512]{2,1,0:T(8,128)S(1)}, f32[1,128,512]{2,1,0:T(8,128)}, u32[]{:S(2)}) copy-start(f32[1,128,512]{2,1,0:T(8,128)} %copy-done.24) | copy-start | bytes 786436
  29.4 1.0 %copy-start.4 = (f32[4,128,512]{2,1,0:T(8,128)}, f32[4,128,512]{2,1,0:T(8,128)S(1)}, u32[]{:S(2)}) copy-start(f32[4,128,512]{2,1,0:T(8,128)S(1)} %get-tuple-element.23.z_ref) | copy-start | bytes 3145732
  30.4 1.0 %copy-start.6 = (f32[4,128,512]{2,1,0:T(8,128)}, f32[4,128,512]{2,1,0:T(8,128)S(1)}, u32[]{:S(2)}) copy-start(f32[4,128,512]{2,1,0:T(8,128)S(1)} %get-tuple-element.19.f_ref.w_ref) | copy-start | bytes 3145732
  31.3 0.8 copy-start.14
  32.1 0.7 copy-start.16
  32.9 22.8 %all-to-all-start.1 = ((f32[32,24,128]{2,1,0:T(8,128)}), f32[32,24,128]{2,1,0:T(8,128)}, u32[]{:S(2)}, u32[]{:S(2)}) async-start(f32[32,24,128]{2,1,0:T(8,128)} %copy-done.16), calls=%async_computation.1 | async-start | bytes 786432 | tf_op jit(solution)/shard_map/all_to_all | solution.py:264
  42.4 1.2 %copy-start.7 = (f32[4,128,512]{2,1,0:T(8,128)S(1)}, f32[4,128,512]{2,1,0:T(8,128)}, u32[]{:S(2)}) copy-start(f32[4,128,512]{2,1,0:T(8,128)} %copy-done.6) | copy-start | bytes 3145732
  43.6 1.2 %copy-start.27 = (f32[1,512,512]{2,1,0:T(8,128)S(1)}, f32[1,512,512]{2,1,0:T(8,128)}, u32[]{:S(2)}) copy-start(f32[1,512,512]{2,1,0:T(8,128)} %inv_ref.3) | copy-start | bytes 3145732
  45.9 1.0 %copy-start.12 = (f32[4,128,512]{2,1,0:T(8,128)}, f32[4,128,512]{2,1,0:T(8,128)S(1)}, u32[]{:S(2)}) copy-start(f32[4,128,512]{2,1,0:T(8,128)S(1)} %get-tuple-element.20.local_ref) | copy-start | bytes 3145732
  46.9 1.5 %collective-permute-start.2 = (f32[1,128,512]{2,1,0:T(8,128)S(1)}, f32[1,128,512]{2,1,0:T(8,128)S(1)}, u32[]{:S(2)}, u32[]{:S(2)}) collective-permute-start(f32[1,128,512]{2,1,0:T(8,128)S(1)} %get-tuple-element.21), channel_id=1, source_target_pairs={{0,1},{1,0},{2,3},{3,2},{4,5},{5,4},{6,7},{7,6},{8,9},{9,8},{10,11... | collective-permute-start | bytes 786440 | tf_op jit(solution)/shard_map/ppermute | solution.py:284
  47.1 2.1 %collective-permute-start.3 = (f32[1,128,512]{2,1,0:T(8,128)S(1)}, f32[1,128,512]{2,1,0:T(8,128)S(1)}, u32[]{:S(2)}, u32[]{:S(2)}) collective-permute-start(f32[1,128,512]{2,1,0:T(8,128)S(1)} %get-tuple-element.22), channel_id=1, source_target_pairs={{1,2},{3,4},{5,6},{7,8},{9,10},{11,12},{13,14},{15,16},{17,18},{19... | collective-permute-start | bytes 786440 | tf_op jit(solution)/shard_map/ppermute | solution.py:284
  48.4 0.7 copy-start.18
  49.2 0.7 copy-start.20
  55.7 1.2 %copy-start.5 = (f32[4,128,512]{2,1,0:T(8,128)S(1)}, f32[4,128,512]{2,1,0:T(8,128)}, u32[]{:S(2)}) copy-start(f32[4,128,512]{2,1,0:T(8,128)} %copy-done.4) | copy-start | bytes 3145732
  56.9 1.2 %copy-start.8 = (f32[4,128,512]{2,1,0:T(8,128)S(1)}, f32[4,128,512]{2,1,0:T(8,128)}, u32[]{:S(2)}) copy-start(f32[4,128,512]{2,1,0:T(8,128)} %copy-done.6) | copy-start | bytes 3145732
  58.1 1.2 %copy-start.13 = (f32[4,128,512]{2,1,0:T(8,128)S(1)}, f32[4,128,512]{2,1,0:T(8,128)}, u32[]{:S(2)}) copy-start(f32[4,128,512]{2,1,0:T(8,128)} %copy-done.12) | copy-start | bytes 3145732
  59.3 1.0 %copy-start.15 = (f32[2,128,512]{2,1,0:T(8,128)S(1)}, f32[2,128,512]{2,1,0:T(8,128)}, u32[]{:S(2)}) copy-start(f32[2,128,512]{2,1,0:T(8,128)} %copy-done.14) | copy-start | bytes 1572868
  60.4 0.9 %copy-start.19 = (f32[1,128,512]{2,1,0:T(8,128)S(1)}, f32[1,128,512]{2,1,0:T(8,128)}, u32[]{:S(2)}) copy-start(f32[1,128,512]{2,1,0:T(8,128)} %copy-done.18) | copy-start | bytes 786436
  61.3 0.9 %copy-start.21 = (f32[1,128,512]{2,1,0:T(8,128)S(1)}, f32[1,128,512]{2,1,0:T(8,128)}, u32[]{:S(2)}) copy-start(f32[1,128,512]{2,1,0:T(8,128)} %copy-done.20) | copy-start | bytes 786436
  62.3 18.2 %copy-start.9 = (f32[4,128,512]{2,1,0:T(8,128)S(1)}, f32[4,128,512]{2,1,0:T(8,128)}, u32[]{:S(2)}) copy-start(f32[4,128,512]{2,1,0:T(8,128)} %copy-done.6) | copy-start | bytes 3145732

commit v2 on v1

--- a/solution.py
+++ b/solution.py
@@ -6,6 +6,7 @@
 from jax.experimental.pallas import tpu as pltpu
 from jax.sharding import PartitionSpec as P
 
+
 F32 = jnp.float32
 BF16 = jnp.bfloat16
 AXIS = "sub"
@@ -45,8 +46,8 @@
 
 
 def project(summed, by, bz, fold):
-    half = dot3(halves(summed), halves(bz))
-    return pack(dot3(halves(by), halves(half), TN), fold)
+    half = dot3(halves(summed), halves(bz), NT)
+    return pack(dot3(halves(by), halves(half)), fold)
 
 
 def coarse_of(gath_ref, gamma_ref, tree_ref, rows, layers, fold, levels, count):
@@ -81,11 +82,19 @@
     return out
 
 
-def spreads(coarse, by, bz):
-    ky = by.shape[1]
-    back = dot3(halves(jnp.concatenate(coarse, axis=0)), halves(bz), NT)
-    by_parts = halves(by)
-    return [dot3(by_parts, halves(back[i * ky : (i + 1) * ky])) for i in range(len(coarse))]
+def coarse_kernel(
+    gath_ref, by_ref, bz_ref, gamma_ref, out_ref, tree_ref, *, fold, levels, count, rows, layers
+):
+    coarse = coarse_of(gath_ref, gamma_ref, tree_ref, rows, layers, fold, levels, count)
+    ky = by_ref.shape[0]
+    back = dot3(halves(jnp.concatenate(coarse, axis=0)), halves(bz_ref[...]))
+    back_high, back_low = halves(back)
+    by_high, by_low = halves(by_ref[...])
+    left = jnp.concatenate([by_high, by_high, by_low], axis=0)
+    for i in range(len(coarse)):
+        high, low = (part[i * ky : (i + 1) * ky] for part in (back_high, back_low))
+        right = jnp.concatenate([high, low, high], axis=0)
+        out_ref[i] = lax.dot_general(left, right, TN, preferred_element_type=F32)
 
 
 def stencil(prev, here, after, sigma, wind):
@@ -119,34 +128,45 @@
     return lax.rem(lax.axis_index(AXIS), 2) == 0
 
 
-def first_kernel(r_ref, by_ref, bz_ref, out_ref, *, fold):
+def send_edges(local_ref, even_ref, odd_ref):
+    layers = local_ref.shape[0]
+    even = even_here()
+    even_ref[0] = local_ref[jnp.where(even, layers - 1, 0)]
+    odd_ref[0] = local_ref[jnp.where(even, 0, layers - 1)]
+
+
+def first_kernel(
+    r_hbm, inv_hbm, by_ref, bz_ref,
+    out_ref, r_ref, high_ref, low_ref, local_ref, even_ref, odd_ref,
+    inv_ref, sems, *, fold,
+):
     layers = r_ref.shape[0]
+    loads = [pltpu.make_async_copy(r_hbm.at[x], r_ref.at[x], sems.at[x]) for x in range(layers)]
+    loads.append(pltpu.make_async_copy(inv_hbm.at[0], inv_ref, sems.at[layers]))
+    for load in loads:
+        load.start()
+    loads[0].wait()
     summed = r_ref[0]
     for x in range(1, layers):
+        loads[x].wait()
         summed = summed + r_ref[x]
     packed = project(summed, by_ref[...], bz_ref[...], fold)
     out_ref[...] = jnp.broadcast_to(packed[None], out_ref.shape)
-
-
-def local_kernel(f_ref, inv_ref, local_ref, even_ref, odd_ref):
-    layers, rows, depth = f_ref.shape
-    inverse = halves(inv_ref[0])
-    for x in range(layers):
-        local_ref[x] = dot3(halves(f_ref[x]), inverse)
-    even = even_here()
-    even_ref[0] = local_ref[jnp.where(even, layers - 1, 0)]
-    odd_ref[0] = local_ref[jnp.where(even, 0, layers - 1)]
+    loads[layers].wait()
+    inverse = halves(inv_ref[...])
+    high_ref[...], low_ref[...] = inverse
+    for x in range(layers):
+        local_ref[x] = dot3(halves(r_ref[x]), inverse)
+    send_edges(local_ref, even_ref, odd_ref)
 
 
 def middle_kernel(
-    gath_ref, local_ref, even_ref, odd_ref, r_ref, sigma_ref, wind_ref, by_ref, bz_ref, gamma_ref,
-    z_ref, edge_ref, w_ref, out_ref, tree_ref, *, fold, levels, count, rows,
+    spread_ref, local_ref, even_ref, odd_ref, r_ref, sigma_ref, wind_ref, by_ref, bz_ref,
+    high_ref, low_ref,
+    z_ref, edge_ref, w_ref, out_ref, local2_ref, even2_ref, odd2_ref, *, fold, count, rows,
 ):
     layers = r_ref.shape[0]
-    bz = bz_ref[...]
-    by = by_ref[...]
-    coarse = coarse_of(gath_ref, gamma_ref, tree_ref, rows, layers, fold, levels, count)
-    before, own, after = spreads(coarse, by, bz)
+    before, own, after = (spread_ref[i] for i in range(3))
     even = even_here().astype(F32)
     from_pair = even_ref[0]
     from_other = odd_ref[0]
@@ -168,10 +188,14 @@
         else:
             rr, rw, ww = rr + parts[0], rw + parts[1], ww + parts[2]
             summed = summed + w
-    packed = project(summed, by, bz, fold)
+    packed = project(summed, by_ref[...], bz_ref[...], fold)
     scalars = jnp.concatenate([rr, rw, ww, jnp.zeros((5, LANES), F32)], axis=0)
     out_ref[:, :rows, :] = jnp.broadcast_to(packed[None], (count,) + packed.shape)
     out_ref[:, rows:, :] = jnp.broadcast_to(scalars[None], (count,) + scalars.shape)
+    inverse = (high_ref[...], low_ref[...])
+    for x in range(layers):
+        local2_ref[x] = dot3(halves(w_ref[x]), inverse)
+    send_edges(local2_ref, even2_ref, odd2_ref)
 
 
 def first_scalars(gath_ref, rows):
@@ -187,15 +211,13 @@
 
 
 def last_kernel(
-    gath_ref, local_ref, even_ref, odd_ref, r_ref, z_ref, edge_ref, w_ref, sigma_ref, wind_ref,
-    by_ref, bz_ref, gamma_ref,
-    z2_ref, u_ref, out_ref, tree_ref, edge2_ref, *, fold, levels, count, rows,
+    gath_ref, spread_ref, local_ref, even_ref, odd_ref, r_ref, z_ref, edge_ref, w_ref,
+    sigma_ref, wind_ref, z2_ref, u_ref, out_ref, edge2_ref, *, rows,
 ):
     layers = r_ref.shape[0]
     beta, h11, h21 = first_scalars(gath_ref, rows)
     scale = 1.0 / (h21 * beta)
-    coarse = coarse_of(gath_ref, gamma_ref, tree_ref, rows, layers, fold, levels, count)
-    before, own, after = spreads(coarse, by_ref[...], bz_ref[...])
+    before, own, after = (spread_ref[i] for i in range(3))
     even = even_here().astype(F32)
     from_pair = even_ref[0]
     from_other = odd_ref[0]
@@ -246,15 +268,16 @@
         res_ref[x] = r_ref[x] - (y_one * w_ref[x] + y_two * u_ref[x])
 
 
-def call(kernel, name, outs, args, scratch=(), flops=0):
+def call(kernel, outs, args, scratch=(), flops=0, hbm=()):
     vmem = pl.BlockSpec(memory_space=pltpu.VMEM)
+    far = pl.BlockSpec(memory_space=pltpu.HBM)
+    outs = [s if isinstance(s, jax.ShapeDtypeStruct) else jax.ShapeDtypeStruct(s, F32) for s in outs]
     return pl.pallas_call(
         kernel,
-        name=name,
-        out_shape=[jax.ShapeDtypeStruct(s, F32) for s in outs],
-        in_specs=[vmem] * len(args),
+        out_shape=outs,
+        in_specs=[far if i in hbm else vmem for i in range(len(args))],
         out_specs=[vmem] * len(outs),
-        scratch_shapes=[pltpu.VMEM(s, F32) for s in scratch],
+        scratch_shapes=[pltpu.VMEM(s, F32) if isinstance(s, tuple) else s for s in scratch],
         compiler_params=pltpu.CompilerParams(vmem_limit_bytes=24 << 20),
         cost_estimate=pl.CostEstimate(flops=flops, bytes_accessed=0, transcendentals=0),
     )(*args)
@@ -273,41 +296,50 @@
     rows, width = ky // fold, kz * fold
     field = (layers, ny, nz)
     edge = (1, ny, nz)
+    square = jax.ShapeDtypeStruct((nz, nz), BF16)
     pairs = [(i, i ^ 1) for i in range(count)]
     others = [(i, i + 1) for i in range(1, count - 1, 2)]
     others = others + [(j, i) for i, j in others]
     matmul = 6 * layers * ny * nz * nz
-    sizes = dict(fold=fold, levels=levels, count=count, rows=rows)
-
-    def local_of(f):
-        local, even, odd = call(local_kernel, "local", [field, edge, edge], (f, local_inverse), flops=matmul)
-        return local, lax.ppermute(even, AXIS, pairs), lax.ppermute(odd, AXIS, others)
-
-    (sent,) = call(
-        functools.partial(first_kernel, fold=fold), "first", [(count, rows, width)],
-        (right_side, basis_y, basis_z), flops=matmul // 8,
-    )
-    gathered = exchange(sent)
-    local, even, odd = local_of(right_side)
-    tree = (count, rows, width)
-    z, edges, w, sent = call(
-        functools.partial(middle_kernel, **sizes), "middle",
-        [field, (2, ny, nz), field, (count, rows + 8, width)],
-        (gathered, local, even, odd, right_side, sigma, wind, basis_y, basis_z, gamma),
-        [tree], flops=matmul,
-    )
-    gathered = exchange(sent)
-    local, even, odd = local_of(w)
+    by, bz = basis_y.T, basis_z.T
+
+    def round_of(sent, even, odd):
+        even = lax.ppermute(even, AXIS, pairs)
+        odd = lax.ppermute(odd, AXIS, others)
+        gathered = exchange(sent)
+        (spread,) = call(
+            functools.partial(
+                coarse_kernel, fold=fold, levels=levels, count=count, rows=rows, layers=layers
+            ),
+            [(3, ny, nz)], (gathered, by, bz, gamma), [(count, rows, width)],
+            flops=matmul // 8,
+        )
+        return gathered, spread, even, odd
+
+    sent, r, high, low, local, even, odd = call(
+        functools.partial(first_kernel, fold=fold),
+        [(count, rows, width), field, square, square, field, edge, edge],
+        (right_side, local_inverse, by, bz),
+        [(nz, nz), pltpu.SemaphoreType.DMA((layers + 1,))], flops=matmul, hbm=(0, 1),
+    )
+    _, spread, even, odd = round_of(sent, even, odd)
+    z, edges, w, sent, local, even, odd = call(
+        functools.partial(middle_kernel, fold=fold, count=count, rows=rows),
+        [field, (2, ny, nz), field, (count, rows + 8, width), field, edge, edge],
+        (spread, local, even, odd, r, sigma, wind, by, bz, high, low),
+        flops=2 * matmul,
+    )
+    gathered, spread, even, odd = round_of(sent, even, odd)
     z2, u, sent = call(
-        functools.partial(last_kernel, **sizes), "last",
+        functools.partial(last_kernel, rows=rows),
         [field, field, (count, LANES)],
-        (gathered, local, even, odd, right_side, z, edges, w, sigma, wind, basis_y, basis_z, gamma),
-        [tree, (2, ny, nz)], flops=matmul,
+        (gathered, spread, local, even, odd, r, z, edges, w, sigma, wind),
+        [(2, ny, nz)], flops=matmul,
     )
     sums = exchange(sent)
     return call(
-        functools.partial(finish_kernel, rows=rows), "finish", [field, field],
-        (sums, gathered, right_side, z, w, z2, u), flops=matmul // 8,
+        functools.partial(finish_kernel, rows=rows), [field, field],
+        (sums, gathered, r, z, w, z2, u), flops=matmul // 8,
     )
 
 

time: 84.3 us -> 82.4 us (0.977)
  waiting for transfers between devices: 11.5 us -> 20.5 us
  blocking collectives: 14.9 us -> 9.7 us
  starting transfers between devices: 18.7 us -> 15.2 us
  Pallas kernels: 12.7 us -> 11.3 us
    all_to_all x2, waiting for transfers between devices: 10.1 us -> 20.5 us  [exchange(): return lax.all_to_all(block, AXIS, 0, 0, tiled=True)]
    all_to_all x1, blocking collectives: 14.9 us -> 9.7 us  [exchange(): return lax.all_to_all(block, AXIS, 0, 0, tiled=True)]
    all_to_all x2, starting transfers between devices: 17 us -> 11.8 us  [exchange(): return lax.all_to_all(block, AXIS, 0, 0, tiled=True)]
    ppermute x4, starting transfers between devices: 1.69 us -> 3.35 us  [the longest x2 2.72 us: round_of(): odd = lax.ppermute(odd, AXIS, others)]
    pallas_call x6, Pallas kernels: 12.7 us -> 11.3 us  [call(): pl.pallas_call(kernel, out_shape=outs, in_specs=[far if i in hbm else vme...]
    ppermute x4, waiting for transfers between devices: 1.37 us -> 0.01 us  [the longest x2 0.01 us: round_of(): even = lax.ppermute(even, AXIS, pairs)]
    unnamed x58 -> x64, local copies, waits for them, and re-layouts: 24.7 us -> 24.1 us
  transfers between devices with their start and end apart: 6 -> 6, of which waited for: 4 -> 2; matrix products, arithmetic and copies ran while one was open for 0% -> 0% of each run, Pallas kernels for 3% -> 1%
where the time goes in v2:
time: 82.4 us; the launch traced here: 81.6 us
  local copies, waits for them, and re-layouts  24.1 us (29%)
  waiting for transfers between devices  20.5 us (25%)
  starting transfers between devices  15.2 us (18%)
  Pallas kernels  11.3 us (14%)
  blocking collectives  9.7 us (12%)
    unnamed x64, local copies, waits for them, and re-layouts  24.1 us
    all_to_all x2, waiting for transfers between devices, exchange(): return lax.all_to_all(block, AXIS, 0, 0, tiled=True)  20.5 us
    all_to_all x2, starting transfers between devices, exchange(): return lax.all_to_all(block, AXIS, 0, 0, tiled=True)  11.8 us
    pallas_call x6, Pallas kernels, call(): pl.pallas_call(kernel, out_shape=outs, in_specs=[far if i in hbm else vme...  11.3 us
    all_to_all x1, blocking collectives, exchange(): return lax.all_to_all(block, AXIS, 0, 0, tiled=True)  9.7 us
    ppermute x2, starting transfers between devices, round_of(): odd = lax.ppermute(odd, AXIS, others)  2.72 us
  transfers between devices with their start and end apart: 6, of which 2 were waited for; matrix products, arithmetic and copies ran while one was open for 0% of the time, Pallas kernels for 1%

profile of v2, /device:TPU:0, one launch (start us, length us, event | category | flops | bytes accessed | tf_op | source)
XLA Modules:
  0.0 81.6 jit_solution(15858519156249110117)
XLA Ops:
  0.6 0.0 copy-start.7
  0.6 0.9 %copy-done.7 = f32[512,64]{0,1:T(8,128)S(1)} copy-done((f32[512,64]{0,1:T(8,128)S(1)}, f32[512,64]{0,1:T(8,128)}, u32[]{:S(2)}) %copy-start.7) | copy-done | bytes 131096
  1.5 0.7 copy-done.24
  2.3 1.2 %copy-done.26 = f32[4,128,512]{2,1,0:T(8,128)S(1)} copy-done((f32[4,128,512]{2,1,0:T(8,128)S(1)}, f32[4,128,512]{2,1,0:T(8,128)}, u32[]{:S(2)}) %copy-start.26) | copy-done | bytes 1048600
  3.5 1.2 %copy-done.27 = f32[1,512,512]{2,1,0:T(8,128)S(1)} copy-done((f32[1,512,512]{2,1,0:T(8,128)S(1)}, f32[1,512,512]{2,1,0:T(8,128)}, u32[]{:S(2)}) %copy-start.27) | copy-done | bytes 1048600
  4.7 1.9 %shard_map.86 = (f32[32,16,128]{2,1,0:T(8,128)S(1)}, f32[4,128,512]{2,1,0:T(8,128)S(1)}, bf16[512,512]{1,0:T(8,128)(2,1)S(1)}, bf16[512,512]{1,0:T(8,128)(2,1)S(...) custom-call(f32[4,128,512]{2,1,0:T(8,128)S(1)} %copy-done.26, ...), custom_call_target="tpu_custom_call" | custom-call | flops 805306368 | tf_op jit(solution)/shard_map/pallas_call | solution.py:275
  6.6 0.0 copy-start.10
  6.6 1.0 %copy-done.10 = f32[4,128,512]{2,1,0:T(8,128)} copy-done((f32[4,128,512]{2,1,0:T(8,128)}, f32[4,128,512]{2,1,0:T(8,128)S(1)}, u32[]{:S(2)}) %copy-start.10) | copy-done | bytes 1048600
  7.6 0.8 copy-done.16
  8.4 0.8 copy-done.18
  9.1 0.7 copy-done.23
  9.9 0.7 copy-done.30
  10.6 0.7 copy-done.31
  11.3 7.3 %all-to-all-start = ((f32[32,16,128]{2,1,0:T(8,128)}), f32[32,16,128]{2,1,0:T(8,128)S(1)}, u32[]{:S(2)}, u32[]{:S(2)}) async-start(f32[32,16,128]{2,1,0:T(8,128)} %copy-done.23), calls=%async_computation | async-start | bytes 524288 | tf_op jit(solution)/shard_map/all_to_all | solution.py:287
  18.6 0.3 collective-permute-start
  18.9 1.4 %collective-permute-start.1 = (f32[1,128,512]{2,1,0:T(8,128)}, f32[1,128,512]{2,1,0:T(8,128)}, u32[]{:S(2)}, u32[]{:S(2)}) collective-permute-start(f32[1,128,512]{2,1,0:T(8,128)} %copy-done.30), channel_id=1, source_target_pairs={{1,2},{3,4},{5,6},{7,8},{9,10},{11,12},{13,14},{15,16},{17,18},{19... | collective-permute-start | bytes 786440 | tf_op jit(solution)/shard_map/ppermute | solution.py:308
  20.3 8.9 %all-to-all-done.gath_ref = f32[32,16,128]{2,1,0:T(8,128)S(1)} async-done(((f32[32,16,128]{2,1,0:T(8,128)}), f32[32,16,128]{2,1,0:T(8,128)S(1)}, u32[]{:S(2)}, u32[]{:S(2)}) %all-to-all-start) | async-done | bytes 262176 | tf_op jit(solution)/shard_map/all_to_all | solution.py:287
  29.2 0.9 %copy-done.21 = f32[5,32,64]{2,1,0:T(8,128)S(1)} copy-done((f32[5,32,64]{2,1,0:T(8,128)S(1)}, f32[5,32,64]{2,1,0:T(8,128)}, u32[]{:S(2)}) %copy-start.21) | copy-done | bytes 40984
  30.1 0.6 shard_map.87.spread_ref
  30.6 0.0 collective-permute-done.even_ref
  30.7 0.0 collective-permute-done.1.odd_ref
  30.7 0.4 copy-done.17
  31.1 1.2 %copy-done.11 = f32[4,128,512]{2,1,0:T(8,128)S(1)} copy-done((f32[4,128,512]{2,1,0:T(8,128)S(1)}, f32[4,128,512]{2,1,0:T(8,128)}, u32[]{:S(2)}) %copy-start.11) | copy-done | bytes 1048600
  32.3 1.0 %copy-done.19 = bf16[512,512]{1,0:T(8,128)(2,1)S(1)} copy-done((bf16[512,512]{1,0:T(8,128)(2,1)S(1)}, bf16[512,512]{1,0:T(8,128)(2,1)}, u32[]{:S(2)}) %copy-start.19) | copy-done | bytes 524312
  33.4 3.5 %shard_map.88 = (f32[4,128,512]{2,1,0:T(8,128)S(1)}, f32[2,128,512]{2,1,0:T(8,128)S(1)}, f32[4,128,512]{2,1,0:T(8,128)S(1)}, f32[32,24,128]{2,1,0:T(8,128)S(1)},...) custom-call(f32[3,128,512]{2,1,0:T(8,128)S(1)} %shard_map.87.spread_ref, ...), custom_call_target="tpu_custom_call" | custom-call | flops 1610612736 | tf_op jit(solution)/shard_map/pallas_call | solution.py:275
  36.9 0.0 copy-start.2
  36.9 1.0 %copy-done.2 = f32[4,128,512]{2,1,0:T(8,128)} copy-done((f32[4,128,512]{2,1,0:T(8,128)}, f32[4,128,512]{2,1,0:T(8,128)S(1)}, u32[]{:S(2)}) %copy-start.2) | copy-done | bytes 1048600
  37.8 1.0 %copy-done.4 = f32[4,128,512]{2,1,0:T(8,128)} copy-done((f32[4,128,512]{2,1,0:T(8,128)}, f32[4,128,512]{2,1,0:T(8,128)S(1)}, u32[]{:S(2)}) %copy-start.4) | copy-done | bytes 1048600
  38.8 1.0 %copy-done.12 = f32[4,128,512]{2,1,0:T(8,128)} copy-done((f32[4,128,512]{2,1,0:T(8,128)}, f32[4,128,512]{2,1,0:T(8,128)S(1)}, u32[]{:S(2)}) %copy-start.12) | copy-done | bytes 1048600
  39.8 0.8 copy-done.14
  40.6 0.7 copy-done.20
  41.4 0.7 copy-done.28
  42.1 0.7 copy-done.29
  42.8 4.5 %all-to-all-start.1 = ((f32[32,24,128]{2,1,0:T(8,128)}), f32[32,24,128]{2,1,0:T(8,128)S(1)}, u32[]{:S(2)}, u32[]{:S(2)}) async-start(f32[32,24,128]{2,1,0:T(8,128)} %copy-done.20), calls=%async_computation.1 | async-start | bytes 786432 | tf_op jit(solution)/shard_map/all_to_all | solution.py:287
  47.3 0.3 collective-permute-start.2
  47.6 1.4 %collective-permute-start.3 = (f32[1,128,512]{2,1,0:T(8,128)}, f32[1,128,512]{2,1,0:T(8,128)}, u32[]{:S(2)}, u32[]{:S(2)}) collective-permute-start(f32[1,128,512]{2,1,0:T(8,128)} %copy-done.28), channel_id=1, source_target_pairs={{1,2},{3,4},{5,6},{7,8},{9,10},{11,12},{13,14},{15,16},{17,18},{19... | collective-permute-start | bytes 786440 | tf_op jit(solution)/shard_map/ppermute | solution.py:308
  49.0 11.6 %all-to-all-done.1.gath_ref = f32[32,24,128]{2,1,0:T(8,128)S(1)} async-done(((f32[32,24,128]{2,1,0:T(8,128)}), f32[32,24,128]{2,1,0:T(8,128)S(1)}, u32[]{:S(2)}, u32[]{:S(2)}) %all-to-all-start.1) | async-done | bytes 393248 | tf_op jit(solution)/shard_map/all_to_all | solution.py:287
  60.6 0.9 %copy-done.9 = f32[512,64]{0,1:T(8,128)S(1)} copy-done((f32[512,64]{0,1:T(8,128)S(1)}, f32[512,64]{0,1:T(8,128)}, u32[]{:S(2)}) %copy-start.9) | copy-done | bytes 131096
  61.5 0.9 %copy-done.22 = f32[5,32,64]{2,1,0:T(8,128)S(1)} copy-done((f32[5,32,64]{2,1,0:T(8,128)S(1)}, f32[5,32,64]{2,1,0:T(8,128)}, u32[]{:S(2)}) %copy-start.22) | copy-done | bytes 40984
  62.4 0.6 shard_map.89.spread_ref
  62.9 0.0 collective-permute-done.2.even_ref
  63.0 0.6 copy-done.3
  63.6 1.2 %copy-done.5 = f32[4,128,512]{2,1,0:T(8,128)S(1)} copy-done((f32[4,128,512]{2,1,0:T(8,128)S(1)}, f32[4,128,512]{2,1,0:T(8,128)}, u32[]{:S(2)}) %copy-start.5) | copy-done | bytes 1048600
  64.8 1.2 %copy-done.13 = f32[4,128,512]{2,1,0:T(8,128)S(1)} copy-done((f32[4,128,512]{2,1,0:T(8,128)S(1)}, f32[4,128,512]{2,1,0:T(8,128)}, u32[]{:S(2)}) %copy-start.13) | copy-done | bytes 1048600
  66.0 1.0 %copy-done.15 = f32[2,128,512]{2,1,0:T(8,128)S(1)} copy-done((f32[2,128,512]{2,1,0:T(8,128)S(1)}, f32[2,128,512]{2,1,0:T(8,128)}, u32[]{:S(2)}) %copy-start.15) | copy-done | bytes 524312
  67.1 2.9 %shard_map.90 = (f32[4,128,512]{2,1,0:T(8,128)S(1)}, f32[4,128,512]{2,1,0:T(8,128)S(1)}, f32[32,128]{1,0:T(8,128)S(1)}) custom-call(f32[32,24,128]{2,1,0:T(8,128)S(1)} %all-to-all-done.1.gath_ref, f32[3,128,512]{2,1,0:T(8,128)S(1)} %shard_map.89.spread_ref, f32[4,128,512]{2,1,0:T(8,128)S(1)} %copy-done.13, f32[1,128,512]{2,1,0:T(8,128)} %collective-permute-done.2.even_ref, ...), custom_call_target="tpu_custom_call" | custom-call | flops 805306368 | tf_op jit(solution)/shard_map/pallas_call | solution.py:275
  70.0 9.7 %all_to_all.21 = f32[32,1,128]{2,1,0:T(1,128)S(1)} all-to-all(f32[32,1,128]{2,1,0:T(1,128)S(1)} %bitcast.15), channel_id=1, replica_groups=mesh['sub'=32] {'sub'}, dimensions={0} | all-to-all | bytes 32768 | tf_op jit(solution)/shard_map/all_to_all | solution.py:287
  79.7 1.9 %shard_map.91 = (f32[4,128,512]{2,1,0:T(8,128)}, f32[4,128,512]{2,1,0:T(8,128)}) custom-call(f32[32,128]{1,0:T(8,128)S(1)} %bitcast.14, f32[32,24,128]{2,1,0:T(8,128)S(1)} %all-to-all-done.1.gath_ref, f32[4,128,512]{2,1,0:T(8,128)S(1)} %get-tuple-element.23.r_ref, f32[4,128,512]{2,1,0:T(8,128)S(1)} %copy-done.3, f32[4,128,512]{2,1,0:T(8,128)S(1)} %copy-done.6, ...), custom_call_target="tpu_custom_call" | custom-call | flops 100663296 | tf_op jit(solution)/shard_map/pallas_call | solution.py:275
  (35 shorter events, 0.1 us)
Async XLA Ops:
  0.6 0.9 %copy-start.7 = (f32[512,64]{0,1:T(8,128)S(1)}, f32[512,64]{0,1:T(8,128)}, u32[]{:S(2)}) copy-start(f32[512,64]{0,1:T(8,128)} %param.12) | copy-start | bytes 393220
  1.5 0.7 copy-start.24
  2.3 1.2 %copy-start.26 = (f32[4,128,512]{2,1,0:T(8,128)S(1)}, f32[4,128,512]{2,1,0:T(8,128)}, u32[]{:S(2)}) copy-start(f32[4,128,512]{2,1,0:T(8,128)} %r_hbm.1) | copy-start | bytes 3145732
  3.5 1.2 %copy-start.27 = (f32[1,512,512]{2,1,0:T(8,128)S(1)}, f32[1,512,512]{2,1,0:T(8,128)}, u32[]{:S(2)}) copy-start(f32[1,512,512]{2,1,0:T(8,128)} %inv_hbm.1) | copy-start | bytes 3145732
  4.7 24.5 %copy-start.8 = (f32[512,64]{0,1:T(8,128)S(1)}, f32[512,64]{0,1:T(8,128)}, u32[]{:S(2)}) copy-start(f32[512,64]{0,1:T(8,128)} %param.12) | copy-start | bytes 393220
  4.7 24.5 %copy-start.25 = (f32[128,32]{0,1:T(8,128)S(1)}, f32[128,32]{0,1:T(8,128)}, u32[]{:S(2)}) copy-start(f32[128,32]{0,1:T(8,128)} %param.11) | copy-start | bytes 49156
  4.7 26.0 %copy-start.1 = (f32[4,128,512]{2,1,0:T(8,128)S(1)}, f32[4,128,512]{2,1,0:T(8,128)}, u32[]{:S(2)}) copy-start(f32[4,128,512]{2,1,0:T(8,128)} %wind_ref.3) | copy-start | bytes 3145732
  6.6 1.0 %copy-start.10 = (f32[4,128,512]{2,1,0:T(8,128)}, f32[4,128,512]{2,1,0:T(8,128)S(1)}, u32[]{:S(2)}) copy-start(f32[4,128,512]{2,1,0:T(8,128)S(1)} %get-tuple-element.20.local_ref) | copy-start | bytes 3145732
  7.6 0.8 copy-start.16
  8.3 0.8 copy-start.18
  9.1 0.7 copy-start.23
  9.9 0.7 copy-start.30
  10.6 0.7 copy-start.31
  11.3 19.4 %copy-start = (f32[4,128,512]{2,1,0:T(8,128)S(1)}, f32[4,128,512]{2,1,0:T(8,128)}, u32[]{:S(2)}) copy-start(f32[4,128,512]{2,1,0:T(8,128)} %sigma_ref.3) | copy-start | bytes 3145732
  11.3 17.9 %all-to-all-start = ((f32[32,16,128]{2,1,0:T(8,128)}), f32[32,16,128]{2,1,0:T(8,128)S(1)}, u32[]{:S(2)}, u32[]{:S(2)}) async-start(f32[32,16,128]{2,1,0:T(8,128)} %copy-done.23), calls=%async_computation | async-start | bytes 524288 | tf_op jit(solution)/shard_map/all_to_all | solution.py:287
  18.6 12.0 %collective-permute-start = (f32[1,128,512]{2,1,0:T(8,128)}, f32[1,128,512]{2,1,0:T(8,128)}, u32[]{:S(2)}, u32[]{:S(2)}) collective-permute-start(f32[1,128,512]{2,1,0:T(8,128)} %copy-done.31), channel_id=1, source_target_pairs={{0,1},{1,0},{2,3},{3,2},{4,5},{5,4},{6,7},{7,6},{8,9},{9,8},{10,11... | collective-permute-start | bytes 786440 | tf_op jit(solution)/shard_map/ppermute | solution.py:307
  18.9 11.7 %collective-permute-start.1 = (f32[1,128,512]{2,1,0:T(8,128)}, f32[1,128,512]{2,1,0:T(8,128)}, u32[]{:S(2)}, u32[]{:S(2)}) collective-permute-start(f32[1,128,512]{2,1,0:T(8,128)} %copy-done.30), channel_id=1, source_target_pairs={{1,2},{3,4},{5,6},{7,8},{9,10},{11,12},{13,14},{15,16},{17,18},{19... | collective-permute-start | bytes 786440 | tf_op jit(solution)/shard_map/ppermute | solution.py:308
  29.2 0.9 %copy-start.21 = (f32[5,32,64]{2,1,0:T(8,128)S(1)}, f32[5,32,64]{2,1,0:T(8,128)}, u32[]{:S(2)}) copy-start(f32[5,32,64]{2,1,0:T(8,128)} %gamma_ref.3) | copy-start | bytes 122884
  30.1 1.0 %copy-start.17 = (bf16[512,512]{1,0:T(8,128)(2,1)S(1)}, bf16[512,512]{1,0:T(8,128)(2,1)}, u32[]{:S(2)}) copy-start(bf16[512,512]{1,0:T(8,128)(2,1)} %copy-done.16) | copy-start | bytes 1572868
  31.1 1.2 %copy-start.11 = (f32[4,128,512]{2,1,0:T(8,128)S(1)}, f32[4,128,512]{2,1,0:T(8,128)}, u32[]{:S(2)}) copy-start(f32[4,128,512]{2,1,0:T(8,128)} %copy-done.10) | copy-start | bytes 3145732
  32.3 1.0 %copy-start.19 = (bf16[512,512]{1,0:T(8,128)(2,1)S(1)}, bf16[512,512]{1,0:T(8,128)(2,1)}, u32[]{:S(2)}) copy-start(bf16[512,512]{1,0:T(8,128)(2,1)} %copy-done.18) | copy-start | bytes 1572868
  36.9 1.0 %copy-start.2 = (f32[4,128,512]{2,1,0:T(8,128)}, f32[4,128,512]{2,1,0:T(8,128)S(1)}, u32[]{:S(2)}) copy-start(f32[4,128,512]{2,1,0:T(8,128)S(1)} %get-tuple-element.30.z_ref) | copy-start | bytes 3145732
  37.8 1.0 %copy-start.4 = (f32[4,128,512]{2,1,0:T(8,128)}, f32[4,128,512]{2,1,0:T(8,128)S(1)}, u32[]{:S(2)}) copy-start(f32[4,128,512]{2,1,0:T(8,128)S(1)} %get-tuple-element.32.w_ref) | copy-start | bytes 3145732
  38.8 1.0 %copy-start.12 = (f32[4,128,512]{2,1,0:T(8,128)}, f32[4,128,512]{2,1,0:T(8,128)S(1)}, u32[]{:S(2)}) copy-start(f32[4,128,512]{2,1,0:T(8,128)S(1)} %get-tuple-element.27.local_ref) | copy-start | bytes 3145732
  39.8 0.8 copy-start.14
  40.6 0.8 copy-start.20
  41.3 0.7 copy-start.28
  42.1 0.7 copy-start.29
  42.8 17.8 %all-to-all-start.1 = ((f32[32,24,128]{2,1,0:T(8,128)}), f32[32,24,128]{2,1,0:T(8,128)S(1)}, u32[]{:S(2)}, u32[]{:S(2)}) async-start(f32[32,24,128]{2,1,0:T(8,128)} %copy-done.20), calls=%async_computation.1 | async-start | bytes 786432 | tf_op jit(solution)/shard_map/all_to_all | solution.py:287
  47.3 15.6 %collective-permute-start.2 = (f32[1,128,512]{2,1,0:T(8,128)}, f32[1,128,512]{2,1,0:T(8,128)}, u32[]{:S(2)}, u32[]{:S(2)}) collective-permute-start(f32[1,128,512]{2,1,0:T(8,128)} %copy-done.29), channel_id=1, source_target_pairs={{0,1},{1,0},{2,3},{3,2},{4,5},{5,4},{6,7},{7,6},{8,9},{9,8},{10,11... | collective-permute-start | bytes 786440 | tf_op jit(solution)/shard_map/ppermute | solution.py:307
  47.6 15.3 %collective-permute-start.3 = (f32[1,128,512]{2,1,0:T(8,128)}, f32[1,128,512]{2,1,0:T(8,128)}, u32[]{:S(2)}, u32[]{:S(2)}) collective-permute-start(f32[1,128,512]{2,1,0:T(8,128)} %copy-done.28), channel_id=1, source_target_pairs={{1,2},{3,4},{5,6},{7,8},{9,10},{11,12},{13,14},{15,16},{17,18},{19... | collective-permute-start | bytes 786440 | tf_op jit(solution)/shard_map/ppermute | solution.py:308
  60.6 0.9 %copy-start.9 = (f32[512,64]{0,1:T(8,128)S(1)}, f32[512,64]{0,1:T(8,128)}, u32[]{:S(2)}) copy-start(f32[512,64]{0,1:T(8,128)} %param.12) | copy-start | bytes 393220
  61.5 0.9 %copy-start.22 = (f32[5,32,64]{2,1,0:T(8,128)S(1)}, f32[5,32,64]{2,1,0:T(8,128)}, u32[]{:S(2)}) copy-start(f32[5,32,64]{2,1,0:T(8,128)} %gamma_ref.3) | copy-start | bytes 122884
  62.4 1.2 %copy-start.3 = (f32[4,128,512]{2,1,0:T(8,128)S(1)}, f32[4,128,512]{2,1,0:T(8,128)}, u32[]{:S(2)}) copy-start(f32[4,128,512]{2,1,0:T(8,128)} %copy-done.2) | copy-start | bytes 3145732
  63.6 1.2 %copy-start.5 = (f32[4,128,512]{2,1,0:T(8,128)S(1)}, f32[4,128,512]{2,1,0:T(8,128)}, u32[]{:S(2)}) copy-start(f32[4,128,512]{2,1,0:T(8,128)} %copy-done.4) | copy-start | bytes 3145732
  64.8 1.2 %copy-start.13 = (f32[4,128,512]{2,1,0:T(8,128)S(1)}, f32[4,128,512]{2,1,0:T(8,128)}, u32[]{:S(2)}) copy-start(f32[4,128,512]{2,1,0:T(8,128)} %copy-done.12) | copy-start | bytes 3145732
  66.0 1.0 %copy-start.15 = (f32[2,128,512]{2,1,0:T(8,128)S(1)}, f32[2,128,512]{2,1,0:T(8,128)}, u32[]{:S(2)}) copy-start(f32[2,128,512]{2,1,0:T(8,128)} %copy-done.14) | copy-start | bytes 1572868
  67.1 12.6 %copy-start.6 = (f32[4,128,512]{2,1,0:T(8,128)S(1)}, f32[4,128,512]{2,1,0:T(8,128)}, u32[]{:S(2)}) copy-start(f32[4,128,512]{2,1,0:T(8,128)} %copy-done.4) | copy-start | bytes 3145732

commit v3 on v2

--- a/solution.py
+++ b/solution.py
@@ -50,42 +50,55 @@
     return pack(dot3(halves(by), halves(half)), fold)
 
 
-def coarse_of(gath_ref, gamma_ref, tree_ref, rows, layers, fold, levels, count):
-    below = None
-    base = 0
-    offsets = []
-    for level in range(levels):
-        size = count >> (level + 1)
+def join_kernel(got_ref, own_ref, out_ref, *, rows, width, extra):
+    each = rows // 2
+    first = got_ref.shape[0] - each
+    both = got_ref[first:] + own_ref[first:]
+    half = jnp.where(even_here(), both[:, :width], both[:, width : 2 * width])
+    if not extra:
+        for i in range(out_ref.shape[0] // each):
+            out_ref[i * each : (i + 1) * each] = half
+        return
+    sums = [full_sum(both[i : i + 1, 2 * width : 2 * width + LANES]) for i in range(3)]
+    lane = lax.broadcasted_iota(jnp.int32, (1, width), 1)
+    row = jnp.where(
+        lane == 0, sums[0], jnp.where(lane == 1, sums[1], jnp.where(lane == 2, sums[2], 0.0))
+    )
+    block = jnp.concatenate([half, row], axis=0)
+    size = each + 1
+    for i in range(out_ref.shape[0] // size):
+        out_ref[i * size : (i + 1) * size] = block
+
+
+def coarse_kernel(
+    gath_ref, by_ref, bz_ref, gamma_ref, out_ref, tree_ref, *, fold, levels, count, rows, layers
+):
+    each = rows // 2
+    stride = gath_ref.shape[0] // count
+    for i in range(count):
+        tree_ref[i // 2, (i % 2) * each : (i % 2 + 1) * each] = gath_ref[
+            i * stride : i * stride + each
+        ]
+    offsets = [0]
+    for level in range(1, levels):
+        base, size = offsets[-1] + (count >> level), count >> (level + 1)
+        pairs = tree_ref[offsets[-1] : base].reshape((size, 2) + tree_ref.shape[1:])
+        tree_ref[base : base + size] = pairs[:, 0] + pairs[:, 1]
         offsets.append(base)
-        if level == 0:
-            pairs = gath_ref[:, :rows, :].reshape(size, 2, rows, -1)
-        else:
-            pairs = below.reshape(size, 2, rows, -1)
-        below = pairs[:, 0] + pairs[:, 1]
-        tree_ref[pl.ds(base, size)] = below
-        base += size
     scaled = [
         pack(gamma_ref[level], fold) * (1.0 / (layers * 2.0 ** (level + 1)) ** 0.5)
         for level in range(levels)
     ]
     me = lax.axis_index(AXIS)
-    out = []
+    coarse = []
     for shift in (-1, 0, 1):
         who = jnp.clip(me + shift, 0, count - 1)
         total = scaled[0] * tree_ref[offsets[0] + (who >> 1)]
         for level in range(1, levels):
             total = total + scaled[level] * tree_ref[offsets[level] + (who >> (level + 1))]
         if shift:
-            inside = (me + shift == who).astype(F32)
-            total = total * inside
-        out.append(unpack(total, fold))
-    return out
-
-
-def coarse_kernel(
-    gath_ref, by_ref, bz_ref, gamma_ref, out_ref, tree_ref, *, fold, levels, count, rows, layers
-):
-    coarse = coarse_of(gath_ref, gamma_ref, tree_ref, rows, layers, fold, levels, count)
+            total = total * (me + shift == who).astype(F32)
+        coarse.append(unpack(total, fold))
     ky = by_ref.shape[0]
     back = dot3(halves(jnp.concatenate(coarse, axis=0)), halves(bz_ref[...]))
     back_high, back_low = halves(back)
@@ -128,16 +141,27 @@
     return lax.rem(lax.axis_index(AXIS), 2) == 0
 
 
-def send_edges(local_ref, even_ref, odd_ref):
-    layers = local_ref.shape[0]
+def send_edges(local_ref, pair_ref, odd_ref):
+    layers, ny, _ = local_ref.shape
     even = even_here()
-    even_ref[0] = local_ref[jnp.where(even, layers - 1, 0)]
+    pair_ref[:ny] = local_ref[jnp.where(even, layers - 1, 0)]
     odd_ref[0] = local_ref[jnp.where(even, 0, layers - 1)]
+
+
+def send_proj(packed, scalars, pair_ref, ny):
+    each = packed.shape[0] // 2
+    parts = [packed[:each], packed[each:]]
+    if scalars:
+        parts.append(jnp.concatenate(scalars + [jnp.zeros((each - len(scalars), LANES), F32)], axis=0))
+    used = sum(p.shape[1] for p in parts)
+    if used < pair_ref.shape[1]:
+        parts.append(jnp.zeros((each, pair_ref.shape[1] - used), F32))
+    pair_ref[ny:] = jnp.concatenate(parts, axis=1)
 
 
 def first_kernel(
     r_hbm, inv_hbm, by_ref, bz_ref,
-    out_ref, r_ref, high_ref, low_ref, local_ref, even_ref, odd_ref,
+    pair_ref, r_ref, high_ref, low_ref, local_ref, odd_ref,
     inv_ref, sems, *, fold,
 ):
     layers = r_ref.shape[0]
@@ -151,24 +175,24 @@
         loads[x].wait()
         summed = summed + r_ref[x]
     packed = project(summed, by_ref[...], bz_ref[...], fold)
-    out_ref[...] = jnp.broadcast_to(packed[None], out_ref.shape)
+    send_proj(packed, [], pair_ref, r_ref.shape[1])
     loads[layers].wait()
     inverse = halves(inv_ref[...])
     high_ref[...], low_ref[...] = inverse
     for x in range(layers):
         local_ref[x] = dot3(halves(r_ref[x]), inverse)
-    send_edges(local_ref, even_ref, odd_ref)
+    send_edges(local_ref, pair_ref, odd_ref)
 
 
 def middle_kernel(
     spread_ref, local_ref, even_ref, odd_ref, r_ref, sigma_ref, wind_ref, by_ref, bz_ref,
     high_ref, low_ref,
-    z_ref, edge_ref, w_ref, out_ref, local2_ref, even2_ref, odd2_ref, *, fold, count, rows,
+    z_ref, edge_ref, w_ref, pair2_ref, local2_ref, odd2_ref, *, fold,
 ):
     layers = r_ref.shape[0]
     before, own, after = (spread_ref[i] for i in range(3))
     even = even_here().astype(F32)
-    from_pair = even_ref[0]
+    from_pair = even_ref[: r_ref.shape[1]]
     from_other = odd_ref[0]
     edge_ref[0] = before + (from_other * even + from_pair * (1.0 - even))
     edge_ref[1] = after + (from_pair * even + from_other * (1.0 - even))
@@ -189,20 +213,24 @@
             rr, rw, ww = rr + parts[0], rw + parts[1], ww + parts[2]
             summed = summed + w
     packed = project(summed, by_ref[...], bz_ref[...], fold)
-    scalars = jnp.concatenate([rr, rw, ww, jnp.zeros((5, LANES), F32)], axis=0)
-    out_ref[:, :rows, :] = jnp.broadcast_to(packed[None], (count,) + packed.shape)
-    out_ref[:, rows:, :] = jnp.broadcast_to(scalars[None], (count,) + scalars.shape)
+    send_proj(packed, [rr, rw, ww], pair2_ref, r_ref.shape[1])
     inverse = (high_ref[...], low_ref[...])
     for x in range(layers):
         local2_ref[x] = dot3(halves(w_ref[x]), inverse)
-    send_edges(local2_ref, even2_ref, odd2_ref)
+    send_edges(local2_ref, pair2_ref, odd2_ref)
+
+
+def lane_of(row, which):
+    lane = lax.broadcasted_iota(jnp.int32, row.shape, 1)
+    return full_sum(jnp.where(lane == which, row, 0.0))
 
 
 def first_scalars(gath_ref, rows):
-    sums = jnp.sum(gath_ref[:, rows:, :], axis=0)
-    rr = full_sum(sums[0:1])
-    rw = full_sum(sums[1:2])
-    ww = full_sum(sums[2:3])
+    size = rows // 2 + 1
+    row = gath_ref[size - 1 : size]
+    for i in range(2, gath_ref.shape[0] // size, 2):
+        row = row + gath_ref[(i + 1) * size - 1 : (i + 1) * size]
+    rr, rw, ww = (lane_of(row, i) for i in range(3))
     inv_rr = 1.0 / rr
     beta = jnp.sqrt(rr)
     h11 = rw * inv_rr
@@ -219,7 +247,7 @@
     scale = 1.0 / (h21 * beta)
     before, own, after = (spread_ref[i] for i in range(3))
     even = even_here().astype(F32)
-    from_pair = even_ref[0]
+    from_pair = even_ref[: r_ref.shape[1]]
     from_other = odd_ref[0]
     edge2_ref[0] = scale * (
         before + (from_other * even + from_pair * (1.0 - even)) - h11 * edge_ref[0]
@@ -251,10 +279,9 @@
 ):
     beta, h11, h21 = first_scalars(gath_ref, rows)
     sums = jnp.sum(sums_ref[...], axis=0, keepdims=True)
-    lane = lax.broadcasted_iota(jnp.int32, sums.shape, 1)
-    h12 = full_sum(jnp.where(lane == 0, sums, 0.0)) / beta
-    h22 = full_sum(jnp.where(lane == 1, sums, 0.0))
-    h32 = jnp.sqrt(full_sum(jnp.where(lane == 2, sums, 0.0)) - h12 * h12 - h22 * h22)
+    h12 = lane_of(sums, 0) / beta
+    h22 = lane_of(sums, 1)
+    h32 = jnp.sqrt(lane_of(sums, 2) - h12 * h12 - h22 * h22)
     m11 = h11 * h11 + h21 * h21
     m12 = h11 * h12 + h21 * h22
     m22 = h12 * h12 + h22 * h22 + h32 * h32
@@ -302,38 +329,45 @@
     others = others + [(j, i) for i, j in others]
     matmul = 6 * layers * ny * nz * nz
     by, bz = basis_y.T, basis_z.T
-
-    def round_of(sent, even, odd):
-        even = lax.ppermute(even, AXIS, pairs)
+    each = rows // 2
+    pair = (ny + each, nz)
+
+    def round_of(sent, odd, extra):
+        got = lax.ppermute(sent, AXIS, pairs)
         odd = lax.ppermute(odd, AXIS, others)
-        gathered = exchange(sent)
+        size = each + extra
+        (block,) = call(
+            functools.partial(join_kernel, rows=rows, width=width, extra=extra),
+            [(count * size, width)], (got, sent), flops=matmul // 16,
+        )
+        block = exchange(block.reshape(count * size, 1, width)).reshape(count * size, width)
         (spread,) = call(
             functools.partial(
                 coarse_kernel, fold=fold, levels=levels, count=count, rows=rows, layers=layers
             ),
-            [(3, ny, nz)], (gathered, by, bz, gamma), [(count, rows, width)],
+            [(3, ny, nz)], (block, by, bz, gamma), [(count, rows, width)],
             flops=matmul // 8,
         )
-        return gathered, spread, even, odd
-
-    sent, r, high, low, local, even, odd = call(
+        return block, spread, got, odd
+
+    sent, r, high, low, local, odd = call(
         functools.partial(first_kernel, fold=fold),
-        [(count, rows, width), field, square, square, field, edge, edge],
+        [pair, field, square, square, field, edge],
         (right_side, local_inverse, by, bz),
         [(nz, nz), pltpu.SemaphoreType.DMA((layers + 1,))], flops=matmul, hbm=(0, 1),
     )
-    _, spread, even, odd = round_of(sent, even, odd)
-    z, edges, w, sent, local, even, odd = call(
-        functools.partial(middle_kernel, fold=fold, count=count, rows=rows),
-        [field, (2, ny, nz), field, (count, rows + 8, width), field, edge, edge],
-        (spread, local, even, odd, r, sigma, wind, by, bz, high, low),
+    _, spread, got, odd = round_of(sent, odd, 0)
+    z, edges, w, sent, local, odd = call(
+        functools.partial(middle_kernel, fold=fold),
+        [field, (2, ny, nz), field, pair, field, edge],
+        (spread, local, got, odd, r, sigma, wind, by, bz, high, low),
         flops=2 * matmul,
     )
-    gathered, spread, even, odd = round_of(sent, even, odd)
+    gathered, spread, got, odd = round_of(sent, odd, 1)
     z2, u, sent = call(
         functools.partial(last_kernel, rows=rows),
         [field, field, (count, LANES)],
-        (gathered, spread, local, even, odd, r, z, edges, w, sigma, wind),
+        (gathered, spread, local, got, odd, r, z, edges, w, sigma, wind),
         [(2, ny, nz)], flops=matmul,
     )
     sums = exchange(sent)

time: 82.4 us -> 82.8 us (level)
  waiting for transfers between devices: 20.5 us -> 16.4 us
  blocking collectives: 9.7 us -> 13.6 us
  local copies, waits for them, and re-layouts: 24.1 us -> 21 us
  starting transfers between devices: 15.2 us -> 18.3 us
    all_to_all x2, waiting for transfers between devices: 20.5 us -> 14 us  [exchange(): return lax.all_to_all(block, AXIS, 0, 0, tiled=True)]
    all_to_all x1, blocking collectives: 9.7 us -> 13.6 us  [exchange(): return lax.all_to_all(block, AXIS, 0, 0, tiled=True)]
    unnamed x64 -> x62, local copies, waits for them, and re-layouts: 24.1 us -> 21 us
    ppermute x2, waiting for transfers between devices: 0.01 us -> 2.37 us  [round_of(): got = lax.ppermute(sent, AXIS, pairs)]
    ppermute x2, starting transfers between devices: 0.63 us -> 2.49 us  [round_of(): got = lax.ppermute(sent, AXIS, pairs)]
    all_to_all x2, starting transfers between devices: 11.8 us -> 13.1 us  [exchange(): return lax.all_to_all(block, AXIS, 0, 0, tiled=True)]
    pallas_call x6 -> x8, Pallas kernels: 11.3 us -> 11.9 us  [call(): pl.pallas_call(kernel, out_shape=outs, in_specs=[far if i in hbm else vme...]
  transfers between devices with their start and end apart: 6 -> 6, of which waited for: 2 -> 4; matrix products, arithmetic and copies ran while one was open for 0% -> 0% of each run, Pallas kernels for 1% -> 1%
where the time goes in v3:
time: 82.8 us; the launch traced here: 82 us
  local copies, waits for them, and re-layouts  21 us (25%)
  starting transfers between devices  18.3 us (22%)
  waiting for transfers between devices  16.4 us (20%)
  blocking collectives  13.6 us (16%)
  Pallas kernels  11.9 us (14%)
    unnamed x62, local copies, waits for them, and re-layouts  21 us
    all_to_all x2, waiting for transfers between devices, exchange(): return lax.all_to_all(block, AXIS, 0, 0, tiled=True)  14 us
    all_to_all x1, blocking collectives, exchange(): return lax.all_to_all(block, AXIS, 0, 0, tiled=True)  13.6 us
    all_to_all x2, starting transfers between devices, exchange(): return lax.all_to_all(block, AXIS, 0, 0, tiled=True)  13.1 us
    pallas_call x8, Pallas kernels, call(): pl.pallas_call(kernel, out_shape=outs, in_specs=[far if i in hbm else vme...  11.9 us
    ppermute x2, starting transfers between devices, round_of(): odd = lax.ppermute(odd, AXIS, others)  2.74 us
    ppermute x2, starting transfers between devices, round_of(): got = lax.ppermute(sent, AXIS, pairs)  2.49 us
    ppermute x2, waiting for transfers between devices, round_of(): got = lax.ppermute(sent, AXIS, pairs)  2.37 us
  transfers between devices with their start and end apart: 6, of which 4 were waited for; matrix products, arithmetic and copies ran while one was open for 0% of the time, Pallas kernels for 1%

profile of v3, /device:TPU:0, one launch (start us, length us, event | category | flops | bytes accessed | tf_op | source)
XLA Modules:
  0.0 82.0 jit_solution(17528957073740733926)
XLA Ops:
  0.6 0.0 copy-start.7
  0.6 0.9 %copy-done.7 = f32[512,64]{0,1:T(8,128)S(1)} copy-done((f32[512,64]{0,1:T(8,128)S(1)}, f32[512,64]{0,1:T(8,128)}, u32[]{:S(2)}) %copy-start.7) | copy-done | bytes 131096
  1.5 0.7 copy-done.25
  2.3 1.2 %copy-done.27 = f32[4,128,512]{2,1,0:T(8,128)S(1)} copy-done((f32[4,128,512]{2,1,0:T(8,128)S(1)}, f32[4,128,512]{2,1,0:T(8,128)}, u32[]{:S(2)}) %copy-start.27) | copy-done | bytes 1048600
  3.5 1.2 %copy-done.28 = f32[1,512,512]{2,1,0:T(8,128)S(1)} copy-done((f32[1,512,512]{2,1,0:T(8,128)S(1)}, f32[1,512,512]{2,1,0:T(8,128)}, u32[]{:S(2)}) %copy-start.28) | copy-done | bytes 1048600
  4.7 1.8 %shard_map.86 = (f32[136,512]{1,0:T(8,128)S(1)}, f32[4,128,512]{2,1,0:T(8,128)S(1)}, bf16[512,512]{1,0:T(8,128)(2,1)S(1)}, bf16[512,512]{1,0:T(8,128)(2,1)S(1)},...) custom-call(f32[4,128,512]{2,1,0:T(8,128)S(1)} %copy-done.27, f32[1,512,512]{2,1,0:T(8,128)S(1)} %copy-done.28, ...), custom_call_target="tpu_custom_call" | custom-call | flops 805306368 | tf_op jit(solution)/shard_map/pallas_call | solution.py:302
  6.6 0.0 copy-start.13
  6.6 1.0 %copy-done.13 = f32[4,128,512]{2,1,0:T(8,128)} copy-done((f32[4,128,512]{2,1,0:T(8,128)}, f32[4,128,512]{2,1,0:T(8,128)S(1)}, u32[]{:S(2)}) %copy-start.13) | copy-done | bytes 1048600
  7.5 0.8 copy-done.20
  8.3 0.8 copy-done.22
  9.1 0.5 collective-permute-start
  9.6 1.2 %collective-permute-done.got_ref.even_ref = f32[136,512]{1,0:T(8,128)S(1)} collective-permute-done((f32[136,512]{1,0:T(8,128)S(1)}, f32[136,512]{1,0:T(8,128)S(1)}, u32[]{:S(2)}, u32[]{:S(2)}) %collective-permute-start) | collective-permute-done | bytes 278560 | tf_op jit(solution)/shard_map/ppermute | solution.py:336
  10.8 0.7 shard_map.87
  11.5 0.0 copy-done.30
  11.5 0.1 copy-done.9
  11.6 7.2 %all-to-all-start = ((f32[256,1,128]{2,1,0:T(1,128)}), f32[256,1,128]{2,1,0:T(1,128)S(1)}, u32[]{:S(2)}, u32[]{:S(2)}) async-start(f32[256,1,128]{2,1,0:T(1,128)} %bitcast.3), calls=%async_computation | async-start | bytes 262144 | tf_op jit(solution)/shard_map/all_to_all | solution.py:314
  18.8 1.4 %collective-permute-start.1 = (f32[1,128,512]{2,1,0:T(8,128)}, f32[1,128,512]{2,1,0:T(8,128)}, u32[]{:S(2)}, u32[]{:S(2)}) collective-permute-start(f32[1,128,512]{2,1,0:T(8,128)} %copy-done.30), channel_id=1, source_target_pairs={{1,2},{3,4},{5,6},{7,8},{9,10},{11,12},{13,14},{15,16},{17,18},{19... | collective-permute-start | bytes 786440 | tf_op jit(solution)/shard_map/ppermute | solution.py:337
  20.1 6.9 %all-to-all-done = f32[256,1,128]{2,1,0:T(1,128)S(1)} async-done(((f32[256,1,128]{2,1,0:T(1,128)}), f32[256,1,128]{2,1,0:T(1,128)S(1)}, u32[]{:S(2)}, u32[]{:S(2)}) %all-to-all-start) | async-done | bytes 131104 | tf_op jit(solution)/shard_map/all_to_all | solution.py:314
  27.0 0.6 shard_map.88.spread_ref
  27.6 0.0 collective-permute-done.1.odd_ref
  27.7 0.9 %copy-done.10 = f32[136,512]{1,0:T(8,128)S(1)} copy-done((f32[136,512]{1,0:T(8,128)S(1)}, f32[136,512]{1,0:T(8,128)}, u32[]{:S(2)}) %copy-start.10) | copy-done | bytes 278552
  28.6 1.2 %copy-done.14 = f32[4,128,512]{2,1,0:T(8,128)S(1)} copy-done((f32[4,128,512]{2,1,0:T(8,128)S(1)}, f32[4,128,512]{2,1,0:T(8,128)}, u32[]{:S(2)}) %copy-start.14) | copy-done | bytes 1048600
  29.8 1.0 %copy-done.21 = bf16[512,512]{1,0:T(8,128)(2,1)S(1)} copy-done((bf16[512,512]{1,0:T(8,128)(2,1)S(1)}, bf16[512,512]{1,0:T(8,128)(2,1)}, u32[]{:S(2)}) %copy-start.21) | copy-done | bytes 524312
  30.9 1.0 %copy-done.23 = bf16[512,512]{1,0:T(8,128)(2,1)S(1)} copy-done((bf16[512,512]{1,0:T(8,128)(2,1)S(1)}, bf16[512,512]{1,0:T(8,128)(2,1)}, u32[]{:S(2)}) %copy-start.23) | copy-done | bytes 524312
  31.9 3.4 %shard_map.89 = (f32[4,128,512]{2,1,0:T(8,128)S(1)}, f32[2,128,512]{2,1,0:T(8,128)S(1)}, f32[4,128,512]{2,1,0:T(8,128)S(1)}, f32[136,512]{1,0:T(8,128)S(1)}, f32...) custom-call(f32[3,128,512]{2,1,0:T(8,128)S(1)} %shard_map.88.spread_ref, f32[4,128,512]{2,1,0:T(8,128)S(1)} %copy-done.14, ...), custom_call_target="tpu_custom_call" | custom-call | flops 1610612736 | tf_op jit(solution)/shard_map/pallas_call | solution.py:302
  35.3 0.0 copy-start.2
  35.3 1.0 %copy-done.2 = f32[4,128,512]{2,1,0:T(8,128)} copy-done((f32[4,128,512]{2,1,0:T(8,128)}, f32[4,128,512]{2,1,0:T(8,128)S(1)}, u32[]{:S(2)}) %copy-start.2) | copy-done | bytes 1048600
  36.3 1.0 %copy-done.4 = f32[4,128,512]{2,1,0:T(8,128)} copy-done((f32[4,128,512]{2,1,0:T(8,128)}, f32[4,128,512]{2,1,0:T(8,128)S(1)}, u32[]{:S(2)}) %copy-start.4) | copy-done | bytes 1048600
  37.3 1.0 %copy-done.15 = f32[4,128,512]{2,1,0:T(8,128)} copy-done((f32[4,128,512]{2,1,0:T(8,128)}, f32[4,128,512]{2,1,0:T(8,128)S(1)}, u32[]{:S(2)}) %copy-start.15) | copy-done | bytes 1048600
  38.3 0.8 copy-done.18
  39.1 2.0 %collective-permute-start.2 = (f32[136,512]{1,0:T(8,128)S(1)}, f32[136,512]{1,0:T(8,128)S(1)}, u32[]{:S(2)}, u32[]{:S(2)}) collective-permute-start(f32[136,512]{1,0:T(8,128)S(1)} %get-tuple-element.23.own_ref), channel_id=1, source_target_pairs={{0,1},{1,0},{2,3},{3,2},{4,5},{5,4},{6,7},{7,6},{8,9},{9,8},{10,11... | collective-permute-start | bytes 835592 | tf_op jit(solution)/shard_map/ppermute | solution.py:336
  41.1 1.2 %collective-permute-done.2.got_ref.even_ref = f32[136,512]{1,0:T(8,128)S(1)} collective-permute-done((f32[136,512]{1,0:T(8,128)S(1)}, f32[136,512]{1,0:T(8,128)S(1)}, u32[]{:S(2)}, u32[]{:S(2)}) %collective-permute-start.2) | collective-permute-done | bytes 278560 | tf_op jit(solution)/shard_map/ppermute | solution.py:336
  42.2 0.1 shard_map.90
  42.4 0.6 copy-done.11
  42.9 0.7 copy-done.17
  43.6 5.9 %all-to-all-start.1 = ((f32[288,1,128]{2,1,0:T(1,128)}), f32[288,1,128]{2,1,0:T(1,128)S(1)}, u32[]{:S(2)}, u32[]{:S(2)}) async-start(f32[288,1,128]{2,1,0:T(1,128)} %bitcast.21), calls=%async_computation.1 | async-start | bytes 294912 | tf_op jit(solution)/shard_map/all_to_all | solution.py:314
  49.5 1.4 %collective-permute-start.3 = (f32[1,128,512]{2,1,0:T(8,128)}, f32[1,128,512]{2,1,0:T(8,128)}, u32[]{:S(2)}, u32[]{:S(2)}) collective-permute-start(f32[1,128,512]{2,1,0:T(8,128)} %copy-done.29), channel_id=1, source_target_pairs={{1,2},{3,4},{5,6},{7,8},{9,10},{11,12},{13,14},{15,16},{17,18},{19... | collective-permute-start | bytes 786440 | tf_op jit(solution)/shard_map/ppermute | solution.py:337
  50.9 7.1 %all-to-all-done.1 = f32[288,1,128]{2,1,0:T(1,128)S(1)} async-done(((f32[288,1,128]{2,1,0:T(1,128)}), f32[288,1,128]{2,1,0:T(1,128)S(1)}, u32[]{:S(2)}, u32[]{:S(2)}) %all-to-all-start.1) | async-done | bytes 147488 | tf_op jit(solution)/shard_map/all_to_all | solution.py:314
  58.0 0.6 shard_map.91.spread_ref
  58.6 0.0 collective-permute-done.3.odd_ref
  58.6 0.6 copy-done.3
  59.2 1.2 %copy-done.5 = f32[4,128,512]{2,1,0:T(8,128)S(1)} copy-done((f32[4,128,512]{2,1,0:T(8,128)S(1)}, f32[4,128,512]{2,1,0:T(8,128)}, u32[]{:S(2)}) %copy-start.5) | copy-done | bytes 1048600
  60.5 1.0 %copy-done.12 = f32[136,512]{1,0:T(8,128)S(1)} copy-done((f32[136,512]{1,0:T(8,128)S(1)}, f32[136,512]{1,0:T(8,128)}, u32[]{:S(2)}) %copy-start.12) | copy-done | bytes 278552
  61.4 1.2 %copy-done.16 = f32[4,128,512]{2,1,0:T(8,128)S(1)} copy-done((f32[4,128,512]{2,1,0:T(8,128)S(1)}, f32[4,128,512]{2,1,0:T(8,128)}, u32[]{:S(2)}) %copy-start.16) | copy-done | bytes 1048600
  62.6 1.0 %copy-done.19 = f32[2,128,512]{2,1,0:T(8,128)S(1)} copy-done((f32[2,128,512]{2,1,0:T(8,128)S(1)}, f32[2,128,512]{2,1,0:T(8,128)}, u32[]{:S(2)}) %copy-start.19) | copy-done | bytes 524312
  63.7 2.8 %shard_map.92 = (f32[4,128,512]{2,1,0:T(8,128)S(1)}, f32[4,128,512]{2,1,0:T(8,128)S(1)}, f32[32,128]{1,0:T(8,128)S(1)}) custom-call(f32[288,128]{1,0:T(8,128)S(1)} %bitcast.15, f32[3,128,512]{2,1,0:T(8,128)S(1)} %shard_map.91.spread_ref, f32[4,128,512]{2,1,0:T(8,128)S(1)} %copy-done.16, f32[136,512]{1,0:T(8,128)S(1)} %copy-done.12, ...), custom_call_target="tpu_custom_call" | custom-call | flops 805306368 | tf_op jit(solution)/shard_map/pallas_call | solution.py:302
  66.5 13.6 %all_to_all.21 = f32[32,1,128]{2,1,0:T(1,128)S(1)} all-to-all(f32[32,1,128]{2,1,0:T(1,128)S(1)} %bitcast.28), channel_id=1, replica_groups=mesh['sub'=32] {'sub'}, dimensions={0} | all-to-all | bytes 32768 | tf_op jit(solution)/shard_map/all_to_all | solution.py:314
  80.1 1.9 %shard_map.93 = (f32[4,128,512]{2,1,0:T(8,128)}, f32[4,128,512]{2,1,0:T(8,128)}) custom-call(f32[32,128]{1,0:T(8,128)S(1)} %bitcast.27, f32[288,128]{1,0:T(8,128)S(1)} %bitcast.16, f32[4,128,512]{2,1,0:T(8,128)S(1)} %get-tuple-element.20.r_ref, f32[4,128,512]{2,1,0:T(8,128)S(1)} %copy-done.3, f32[4,128,512]{2,1,0:T(8,128)S(1)} %copy-done.6, ...), custom_call_target="tpu_custom_call" | custom-call | flops 100663296 | tf_op jit(solution)/shard_map/pallas_call | solution.py:302
  (35 shorter events, 0.1 us)
Async XLA Ops:
  0.6 0.9 %copy-start.7 = (f32[512,64]{0,1:T(8,128)S(1)}, f32[512,64]{0,1:T(8,128)}, u32[]{:S(2)}) copy-start(f32[512,64]{0,1:T(8,128)} %param.12) | copy-start | bytes 393220
  1.5 0.7 copy-start.25
  2.3 1.2 %copy-start.27 = (f32[4,128,512]{2,1,0:T(8,128)S(1)}, f32[4,128,512]{2,1,0:T(8,128)}, u32[]{:S(2)}) copy-start(f32[4,128,512]{2,1,0:T(8,128)} %r_hbm.1) | copy-start | bytes 3145732
  3.5 1.2 %copy-start.28 = (f32[1,512,512]{2,1,0:T(8,128)S(1)}, f32[1,512,512]{2,1,0:T(8,128)}, u32[]{:S(2)}) copy-start(f32[1,512,512]{2,1,0:T(8,128)} %inv_hbm.1) | copy-start | bytes 3145732
  4.7 22.3 %copy-start.8 = (f32[512,64]{0,1:T(8,128)S(1)}, f32[512,64]{0,1:T(8,128)}, u32[]{:S(2)}) copy-start(f32[512,64]{0,1:T(8,128)} %param.12) | copy-start | bytes 393220
  4.7 22.3 %copy-start.24 = (f32[5,32,64]{2,1,0:T(8,128)S(1)}, f32[5,32,64]{2,1,0:T(8,128)}, u32[]{:S(2)}) copy-start(f32[5,32,64]{2,1,0:T(8,128)} %gamma_ref.3) | copy-start | bytes 122884
  4.7 22.3 %copy-start.26 = (f32[128,32]{0,1:T(8,128)S(1)}, f32[128,32]{0,1:T(8,128)}, u32[]{:S(2)}) copy-start(f32[128,32]{0,1:T(8,128)} %param.11) | copy-start | bytes 49156
  6.6 1.0 %copy-start.13 = (f32[4,128,512]{2,1,0:T(8,128)}, f32[4,128,512]{2,1,0:T(8,128)S(1)}, u32[]{:S(2)}) copy-start(f32[4,128,512]{2,1,0:T(8,128)S(1)} %get-tuple-element.18.local_ref) | copy-start | bytes 3145732
  7.5 0.8 copy-start.20
  8.3 0.8 copy-start.22
  9.1 2.4 %copy-start.30 = (f32[1,128,512]{2,1,0:T(8,128)}, f32[1,128,512]{2,1,0:T(8,128)S(1)}, u32[]{:S(2)}) copy-start(f32[1,128,512]{2,1,0:T(8,128)S(1)} %get-tuple-element.19) | copy-start | bytes 786436
  9.1 18.5 %copy-start = (f32[4,128,512]{2,1,0:T(8,128)S(1)}, f32[4,128,512]{2,1,0:T(8,128)}, u32[]{:S(2)}) copy-start(f32[4,128,512]{2,1,0:T(8,128)} %sigma_ref.3) | copy-start | bytes 3145732
  9.1 18.5 %copy-start.1 = (f32[4,128,512]{2,1,0:T(8,128)S(1)}, f32[4,128,512]{2,1,0:T(8,128)}, u32[]{:S(2)}) copy-start(f32[4,128,512]{2,1,0:T(8,128)} %wind_ref.3) | copy-start | bytes 3145732
  9.1 1.7 %collective-permute-start = (f32[136,512]{1,0:T(8,128)S(1)}, f32[136,512]{1,0:T(8,128)S(1)}, u32[]{:S(2)}, u32[]{:S(2)}) collective-permute-start(f32[136,512]{1,0:T(8,128)S(1)} %get-tuple-element.17.own_ref), channel_id=1, source_target_pairs={{0,1},{1,0},{2,3},{3,2},{4,5},{5,4},{6,7},{7,6},{8,9},{9,8},{10,11... | collective-permute-start | bytes 835592 | tf_op jit(solution)/shard_map/ppermute | solution.py:336
  10.8 0.8 copy-start.9
  11.6 15.5 %all-to-all-start = ((f32[256,1,128]{2,1,0:T(1,128)}), f32[256,1,128]{2,1,0:T(1,128)S(1)}, u32[]{:S(2)}, u32[]{:S(2)}) async-start(f32[256,1,128]{2,1,0:T(1,128)} %bitcast.3), calls=%async_computation | async-start | bytes 262144 | tf_op jit(solution)/shard_map/all_to_all | solution.py:314
  18.8 8.9 %collective-permute-start.1 = (f32[1,128,512]{2,1,0:T(8,128)}, f32[1,128,512]{2,1,0:T(8,128)}, u32[]{:S(2)}, u32[]{:S(2)}) collective-permute-start(f32[1,128,512]{2,1,0:T(8,128)} %copy-done.30), channel_id=1, source_target_pairs={{1,2},{3,4},{5,6},{7,8},{9,10},{11,12},{13,14},{15,16},{17,18},{19... | collective-permute-start | bytes 786440 | tf_op jit(solution)/shard_map/ppermute | solution.py:337
  27.7 1.0 %copy-start.10 = (f32[136,512]{1,0:T(8,128)S(1)}, f32[136,512]{1,0:T(8,128)}, u32[]{:S(2)}) copy-start(f32[136,512]{1,0:T(8,128)} %copy-done.9) | copy-start | bytes 835588
  28.6 1.2 %copy-start.14 = (f32[4,128,512]{2,1,0:T(8,128)S(1)}, f32[4,128,512]{2,1,0:T(8,128)}, u32[]{:S(2)}) copy-start(f32[4,128,512]{2,1,0:T(8,128)} %copy-done.13) | copy-start | bytes 3145732
  29.8 1.0 %copy-start.21 = (bf16[512,512]{1,0:T(8,128)(2,1)S(1)}, bf16[512,512]{1,0:T(8,128)(2,1)}, u32[]{:S(2)}) copy-start(bf16[512,512]{1,0:T(8,128)(2,1)} %copy-done.20) | copy-start | bytes 1572868
  30.9 1.0 %copy-start.23 = (bf16[512,512]{1,0:T(8,128)(2,1)S(1)}, bf16[512,512]{1,0:T(8,128)(2,1)}, u32[]{:S(2)}) copy-start(bf16[512,512]{1,0:T(8,128)(2,1)} %copy-done.22) | copy-start | bytes 1572868
  35.3 1.0 %copy-start.2 = (f32[4,128,512]{2,1,0:T(8,128)}, f32[4,128,512]{2,1,0:T(8,128)S(1)}, u32[]{:S(2)}) copy-start(f32[4,128,512]{2,1,0:T(8,128)S(1)} %get-tuple-element.26.z_ref) | copy-start | bytes 3145732
  36.3 1.0 %copy-start.4 = (f32[4,128,512]{2,1,0:T(8,128)}, f32[4,128,512]{2,1,0:T(8,128)S(1)}, u32[]{:S(2)}) copy-start(f32[4,128,512]{2,1,0:T(8,128)S(1)} %get-tuple-element.28.w_ref) | copy-start | bytes 3145732
  37.3 1.0 %copy-start.15 = (f32[4,128,512]{2,1,0:T(8,128)}, f32[4,128,512]{2,1,0:T(8,128)S(1)}, u32[]{:S(2)}) copy-start(f32[4,128,512]{2,1,0:T(8,128)S(1)} %get-tuple-element.24.local_ref) | copy-start | bytes 3145732
  38.3 0.8 copy-start.18
  39.0 3.3 %copy-start.29 = (f32[1,128,512]{2,1,0:T(8,128)}, f32[1,128,512]{2,1,0:T(8,128)S(1)}, u32[]{:S(2)}) copy-start(f32[1,128,512]{2,1,0:T(8,128)S(1)} %get-tuple-element.25) | copy-start | bytes 786436
  39.1 3.2 %collective-permute-start.2 = (f32[136,512]{1,0:T(8,128)S(1)}, f32[136,512]{1,0:T(8,128)S(1)}, u32[]{:S(2)}, u32[]{:S(2)}) collective-permute-start(f32[136,512]{1,0:T(8,128)S(1)} %get-tuple-element.23.own_ref), channel_id=1, source_target_pairs={{0,1},{1,0},{2,3},{3,2},{4,5},{5,4},{6,7},{7,6},{8,9},{9,8},{10,11... | collective-permute-start | bytes 835592 | tf_op jit(solution)/shard_map/ppermute | solution.py:336
  42.2 0.7 copy-start.11
  42.9 0.7 copy-start.17
  43.6 14.4 %all-to-all-start.1 = ((f32[288,1,128]{2,1,0:T(1,128)}), f32[288,1,128]{2,1,0:T(1,128)S(1)}, u32[]{:S(2)}, u32[]{:S(2)}) async-start(f32[288,1,128]{2,1,0:T(1,128)} %bitcast.21), calls=%async_computation.1 | async-start | bytes 294912 | tf_op jit(solution)/shard_map/all_to_all | solution.py:314
  49.5 9.1 %collective-permute-start.3 = (f32[1,128,512]{2,1,0:T(8,128)}, f32[1,128,512]{2,1,0:T(8,128)}, u32[]{:S(2)}, u32[]{:S(2)}) collective-permute-start(f32[1,128,512]{2,1,0:T(8,128)} %copy-done.29), channel_id=1, source_target_pairs={{1,2},{3,4},{5,6},{7,8},{9,10},{11,12},{13,14},{15,16},{17,18},{19... | collective-permute-start | bytes 786440 | tf_op jit(solution)/shard_map/ppermute | solution.py:337
  58.0 1.2 %copy-start.3 = (f32[4,128,512]{2,1,0:T(8,128)S(1)}, f32[4,128,512]{2,1,0:T(8,128)}, u32[]{:S(2)}) copy-start(f32[4,128,512]{2,1,0:T(8,128)} %copy-done.2) | copy-start | bytes 3145732
  59.2 1.2 %copy-start.5 = (f32[4,128,512]{2,1,0:T(8,128)S(1)}, f32[4,128,512]{2,1,0:T(8,128)}, u32[]{:S(2)}) copy-start(f32[4,128,512]{2,1,0:T(8,128)} %copy-done.4) | copy-start | bytes 3145732
  60.5 1.0 %copy-start.12 = (f32[136,512]{1,0:T(8,128)S(1)}, f32[136,512]{1,0:T(8,128)}, u32[]{:S(2)}) copy-start(f32[136,512]{1,0:T(8,128)} %copy-done.11) | copy-start | bytes 835588
  61.4 1.2 %copy-start.16 = (f32[4,128,512]{2,1,0:T(8,128)S(1)}, f32[4,128,512]{2,1,0:T(8,128)}, u32[]{:S(2)}) copy-start(f32[4,128,512]{2,1,0:T(8,128)} %copy-done.15) | copy-start | bytes 3145732
  62.6 1.0 %copy-start.19 = (f32[2,128,512]{2,1,0:T(8,128)S(1)}, f32[2,128,512]{2,1,0:T(8,128)}, u32[]{:S(2)}) copy-start(f32[2,128,512]{2,1,0:T(8,128)} %copy-done.18) | copy-start | bytes 1572868
  63.7 16.4 %copy-start.6 = (f32[4,128,512]{2,1,0:T(8,128)S(1)}, f32[4,128,512]{2,1,0:T(8,128)}, u32[]{:S(2)}) copy-start(f32[4,128,512]{2,1,0:T(8,128)} %copy-done.4) | copy-start | bytes 3145732

commit v4 on v3

--- a/solution.py
+++ b/solution.py
@@ -14,6 +14,8 @@
 NN = (((1,), (0,)), ((), ()))
 NT = (((1,), (1,)), ((), ()))
 TN = (((0,), (0,)), ((), ()))
+CHUNK = 16
+FIRST_LIMIT = 51
 
 
 def halves(x):
@@ -110,27 +112,56 @@
         out_ref[i] = lax.dot_general(left, right, TN, preferred_element_type=F32)
 
 
-def stencil(prev, here, after, sigma, wind):
-    rows, depth = here.shape
-    row = lax.broadcasted_iota(jnp.int32, here.shape, 0)
-    col = lax.broadcasted_iota(jnp.int32, here.shape, 1)
-    beside = (
-        after
-        + prev
-        + jnp.where(row == rows - 1, 0.0, pltpu.roll(here, rows - 1, 0))
-        + jnp.where(row == 0, 0.0, pltpu.roll(here, 1, 0))
-        + jnp.where(col == depth - 1, 0.0, pltpu.roll(here, depth - 1, 1))
-        + jnp.where(col == 0, 0.0, pltpu.roll(here, 1, 1))
-    )
-    return (6.0 + sigma) * here - beside + wind * (after - prev)
-
-
-def lane_sum(x):
-    total = jnp.sum(x, axis=0, keepdims=True)
-    out = total[:, :LANES]
-    for i in range(1, x.shape[1] // LANES):
-        out = out + total[:, i * LANES : (i + 1) * LANES]
-    return out
+PAD = 8
+
+
+def tiles_of(ref):
+    return ref.shape[-1] // LANES
+
+
+def columns(j):
+    return slice(j * LANES, (j + 1) * LANES)
+
+
+def fill_tiles(tiled_ref, index, tile, j):
+    ny = tile.shape[0]
+    tiled_ref[index, j, PAD : PAD + ny] = tile
+
+
+def clear_pads(tiled_ref):
+    layers, tiles, full, _ = tiled_ref.shape
+    zero = jnp.zeros((PAD, LANES), F32)
+    for x in range(1, layers - 1):
+        for j in range(tiles):
+            tiled_ref[x, j, :PAD] = zero
+            tiled_ref[x, j, full - PAD :] = zero
+
+
+def stencil(tiled_ref, sigma_ref, wind_ref, x, first, rows, emit):
+    tiles = tiled_ref.shape[1]
+    lane = lax.broadcasted_iota(jnp.int32, (rows, LANES), 1)
+    top = PAD + first
+    here = [tiled_ref[x + 1, j, top : top + rows] for j in range(tiles)]
+    up = [pltpu.roll(h, LANES - 1, 1) for h in here] + [jnp.zeros_like(here[0])]
+    down = [jnp.zeros_like(here[0])] + [pltpu.roll(h, 1, 1) for h in here]
+    for j in range(tiles):
+        prev = tiled_ref[x, j, top : top + rows]
+        after = tiled_ref[x + 2, j, top : top + rows]
+        beside = (
+            (after + prev)
+            + (tiled_ref[x + 1, j, top - 1 : top - 1 + rows] + tiled_ref[x + 1, j, top + 1 : top + 1 + rows])
+            + (
+                jnp.where(lane == LANES - 1, up[j + 1], up[j])
+                + jnp.where(lane == 0, down[j], down[j + 1])
+            )
+        )
+        at = (x, slice(first, first + rows), columns(j))
+        value = (6.0 + sigma_ref[at]) * here[j] - beside + wind_ref[at] * (after - prev)
+        emit(at, value)
+
+
+def rows_sum(x):
+    return jnp.sum(x.reshape(x.shape[0] // 8, 8, LANES), axis=0)
 
 
 def full_sum(x):
@@ -160,63 +191,76 @@
 
 
 def first_kernel(
-    r_hbm, inv_hbm, by_ref, bz_ref,
-    pair_ref, r_ref, high_ref, low_ref, local_ref, odd_ref,
-    inv_ref, sems, *, fold,
+    r_hbm, inv_hbm, local_ref, summed_ref, odd_ref, high_ref, low_ref, rr_ref, r_ref, inv_ref, sems
 ):
-    layers = r_ref.shape[0]
-    loads = [pltpu.make_async_copy(r_hbm.at[x], r_ref.at[x], sems.at[x]) for x in range(layers)]
-    loads.append(pltpu.make_async_copy(inv_hbm.at[0], inv_ref, sems.at[layers]))
+    layers, _, _ = r_ref.shape
+    moves = [(r_hbm.at[x], r_ref.at[x]) for x in range(layers)] + [(inv_hbm.at[0], inv_ref)]
+    loads = [pltpu.make_async_copy(*move, sems.at[i]) for i, move in enumerate(moves)]
     for load in loads:
         load.start()
-    loads[0].wait()
-    summed = r_ref[0]
-    for x in range(1, layers):
-        loads[x].wait()
-        summed = summed + r_ref[x]
-    packed = project(summed, by_ref[...], bz_ref[...], fold)
-    send_proj(packed, [], pair_ref, r_ref.shape[1])
+    for load in loads[:layers]:
+        load.wait()
+    total = jnp.zeros((8, LANES), F32)
+    for j in range(tiles_of(r_ref)):
+        summed = None
+        for x in range(layers):
+            r = r_ref[x, :, columns(j)]
+            total = total + rows_sum(r * r)
+            summed = r if x == 0 else summed + r
+        summed_ref[:, columns(j)] = summed
+    rr_ref[:8] = total
     loads[layers].wait()
     inverse = halves(inv_ref[...])
     high_ref[...], low_ref[...] = inverse
     for x in range(layers):
         local_ref[x] = dot3(halves(r_ref[x]), inverse)
-    send_edges(local_ref, pair_ref, odd_ref)
+    odd_ref[0] = local_ref[jnp.where(even_here(), 0, layers - 1)]
+
+
+def project_kernel(summed_ref, local_ref, by_ref, bz_ref, pair_ref, *, fold):
+    layers, ny, _ = local_ref.shape
+    pair_ref[:ny] = local_ref[jnp.where(even_here(), layers - 1, 0)]
+    send_proj(project(summed_ref[...], by_ref[...], bz_ref[...], fold), [], pair_ref, ny)
+
+
+def halo_of(even_ref, odd_ref, j):
+    ny = odd_ref.shape[1]
+    even = even_here()
+    pair = even_ref[:ny, columns(j)]
+    odd = odd_ref[0, :, columns(j)]
+    return jnp.where(even, odd, pair), jnp.where(even, pair, odd)
 
 
 def middle_kernel(
     spread_ref, local_ref, even_ref, odd_ref, r_ref, sigma_ref, wind_ref, by_ref, bz_ref,
-    high_ref, low_ref,
-    z_ref, edge_ref, w_ref, pair2_ref, local2_ref, odd2_ref, *, fold,
+    high_ref, low_ref, rr_ref,
+    z_ref, w_ref, pair2_ref, local2_ref, odd2_ref, *, fold,
 ):
-    layers = r_ref.shape[0]
-    before, own, after = (spread_ref[i] for i in range(3))
-    even = even_here().astype(F32)
-    from_pair = even_ref[: r_ref.shape[1]]
-    from_other = odd_ref[0]
-    edge_ref[0] = before + (from_other * even + from_pair * (1.0 - even))
-    edge_ref[1] = after + (from_pair * even + from_other * (1.0 - even))
+    layers, ny, _ = r_ref.shape
+    clear_pads(z_ref)
+    for j in range(tiles_of(r_ref)):
+        before, after = halo_of(even_ref, odd_ref, j)
+        fill_tiles(z_ref, 0, spread_ref[0, :, columns(j)] + before, j)
+        fill_tiles(z_ref, layers + 1, spread_ref[2, :, columns(j)] + after, j)
+        own = spread_ref[1, :, columns(j)]
+        for x in range(layers):
+            fill_tiles(z_ref, x + 1, local_ref[x, :, columns(j)] + own, j)
+    sums = [rr_ref[:8]] + [jnp.zeros((8, LANES), F32)] * 2
+
+    def emit(at, w):
+        w_ref[at] = w
+        sums[1] = sums[1] + rows_sum(r_ref[at] * w)
+        sums[2] = sums[2] + rows_sum(w * w)
+
     for x in range(layers):
-        z_ref[x] = local_ref[x] + own
-    rr = rw = ww = summed = None
-    for x in range(layers):
-        prev = edge_ref[0] if x == 0 else z_ref[x - 1]
-        nxt = edge_ref[1] if x == layers - 1 else z_ref[x + 1]
-        w = stencil(prev, z_ref[x], nxt, sigma_ref[x], wind_ref[x])
-        w_ref[x] = w
-        r = r_ref[x]
-        parts = (lane_sum(r * r), lane_sum(r * w), lane_sum(w * w))
-        if x == 0:
-            rr, rw, ww = parts
-            summed = w
-        else:
-            rr, rw, ww = rr + parts[0], rw + parts[1], ww + parts[2]
-            summed = summed + w
+        for first in range(0, ny, CHUNK):
+            stencil(z_ref, sigma_ref, wind_ref, x, first, CHUNK, emit)
+        local2_ref[x] = dot3(halves(w_ref[x]), (high_ref[...], low_ref[...]))
+    summed = w_ref[0]
+    for x in range(1, layers):
+        summed = summed + w_ref[x]
     packed = project(summed, by_ref[...], bz_ref[...], fold)
-    send_proj(packed, [rr, rw, ww], pair2_ref, r_ref.shape[1])
-    inverse = (high_ref[...], low_ref[...])
-    for x in range(layers):
-        local2_ref[x] = dot3(halves(w_ref[x]), inverse)
+    send_proj(packed, [jnp.sum(s, axis=0, keepdims=True) for s in sums], pair2_ref, ny)
     send_edges(local2_ref, pair2_ref, odd2_ref)
 
 
@@ -239,45 +283,51 @@
 
 
 def last_kernel(
-    gath_ref, spread_ref, local_ref, even_ref, odd_ref, r_ref, z_ref, edge_ref, w_ref,
-    sigma_ref, wind_ref, z2_ref, u_ref, out_ref, edge2_ref, *, rows,
+    gath_ref, spread_ref, local_ref, even_ref, odd_ref, r_ref, z_ref, w_ref,
+    sigma_ref, wind_ref, z2_ref, u_ref, out_ref, known_ref, *, rows,
 ):
-    layers = r_ref.shape[0]
+    layers, ny, _ = r_ref.shape
     beta, h11, h21 = first_scalars(gath_ref, rows)
     scale = 1.0 / (h21 * beta)
-    before, own, after = (spread_ref[i] for i in range(3))
-    even = even_here().astype(F32)
-    from_pair = even_ref[: r_ref.shape[1]]
-    from_other = odd_ref[0]
-    edge2_ref[0] = scale * (
-        before + (from_other * even + from_pair * (1.0 - even)) - h11 * edge_ref[0]
-    )
-    edge2_ref[1] = scale * (
-        after + (from_pair * even + from_other * (1.0 - even)) - h11 * edge_ref[1]
-    )
+    minus = scale * h11
+    clear_pads(z2_ref)
+
+    def combine(index, image, j):
+        old = z_ref[index, j, PAD : PAD + ny]
+        fill_tiles(z2_ref, index, scale * image - minus * old, j)
+
+    for j in range(tiles_of(r_ref)):
+        before, after = halo_of(even_ref, odd_ref, j)
+        combine(0, spread_ref[0, :, columns(j)] + before, j)
+        combine(layers + 1, spread_ref[2, :, columns(j)] + after, j)
+        own = spread_ref[1, :, columns(j)]
+        for x in range(layers):
+            combine(x + 1, local_ref[x, :, columns(j)] + own, j)
+    sums = [jnp.zeros((8, LANES), F32)] * 3
+
+    def emit(at, u):
+        u_ref[at] = u
+        for i, product in enumerate((r_ref[at] * u, w_ref[at] * u, u * u)):
+            sums[i] = sums[i] + rows_sum(product)
+
     for x in range(layers):
-        z2_ref[x] = scale * (local_ref[x] + own - h11 * z_ref[x])
-    a = b = c = None
-    for x in range(layers):
-        prev = edge2_ref[0] if x == 0 else z2_ref[x - 1]
-        nxt = edge2_ref[1] if x == layers - 1 else z2_ref[x + 1]
-        u = stencil(prev, z2_ref[x], nxt, sigma_ref[x], wind_ref[x])
-        u_ref[x] = u
-        r = r_ref[x]
-        v2 = scale * (w_ref[x] - h11 * r)
-        parts = (lane_sum(r * u), lane_sum(v2 * u), lane_sum(u * u))
-        a, b, c = parts if x == 0 else (a + parts[0], b + parts[1], c + parts[2])
+        for first in range(0, ny, CHUNK):
+            stencil(z2_ref, sigma_ref, wind_ref, x, first, CHUNK, emit)
     lane = lax.broadcasted_iota(jnp.int32, (1, LANES), 1)
-    row = jnp.where(
-        lane == 0, full_sum(a), jnp.where(lane == 1, full_sum(b), jnp.where(lane == 2, full_sum(c), 0.0))
-    )
+    a, b, c = (full_sum(s) for s in sums)
+    b = scale * b - minus * a
+    row = jnp.where(lane == 0, a, jnp.where(lane == 1, b, jnp.where(lane == 2, c, 0.0)))
     out_ref[...] = jnp.broadcast_to(row, out_ref.shape)
+    for i, value in enumerate((beta, h11, h21)):
+        known_ref[8 * i : 8 * i + 8] = jnp.broadcast_to(value, (8, LANES))
 
 
 def finish_kernel(
-    sums_ref, gath_ref, r_ref, z_ref, w_ref, z2_ref, u_ref, sol_ref, res_ref, *, rows
+    sums_ref, known_ref, r_ref, z_ref, w_ref, z2_ref, u_ref, sol_hbm, res_hbm,
+    sol_ref, res_ref, sems,
 ):
-    beta, h11, h21 = first_scalars(gath_ref, rows)
+    layers, ny, _ = r_ref.shape
+    beta, h11, h21 = (known_ref[8 * i : 8 * i + 1, :1] for i in range(3))
     sums = jnp.sum(sums_ref[...], axis=0, keepdims=True)
     h12 = lane_of(sums, 0) / beta
     h22 = lane_of(sums, 1)
@@ -290,12 +340,21 @@
     determ = m11 * m22 - m12 * m12
     y_one = (m22 * q_one - m12 * q_two) / determ / beta
     y_two = (m11 * q_two - m12 * q_one) / determ
-    for x in range(r_ref.shape[0]):
-        sol_ref[x] = y_one * z_ref[x] + y_two * z2_ref[x]
+    stores = []
+    for x in range(layers):
+        for j in range(tiles_of(r_ref)):
+            inside = (x + 1, j, slice(PAD, PAD + ny))
+            sol_ref[x, :, columns(j)] = y_one * z_ref[inside] + y_two * z2_ref[inside]
         res_ref[x] = r_ref[x] - (y_one * w_ref[x] + y_two * u_ref[x])
-
-
-def call(kernel, outs, args, scratch=(), flops=0, hbm=()):
+        for i, (src, dst) in enumerate(((sol_ref, sol_hbm), (res_ref, res_hbm))):
+            store = pltpu.make_async_copy(src.at[x], dst.at[x], sems.at[2 * x + i])
+            store.start()
+            stores.append(store)
+    for store in stores:
+        store.wait()
+
+
+def call(kernel, outs, args, scratch=(), flops=0, hbm=(), far_out=False, limit=24):
     vmem = pl.BlockSpec(memory_space=pltpu.VMEM)
     far = pl.BlockSpec(memory_space=pltpu.HBM)
     outs = [s if isinstance(s, jax.ShapeDtypeStruct) else jax.ShapeDtypeStruct(s, F32) for s in outs]
@@ -303,9 +362,9 @@
         kernel,
         out_shape=outs,
         in_specs=[far if i in hbm else vmem for i in range(len(args))],
-        out_specs=[vmem] * len(outs),
+        out_specs=[far if far_out else vmem] * len(outs),
         scratch_shapes=[pltpu.VMEM(s, F32) if isinstance(s, tuple) else s for s in scratch],
-        compiler_params=pltpu.CompilerParams(vmem_limit_bytes=24 << 20),
+        compiler_params=pltpu.CompilerParams(vmem_limit_bytes=limit << 20),
         cost_estimate=pl.CostEstimate(flops=flops, bytes_accessed=0, transcendentals=0),
     )(*args)
 
@@ -323,7 +382,6 @@
     rows, width = ky // fold, kz * fold
     field = (layers, ny, nz)
     edge = (1, ny, nz)
-    square = jax.ShapeDtypeStruct((nz, nz), BF16)
     pairs = [(i, i ^ 1) for i in range(count)]
     others = [(i, i + 1) for i in range(1, count - 1, 2)]
     others = others + [(j, i) for i, j in others]
@@ -331,6 +389,7 @@
     by, bz = basis_y.T, basis_z.T
     each = rows // 2
     pair = (ny + each, nz)
+    tiled = (layers + 2, nz // LANES, ny + 2 * PAD, LANES)
 
     def round_of(sent, odd, extra):
         got = lax.ppermute(sent, AXIS, pairs)
@@ -350,30 +409,35 @@
         )
         return block, spread, got, odd
 
-    sent, r, high, low, local, odd = call(
-        functools.partial(first_kernel, fold=fold),
-        [pair, field, square, square, field, edge],
-        (right_side, local_inverse, by, bz),
-        [(nz, nz), pltpu.SemaphoreType.DMA((layers + 1,))], flops=matmul, hbm=(0, 1),
+    square = jax.ShapeDtypeStruct((nz, nz), BF16)
+    local, summed, odd, high, low, rr = call(
+        first_kernel, [field, (ny, nz), edge, square, square, (32, LANES)],
+        (right_side, local_inverse),
+        [field, (nz, nz), pltpu.SemaphoreType.DMA((layers + 1,))],
+        flops=matmul, hbm=(0, 1), limit=FIRST_LIMIT,
+    )
+    (sent,) = call(
+        functools.partial(project_kernel, fold=fold), [pair],
+        (summed, local, by, bz), flops=matmul // 8,
     )
     _, spread, got, odd = round_of(sent, odd, 0)
-    z, edges, w, sent, local, odd = call(
+    z, w, sent, local, odd = call(
         functools.partial(middle_kernel, fold=fold),
-        [field, (2, ny, nz), field, pair, field, edge],
-        (spread, local, got, odd, r, sigma, wind, by, bz, high, low),
+        [tiled, field, pair, field, edge],
+        (spread, local, got, odd, right_side, sigma, wind, by, bz, high, low, rr),
         flops=2 * matmul,
     )
     gathered, spread, got, odd = round_of(sent, odd, 1)
-    z2, u, sent = call(
+    z2, u, sent, known = call(
         functools.partial(last_kernel, rows=rows),
-        [field, field, (count, LANES)],
-        (gathered, spread, local, got, odd, r, z, edges, w, sigma, wind),
-        [(2, ny, nz)], flops=matmul,
+        [tiled, field, (count, LANES), (32, LANES)],
+        (gathered, spread, local, got, odd, right_side, z, w, sigma, wind), flops=matmul,
     )
     sums = exchange(sent)
     return call(
-        functools.partial(finish_kernel, rows=rows), [field, field],
-        (sums, gathered, r, z, w, z2, u), flops=matmul // 8,
+        finish_kernel, [field, field], (sums, known, right_side, z, w, z2, u),
+        [field, field, pltpu.SemaphoreType.DMA((2 * layers,))],
+        flops=matmul // 8, far_out=True,
     )
 
 

time: 82.8 us -> 75.4 us (0.911)
  local copies, waits for them, and re-layouts: 21 us -> 14.2 us
    unnamed x62 -> x46, local copies, waits for them, and re-layouts: 21 us -> 14.2 us
    pallas_call x8 -> x9, Pallas kernels: 11.9 us -> 11.5 us  [call(): pl.pallas_call(kernel, out_shape=outs, in_specs=[far if i in hbm else vme...]
  transfers between devices with their start and end apart: 6 -> 6, of which waited for: 4 -> 4; matrix products, arithmetic and copies ran while one was open for 0% -> 0% of each run, Pallas kernels for 1% -> 2%
where the time goes in v4:
time: 75.4 us; the launch traced here: 74.7 us
  starting transfers between devices  17.5 us (23%)
  waiting for transfers between devices  17.1 us (23%)
  local copies, waits for them, and re-layouts  14.2 us (19%)
  blocking collectives  13.6 us (18%)
  Pallas kernels  11.5 us (15%)
  between operations  0.77 us (1%)
    all_to_all x2, waiting for transfers between devices, exchange(): return lax.all_to_all(block, AXIS, 0, 0, tiled=True)  14.7 us
    unnamed x46, local copies, waits for them, and re-layouts  14.2 us
    all_to_all x1, blocking collectives, exchange(): return lax.all_to_all(block, AXIS, 0, 0, tiled=True)  13.6 us
    all_to_all x2, starting transfers between devices, exchange(): return lax.all_to_all(block, AXIS, 0, 0, tiled=True)  13.1 us
    pallas_call x9, Pallas kernels, call(): pl.pallas_call(kernel, out_shape=outs, in_specs=[far if i in hbm else vme...  11.5 us
    ppermute x2, starting transfers between devices, round_of(): got = lax.ppermute(sent, AXIS, pairs)  2.41 us
    ppermute x2, waiting for transfers between devices, round_of(): got = lax.ppermute(sent, AXIS, pairs)  2.37 us
    ppermute x2, starting transfers between devices, round_of(): odd = lax.ppermute(odd, AXIS, others)  2.05 us
  transfers between devices with their start and end apart: 6, of which 4 were waited for; matrix products, arithmetic and copies ran while one was open for 0% of the time, Pallas kernels for 2%

profile of v4, /device:TPU:0, one launch (start us, length us, event | category | flops | bytes accessed | tf_op | source)
XLA Modules:
  0.0 74.7 jit_solution(9720626310707676983)
XLA Ops:
  0.6 0.0 copy-start.10
  0.6 0.0 copy-start.18
  0.7 2.7 %shard_map.86 = (f32[4,128,512]{2,1,0:T(8,128)S(1)}, f32[128,512]{1,0:T(8,128)S(1)}, f32[1,128,512]{2,1,0:T(8,128)S(1)}, bf16[512,512]{1,0:T(8,128)(2,1)S(1)}, b...) custom-call(f32[4,128,512]{2,1,0:T(8,128)} %r_ref.5, f32[1,512,512]{2,1,0:T(8,128)} %inv_hbm.1), custom_call_target="tpu_custom_call" | custom-call | flops 805306368 | tf_op jit(solution)/shard_map/pallas_call | solution.py:361
  3.4 0.0 copy-start.22
  3.4 0.7 copy-done.22
  4.1 0.0 copy-done.10
  4.1 0.0 copy-done.18
  4.1 0.0 copy-start
  4.1 0.5 shard_map.87.own_ref
  4.6 1.0 %copy-done.1 = f32[4,128,512]{2,1,0:T(8,128)} copy-done((f32[4,128,512]{2,1,0:T(8,128)}, f32[4,128,512]{2,1,0:T(8,128)S(1)}, u32[]{:S(2)}) %copy-start.1) | copy-done | bytes 1048600
  5.6 0.5 collective-permute-start
  6.1 1.2 %collective-permute-done.got_ref.even_ref = f32[136,512]{1,0:T(8,128)S(1)} collective-permute-done((f32[136,512]{1,0:T(8,128)S(1)}, f32[136,512]{1,0:T(8,128)S(1)}, u32[]{:S(2)}, u32[]{:S(2)}) %collective-permute-start) | collective-permute-done | bytes 278560 | tf_op jit(solution)/shard_map/ppermute | solution.py:395
  7.3 0.7 shard_map.88
  8.0 0.0 copy-done.13
  8.0 0.0 copy-done.15
  8.0 7.2 %all-to-all-start = ((f32[256,1,128]{2,1,0:T(1,128)}), f32[256,1,128]{2,1,0:T(1,128)S(1)}, u32[]{:S(2)}, u32[]{:S(2)}) async-start(f32[256,1,128]{2,1,0:T(1,128)} %bitcast.3), calls=%async_computation | async-start | bytes 262144 | tf_op jit(solution)/shard_map/all_to_all | solution.py:373
  15.2 0.7 collective-permute-start.1
  15.8 7.6 %all-to-all-done = f32[256,1,128]{2,1,0:T(1,128)S(1)} async-done(((f32[256,1,128]{2,1,0:T(1,128)}), f32[256,1,128]{2,1,0:T(1,128)S(1)}, u32[]{:S(2)}, u32[]{:S(2)}) %all-to-all-start) | async-done | bytes 131104 | tf_op jit(solution)/shard_map/all_to_all | solution.py:373
  23.4 0.0 copy-done.17
  23.4 0.6 shard_map.89.spread_ref
  24.0 0.0 collective-permute-done.1.odd_ref
  24.0 0.0 copy-start.19
  24.0 0.7 copy-done.19
  24.7 0.0 copy-done
  24.7 0.0 copy-done.2
  24.7 1.2 %copy-done.3 = f32[4,128,512]{2,1,0:T(8,128)S(1)} copy-done((f32[4,128,512]{2,1,0:T(8,128)S(1)}, f32[4,128,512]{2,1,0:T(8,128)}, u32[]{:S(2)}) %copy-start.3) | copy-done | bytes 1048600
  26.0 1.2 %copy-done.5 = f32[4,128,512]{2,1,0:T(8,128)S(1)} copy-done((f32[4,128,512]{2,1,0:T(8,128)S(1)}, f32[4,128,512]{2,1,0:T(8,128)}, u32[]{:S(2)}) %copy-start.5) | copy-done | bytes 1048600
  27.2 1.0 %copy-done.14 = bf16[512,512]{1,0:T(8,128)(2,1)S(1)} copy-done((bf16[512,512]{1,0:T(8,128)(2,1)S(1)}, bf16[512,512]{1,0:T(8,128)(2,1)}, u32[]{:S(2)}) %copy-start.14) | copy-done | bytes 524312
  28.2 1.0 %copy-done.16 = bf16[512,512]{1,0:T(8,128)(2,1)S(1)} copy-done((bf16[512,512]{1,0:T(8,128)(2,1)S(1)}, bf16[512,512]{1,0:T(8,128)(2,1)}, u32[]{:S(2)}) %copy-start.16) | copy-done | bytes 524312
  29.3 0.9 %copy-done.20 = f32[1,128,512]{2,1,0:T(8,128)S(1)} copy-done((f32[1,128,512]{2,1,0:T(8,128)S(1)}, f32[1,128,512]{2,1,0:T(8,128)}, u32[]{:S(2)}) %copy-start.20) | copy-done | bytes 262168
  30.2 1.9 %shard_map.90 = (f32[6,4,144,128]{3,2,1,0:T(8,128)S(1)}, f32[4,128,512]{2,1,0:T(8,128)S(1)}, f32[136,512]{1,0:T(8,128)S(1)}, f32[4,128,512]{2,1,0:T(8,128)S(1)}, f32[1,128,512]{2,1,0:T(8,128)S(1)}) custom-call(f32[3,128,512]{2,1,0:T(8,128)S(1)} %shard_map.89.spread_ref, f32[4,128,512]{2,1,0:T(8,128)S(1)} %copy-done.2, ...), custom_call_target="tpu_custom_call" | custom-call | flops 1610612736 | tf_op jit(solution)/shard_map/pallas_call | solution.py:361
  32.1 1.0 %copy-done.7 = f32[4,128,512]{2,1,0:T(8,128)} copy-done((f32[4,128,512]{2,1,0:T(8,128)}, f32[4,128,512]{2,1,0:T(8,128)S(1)}, u32[]{:S(2)}) %copy-start.7) | copy-done | bytes 1048600
  33.1 1.0 %copy-done.11 = f32[4,128,512]{2,1,0:T(8,128)} copy-done((f32[4,128,512]{2,1,0:T(8,128)}, f32[4,128,512]{2,1,0:T(8,128)S(1)}, u32[]{:S(2)}) %copy-start.11) | copy-done | bytes 1048600
  34.1 1.9 %collective-permute-start.2 = (f32[136,512]{1,0:T(8,128)S(1)}, f32[136,512]{1,0:T(8,128)S(1)}, u32[]{:S(2)}, u32[]{:S(2)}) collective-permute-start(f32[136,512]{1,0:T(8,128)S(1)} %get-tuple-element.23.own_ref), channel_id=1, source_target_pairs={{0,1},{1,0},{2,3},{3,2},{4,5},{5,4},{6,7},{7,6},{8,9},{9,8},{10,11... | collective-permute-start | bytes 835592 | tf_op jit(solution)/shard_map/ppermute | solution.py:395
  36.0 1.2 %collective-permute-done.2.got_ref.even_ref = f32[136,512]{1,0:T(8,128)S(1)} collective-permute-done((f32[136,512]{1,0:T(8,128)S(1)}, f32[136,512]{1,0:T(8,128)S(1)}, u32[]{:S(2)}, u32[]{:S(2)}) %collective-permute-start.2) | collective-permute-done | bytes 278560 | tf_op jit(solution)/shard_map/ppermute | solution.py:395
  37.2 0.8 %shard_map.91 = f32[288,128]{1,0:T(8,128)} custom-call(f32[136,512]{1,0:T(8,128)S(1)} %collective-permute-done.2.got_ref.even_ref, f32[136,512]{1,0:T(8,128)S(1)} %get-tuple-element.23.own_ref), custom_call_target="tpu_custom_call" | custom-call | flops 50331648 | tf_op jit(solution)/shard_map/pallas_call | solution.py:361
  37.9 5.9 %all-to-all-start.1 = ((f32[288,1,128]{2,1,0:T(1,128)}), f32[288,1,128]{2,1,0:T(1,128)S(1)}, u32[]{:S(2)}, u32[]{:S(2)}) async-start(f32[288,1,128]{2,1,0:T(1,128)} %bitcast.6), calls=%async_computation.1 | async-start | bytes 294912 | tf_op jit(solution)/shard_map/all_to_all | solution.py:373
  43.8 1.4 %collective-permute-start.3 = (f32[1,128,512]{2,1,0:T(8,128)}, f32[1,128,512]{2,1,0:T(8,128)}, u32[]{:S(2)}, u32[]{:S(2)}) collective-permute-start(f32[1,128,512]{2,1,0:T(8,128)} %copy-done.21), channel_id=1, source_target_pairs={{1,2},{3,4},{5,6},{7,8},{9,10},{11,12},{13,14},{15,16},{17,18},{19... | collective-permute-start | bytes 786440 | tf_op jit(solution)/shard_map/ppermute | solution.py:396
  45.2 7.1 %all-to-all-done.1 = f32[288,1,128]{2,1,0:T(1,128)S(1)} async-done(((f32[288,1,128]{2,1,0:T(1,128)}), f32[288,1,128]{2,1,0:T(1,128)S(1)}, u32[]{:S(2)}, u32[]{:S(2)}) %all-to-all-start.1) | async-done | bytes 147488 | tf_op jit(solution)/shard_map/all_to_all | solution.py:373
  52.3 0.6 shard_map.92.spread_ref
  52.9 0.0 collective-permute-done.3.odd_ref
  52.9 0.6 copy-done.4
  53.6 1.2 %copy-done.6 = f32[4,128,512]{2,1,0:T(8,128)S(1)} copy-done((f32[4,128,512]{2,1,0:T(8,128)S(1)}, f32[4,128,512]{2,1,0:T(8,128)}, u32[]{:S(2)}) %copy-start.6) | copy-done | bytes 1048600
  54.8 1.2 %copy-done.8 = f32[4,128,512]{2,1,0:T(8,128)S(1)} copy-done((f32[4,128,512]{2,1,0:T(8,128)S(1)}, f32[4,128,512]{2,1,0:T(8,128)}, u32[]{:S(2)}) %copy-start.8) | copy-done | bytes 1048600
  56.0 1.2 %copy-done.12 = f32[4,128,512]{2,1,0:T(8,128)S(1)} copy-done((f32[4,128,512]{2,1,0:T(8,128)S(1)}, f32[4,128,512]{2,1,0:T(8,128)}, u32[]{:S(2)}) %copy-start.12) | copy-done | bytes 1048600
  57.2 2.2 %shard_map.93 = (f32[6,4,144,128]{3,2,1,0:T(8,128)S(1)}, f32[4,128,512]{2,1,0:T(8,128)S(1)}, f32[32,128]{1,0:T(8,128)S(1)}, f32[32,128]{1,0:T(8,128)S(1)}) custom-call(f32[288,128]{1,0:T(8,128)S(1)} %bitcast.19, f32[3,128,512]{2,1,0:T(8,128)S(1)} %shard_map.92.spread_ref, f32[4,128,512]{2,1,0:T(8,128)S(1)} %copy-done.12, ...), custom_call_target="tpu_custom_call" | custom-call | flops 805306368 | tf_op jit(solution)/shard_map/pallas_call | solution.py:361
  59.5 13.6 %all_to_all.21 = f32[32,1,128]{2,1,0:T(1,128)S(1)} all-to-all(f32[32,1,128]{2,1,0:T(1,128)S(1)} %bitcast.26), channel_id=1, replica_groups=mesh['sub'=32] {'sub'}, dimensions={0} | all-to-all | bytes 32768 | tf_op jit(solution)/shard_map/all_to_all | solution.py:373
  73.1 1.6 %shard_map.94 = (f32[4,128,512]{2,1,0:T(8,128)}, f32[4,128,512]{2,1,0:T(8,128)}) custom-call(f32[32,128]{1,0:T(8,128)S(1)} %bitcast.25, f32[32,128]{1,0:T(8,128)S(1)} %get-tuple-element.29.known_ref, f32[4,128,512]{2,1,0:T(8,128)S(1)} %copy-done, f32[6,4,144,128]{3,2,1,0:T(8,128)S(1)} %get-tuple-element.26.z_ref, f32[4,128,512]{2,1,0:T(8,128)S(1)} %copy-done.9, ...), custom_call_target="tpu_custom_call" | custom-call | flops 100663296 | tf_op jit(solution)/shard_map/pallas_call | solution.py:361
  (20 shorter events, 0.0 us)
Async XLA Ops:
  0.6 3.5 %copy-start.10 = (f32[512,64]{0,1:T(8,128)S(1)}, f32[512,64]{0,1:T(8,128)}, u32[]{:S(2)}) copy-start(f32[512,64]{0,1:T(8,128)} %param.12) | copy-start | bytes 393220
  0.6 3.5 %copy-start.18 = (f32[128,32]{0,1:T(8,128)S(1)}, f32[128,32]{0,1:T(8,128)}, u32[]{:S(2)}) copy-start(f32[128,32]{0,1:T(8,128)} %param.11) | copy-start | bytes 49156
  3.4 0.7 copy-start.22
  4.1 3.9 %copy-start.13 = (bf16[512,512]{1,0:T(8,128)(2,1)}, bf16[512,512]{1,0:T(8,128)(2,1)S(1)}, u32[]{:S(2)}) copy-start(bf16[512,512]{1,0:T(8,128)(2,1)S(1)} %get-tuple-element.20.high_ref) | copy-start | bytes 1572868
  4.1 3.9 %copy-start.15 = (bf16[512,512]{1,0:T(8,128)(2,1)}, bf16[512,512]{1,0:T(8,128)(2,1)S(1)}, u32[]{:S(2)}) copy-start(bf16[512,512]{1,0:T(8,128)(2,1)S(1)} %get-tuple-element.21.low_ref) | copy-start | bytes 1572868
  4.1 19.3 %copy-start.17 = (f32[5,32,64]{2,1,0:T(8,128)S(1)}, f32[5,32,64]{2,1,0:T(8,128)}, u32[]{:S(2)}) copy-start(f32[5,32,64]{2,1,0:T(8,128)} %gamma_ref.3) | copy-start | bytes 122884
  4.1 20.6 %copy-start = (f32[4,128,512]{2,1,0:T(8,128)S(1)}, f32[4,128,512]{2,1,0:T(8,128)}, u32[]{:S(2)}) copy-start(f32[4,128,512]{2,1,0:T(8,128)} %r_ref.5) | copy-start | bytes 3145732
  4.6 1.0 %copy-start.1 = (f32[4,128,512]{2,1,0:T(8,128)}, f32[4,128,512]{2,1,0:T(8,128)S(1)}, u32[]{:S(2)}) copy-start(f32[4,128,512]{2,1,0:T(8,128)S(1)} %get-tuple-element.18.local_ref) | copy-start | bytes 3145732
  5.6 1.7 %collective-permute-start = (f32[136,512]{1,0:T(8,128)S(1)}, f32[136,512]{1,0:T(8,128)S(1)}, u32[]{:S(2)}, u32[]{:S(2)}) collective-permute-start(f32[136,512]{1,0:T(8,128)S(1)} %shard_map.87.own_ref), channel_id=1, source_target_pairs={{0,1},{1,0},{2,3},{3,2},{4,5},{5,4},{6,7},{7,6},{8,9},{9,8},{10,11... | collective-permute-start | bytes 835592 | tf_op jit(solution)/shard_map/ppermute | solution.py:395
  8.0 15.5 %all-to-all-start = ((f32[256,1,128]{2,1,0:T(1,128)}), f32[256,1,128]{2,1,0:T(1,128)S(1)}, u32[]{:S(2)}, u32[]{:S(2)}) async-start(f32[256,1,128]{2,1,0:T(1,128)} %bitcast.3), calls=%async_computation | async-start | bytes 262144 | tf_op jit(solution)/shard_map/all_to_all | solution.py:373
  15.2 8.8 %collective-permute-start.1 = (f32[1,128,512]{2,1,0:T(8,128)}, f32[1,128,512]{2,1,0:T(8,128)S(1)}, u32[]{:S(2)}, u32[]{:S(2)}) collective-permute-start(f32[1,128,512]{2,1,0:T(8,128)} %copy-done.22), channel_id=1, source_target_pairs={{1,2},{3,4},{5,6},{7,8},{9,10},{11,12},{13,14},{15,16},{17,18},{19... | collective-permute-start | bytes 786440 | tf_op jit(solution)/shard_map/ppermute | solution.py:396
  23.4 1.3 %copy-start.2 = (f32[4,128,512]{2,1,0:T(8,128)S(1)}, f32[4,128,512]{2,1,0:T(8,128)}, u32[]{:S(2)}) copy-start(f32[4,128,512]{2,1,0:T(8,128)} %copy-done.1) | copy-start | bytes 3145732
  24.0 0.7 copy-start.19
  24.7 1.2 %copy-start.3 = (f32[4,128,512]{2,1,0:T(8,128)S(1)}, f32[4,128,512]{2,1,0:T(8,128)}, u32[]{:S(2)}) copy-start(f32[4,128,512]{2,1,0:T(8,128)} %sigma_ref.3) | copy-start | bytes 3145732
  26.0 1.2 %copy-start.5 = (f32[4,128,512]{2,1,0:T(8,128)S(1)}, f32[4,128,512]{2,1,0:T(8,128)}, u32[]{:S(2)}) copy-start(f32[4,128,512]{2,1,0:T(8,128)} %wind_ref.3) | copy-start | bytes 3145732
  27.2 1.0 %copy-start.14 = (bf16[512,512]{1,0:T(8,128)(2,1)S(1)}, bf16[512,512]{1,0:T(8,128)(2,1)}, u32[]{:S(2)}) copy-start(bf16[512,512]{1,0:T(8,128)(2,1)} %copy-done.13) | copy-start | bytes 1572868
  28.2 1.0 %copy-start.16 = (bf16[512,512]{1,0:T(8,128)(2,1)S(1)}, bf16[512,512]{1,0:T(8,128)(2,1)}, u32[]{:S(2)}) copy-start(bf16[512,512]{1,0:T(8,128)(2,1)} %copy-done.15) | copy-start | bytes 1572868
  29.3 0.9 %copy-start.20 = (f32[1,128,512]{2,1,0:T(8,128)S(1)}, f32[1,128,512]{2,1,0:T(8,128)}, u32[]{:S(2)}) copy-start(f32[1,128,512]{2,1,0:T(8,128)} %copy-done.19) | copy-start | bytes 786436
  32.1 1.0 %copy-start.7 = (f32[4,128,512]{2,1,0:T(8,128)}, f32[4,128,512]{2,1,0:T(8,128)S(1)}, u32[]{:S(2)}) copy-start(f32[4,128,512]{2,1,0:T(8,128)S(1)} %get-tuple-element.27.w_ref) | copy-start | bytes 3145732
  33.1 1.0 %copy-start.11 = (f32[4,128,512]{2,1,0:T(8,128)}, f32[4,128,512]{2,1,0:T(8,128)S(1)}, u32[]{:S(2)}) copy-start(f32[4,128,512]{2,1,0:T(8,128)S(1)} %get-tuple-element.24.local_ref) | copy-start | bytes 3145732
  34.1 3.9 %copy-start.21 = (f32[1,128,512]{2,1,0:T(8,128)}, f32[1,128,512]{2,1,0:T(8,128)S(1)}, u32[]{:S(2)}) copy-start(f32[1,128,512]{2,1,0:T(8,128)S(1)} %get-tuple-element.25) | copy-start | bytes 786436
  34.1 3.1 %collective-permute-start.2 = (f32[136,512]{1,0:T(8,128)S(1)}, f32[136,512]{1,0:T(8,128)S(1)}, u32[]{:S(2)}, u32[]{:S(2)}) collective-permute-start(f32[136,512]{1,0:T(8,128)S(1)} %get-tuple-element.23.own_ref), channel_id=1, source_target_pairs={{0,1},{1,0},{2,3},{3,2},{4,5},{5,4},{6,7},{7,6},{8,9},{9,8},{10,11... | collective-permute-start | bytes 835592 | tf_op jit(solution)/shard_map/ppermute | solution.py:395
  37.9 14.4 %all-to-all-start.1 = ((f32[288,1,128]{2,1,0:T(1,128)}), f32[288,1,128]{2,1,0:T(1,128)S(1)}, u32[]{:S(2)}, u32[]{:S(2)}) async-start(f32[288,1,128]{2,1,0:T(1,128)} %bitcast.6), calls=%async_computation.1 | async-start | bytes 294912 | tf_op jit(solution)/shard_map/all_to_all | solution.py:373
  43.8 9.1 %collective-permute-start.3 = (f32[1,128,512]{2,1,0:T(8,128)}, f32[1,128,512]{2,1,0:T(8,128)}, u32[]{:S(2)}, u32[]{:S(2)}) collective-permute-start(f32[1,128,512]{2,1,0:T(8,128)} %copy-done.21), channel_id=1, source_target_pairs={{1,2},{3,4},{5,6},{7,8},{9,10},{11,12},{13,14},{15,16},{17,18},{19... | collective-permute-start | bytes 786440 | tf_op jit(solution)/shard_map/ppermute | solution.py:396
  52.3 1.2 %copy-start.4 = (f32[4,128,512]{2,1,0:T(8,128)S(1)}, f32[4,128,512]{2,1,0:T(8,128)}, u32[]{:S(2)}) copy-start(f32[4,128,512]{2,1,0:T(8,128)} %sigma_ref.3) | copy-start | bytes 3145732
  53.6 1.2 %copy-start.6 = (f32[4,128,512]{2,1,0:T(8,128)S(1)}, f32[4,128,512]{2,1,0:T(8,128)}, u32[]{:S(2)}) copy-start(f32[4,128,512]{2,1,0:T(8,128)} %wind_ref.3) | copy-start | bytes 3145732
  54.8 1.2 %copy-start.8 = (f32[4,128,512]{2,1,0:T(8,128)S(1)}, f32[4,128,512]{2,1,0:T(8,128)}, u32[]{:S(2)}) copy-start(f32[4,128,512]{2,1,0:T(8,128)} %copy-done.7) | copy-start | bytes 3145732
  56.0 1.2 %copy-start.12 = (f32[4,128,512]{2,1,0:T(8,128)S(1)}, f32[4,128,512]{2,1,0:T(8,128)}, u32[]{:S(2)}) copy-start(f32[4,128,512]{2,1,0:T(8,128)} %copy-done.11) | copy-start | bytes 3145732
  57.2 15.9 %copy-start.9 = (f32[4,128,512]{2,1,0:T(8,128)S(1)}, f32[4,128,512]{2,1,0:T(8,128)}, u32[]{:S(2)}) copy-start(f32[4,128,512]{2,1,0:T(8,128)} %copy-done.7) | copy-start | bytes 3145732

commit v5 on v4

--- a/solution.py
+++ b/solution.py
@@ -73,7 +73,7 @@
 
 
 def coarse_kernel(
-    gath_ref, by_ref, bz_ref, gamma_ref, out_ref, tree_ref, *, fold, levels, count, rows, layers
+    gath_ref, gamma_ref, out_ref, tree_ref, *, fold, levels, count, rows, layers
 ):
     each = rows // 2
     stride = gath_ref.shape[0] // count
@@ -101,15 +101,21 @@
         if shift:
             total = total * (me + shift == who).astype(F32)
         coarse.append(unpack(total, fold))
+    for i, block in enumerate(coarse):
+        out_ref[i * block.shape[0] : (i + 1) * block.shape[0], : block.shape[1]] = block
+
+
+def fill_spreads(coarse_ref, by_ref, bz_ref, spread_ref):
     ky = by_ref.shape[0]
-    back = dot3(halves(jnp.concatenate(coarse, axis=0)), halves(bz_ref[...]))
-    back_high, back_low = halves(back)
+    back_high, back_low = halves(
+        dot3(halves(coarse_ref[: 3 * ky, : bz_ref.shape[0]]), halves(bz_ref[...]))
+    )
     by_high, by_low = halves(by_ref[...])
     left = jnp.concatenate([by_high, by_high, by_low], axis=0)
-    for i in range(len(coarse)):
+    for i in range(spread_ref.shape[0]):
         high, low = (part[i * ky : (i + 1) * ky] for part in (back_high, back_low))
         right = jnp.concatenate([high, low, high], axis=0)
-        out_ref[i] = lax.dot_general(left, right, TN, preferred_element_type=F32)
+        spread_ref[i] = lax.dot_general(left, right, TN, preferred_element_type=F32)
 
 
 PAD = 8
@@ -193,27 +199,31 @@
 def first_kernel(
     r_hbm, inv_hbm, local_ref, summed_ref, odd_ref, high_ref, low_ref, rr_ref, r_ref, inv_ref, sems
 ):
-    layers, _, _ = r_ref.shape
-    moves = [(r_hbm.at[x], r_ref.at[x]) for x in range(layers)] + [(inv_hbm.at[0], inv_ref)]
+    layers, _, nz = r_ref.shape
+    half = nz // 2
+    moves = [(inv_hbm.at[0, :half], inv_ref.at[:half])]
+    moves += [(r_hbm.at[x], r_ref.at[x]) for x in range(layers)]
+    moves += [(inv_hbm.at[0, half:], inv_ref.at[half:])]
     loads = [pltpu.make_async_copy(*move, sems.at[i]) for i, move in enumerate(moves)]
     for load in loads:
         load.start()
-    for load in loads[:layers]:
-        load.wait()
+    loads[0].wait()
+    upper = halves(inv_ref[:half])
+    high_ref[:half], low_ref[:half] = upper
     total = jnp.zeros((8, LANES), F32)
-    for j in range(tiles_of(r_ref)):
-        summed = None
-        for x in range(layers):
+    for x in range(layers):
+        loads[x + 1].wait()
+        local_ref[x] = dot3(halves(r_ref[x, :, :half]), upper)
+        for j in range(tiles_of(r_ref)):
             r = r_ref[x, :, columns(j)]
             total = total + rows_sum(r * r)
-            summed = r if x == 0 else summed + r
-        summed_ref[:, columns(j)] = summed
+            summed_ref[:, columns(j)] = r if x == 0 else summed_ref[:, columns(j)] + r
     rr_ref[:8] = total
-    loads[layers].wait()
-    inverse = halves(inv_ref[...])
-    high_ref[...], low_ref[...] = inverse
+    loads[layers + 1].wait()
+    lower = halves(inv_ref[half:])
+    high_ref[half:], low_ref[half:] = lower
     for x in range(layers):
-        local_ref[x] = dot3(halves(r_ref[x]), inverse)
+        local_ref[x] += dot3(halves(r_ref[x, :, half:]), lower)
     odd_ref[0] = local_ref[jnp.where(even_here(), 0, layers - 1)]
 
 
@@ -232,11 +242,12 @@
 
 
 def middle_kernel(
-    spread_ref, local_ref, even_ref, odd_ref, r_ref, sigma_ref, wind_ref, by_ref, bz_ref,
+    coarse_ref, local_ref, even_ref, odd_ref, r_ref, sigma_ref, wind_ref, by_ref, bz_ref,
     high_ref, low_ref, rr_ref,
-    z_ref, w_ref, pair2_ref, local2_ref, odd2_ref, *, fold,
+    z_ref, w_ref, pair2_ref, local2_ref, odd2_ref, spread_ref, *, fold,
 ):
     layers, ny, _ = r_ref.shape
+    fill_spreads(coarse_ref, by_ref, bz_ref, spread_ref)
     clear_pads(z_ref)
     for j in range(tiles_of(r_ref)):
         before, after = halo_of(even_ref, odd_ref, j)
@@ -255,7 +266,10 @@
     for x in range(layers):
         for first in range(0, ny, CHUNK):
             stencil(z_ref, sigma_ref, wind_ref, x, first, CHUNK, emit)
-        local2_ref[x] = dot3(halves(w_ref[x]), (high_ref[...], low_ref[...]))
+        if x % 2:
+            both = halves(w_ref[x - 1 : x + 1].reshape(2 * ny, -1))
+            product = dot3(both, (high_ref[...], low_ref[...]))
+            local2_ref[x - 1 : x + 1] = product.reshape(2, ny, -1)
     summed = w_ref[0]
     for x in range(1, layers):
         summed = summed + w_ref[x]
@@ -283,10 +297,11 @@
 
 
 def last_kernel(
-    gath_ref, spread_ref, local_ref, even_ref, odd_ref, r_ref, z_ref, w_ref,
-    sigma_ref, wind_ref, z2_ref, u_ref, out_ref, known_ref, *, rows,
+    gath_ref, coarse_ref, local_ref, even_ref, odd_ref, r_ref, z_ref, w_ref,
+    sigma_ref, wind_ref, by_ref, bz_ref, z2_ref, u_ref, out_ref, known_ref, spread_ref, *, rows,
 ):
     layers, ny, _ = r_ref.shape
+    fill_spreads(coarse_ref, by_ref, bz_ref, spread_ref)
     beta, h11, h21 = first_scalars(gath_ref, rows)
     scale = 1.0 / (h21 * beta)
     minus = scale * h11
@@ -400,38 +415,39 @@
             [(count * size, width)], (got, sent), flops=matmul // 16,
         )
         block = exchange(block.reshape(count * size, 1, width)).reshape(count * size, width)
-        (spread,) = call(
+        (coarse,) = call(
             functools.partial(
                 coarse_kernel, fold=fold, levels=levels, count=count, rows=rows, layers=layers
             ),
-            [(3, ny, nz)], (block, by, bz, gamma), [(count, rows, width)],
-            flops=matmul // 8,
+            [(-(-3 * ky // 32) * 32, LANES)], (block, gamma), [(count, rows, width)],
+            flops=matmul // 16,
         )
-        return block, spread, got, odd
+        return block, coarse, got, odd
 
     square = jax.ShapeDtypeStruct((nz, nz), BF16)
     local, summed, odd, high, low, rr = call(
         first_kernel, [field, (ny, nz), edge, square, square, (32, LANES)],
         (right_side, local_inverse),
-        [field, (nz, nz), pltpu.SemaphoreType.DMA((layers + 1,))],
+        [field, (nz, nz), pltpu.SemaphoreType.DMA((layers + 2,))],
         flops=matmul, hbm=(0, 1), limit=FIRST_LIMIT,
     )
     (sent,) = call(
         functools.partial(project_kernel, fold=fold), [pair],
         (summed, local, by, bz), flops=matmul // 8,
     )
-    _, spread, got, odd = round_of(sent, odd, 0)
+    _, coarse, got, odd = round_of(sent, odd, 0)
     z, w, sent, local, odd = call(
         functools.partial(middle_kernel, fold=fold),
         [tiled, field, pair, field, edge],
-        (spread, local, got, odd, right_side, sigma, wind, by, bz, high, low, rr),
-        flops=2 * matmul,
-    )
-    gathered, spread, got, odd = round_of(sent, odd, 1)
+        (coarse, local, got, odd, right_side, sigma, wind, by, bz, high, low, rr),
+        [(3, ny, nz)], flops=2 * matmul,
+    )
+    gathered, coarse, got, odd = round_of(sent, odd, 1)
     z2, u, sent, known = call(
         functools.partial(last_kernel, rows=rows),
         [tiled, field, (count, LANES), (32, LANES)],
-        (gathered, spread, local, got, odd, right_side, z, w, sigma, wind), flops=matmul,
+        (gathered, coarse, local, got, odd, right_side, z, w, sigma, wind, by, bz),
+        [(3, ny, nz)], flops=matmul,
     )
     sums = exchange(sent)
     return call(

time: 75.4 us -> 63.9 us (0.85)
  blocking collectives: 13.6 us -> 30.9 us
  starting transfers between devices: 17.5 us -> 5.33 us
  waiting for transfers between devices: 17.1 us -> 9.01 us
  local copies, waits for them, and re-layouts: 14.2 us -> 6.89 us
  Pallas kernels: 11.5 us -> 10.6 us
    all_to_all x1 -> x2, blocking collectives: 13.6 us -> 30.9 us  [exchange(): return lax.all_to_all(block, AXIS, 0, 0, tiled=True)]
    all_to_all x2 -> x1, starting transfers between devices: 13.1 us -> 2.58 us  [exchange(): return lax.all_to_all(block, AXIS, 0, 0, tiled=True)]
    all_to_all x2 -> x1, waiting for transfers between devices: 14.7 us -> 7.15 us  [exchange(): return lax.all_to_all(block, AXIS, 0, 0, tiled=True)]
    unnamed x46 -> x26, local copies, waits for them, and re-layouts: 14.2 us -> 6.89 us
    ppermute x2, starting transfers between devices: 2.41 us -> 0.73 us  [round_of(): got = lax.ppermute(sent, AXIS, pairs)]
    pallas_call x9, Pallas kernels: 11.5 us -> 10.6 us  [call(): pl.pallas_call(kernel, out_shape=outs, in_specs=[far if i in hbm else vme...]
  transfers between devices with their start and end apart: 6 -> 5, of which waited for: 4 -> 3; matrix products, arithmetic and copies ran while one was open for 0% -> 0% of each run, Pallas kernels for 2% -> 1%
where the time goes in v5:
time: 63.9 us; the launch traced here: 63.5 us
  blocking collectives  30.9 us (48%)
  Pallas kernels  10.6 us (17%)
  waiting for transfers between devices  9.01 us (14%)
  local copies, waits for them, and re-layouts  6.89 us (11%)
  starting transfers between devices  5.33 us (8%)
  between operations  0.77 us (1%)
    all_to_all x2, blocking collectives, exchange(): return lax.all_to_all(block, AXIS, 0, 0, tiled=True)  30.9 us
    pallas_call x9, Pallas kernels, call(): pl.pallas_call(kernel, out_shape=outs, in_specs=[far if i in hbm else vme...  10.6 us
    all_to_all x1, waiting for transfers between devices, exchange(): return lax.all_to_all(block, AXIS, 0, 0, tiled=True)  7.15 us
    unnamed x26, local copies, waits for them, and re-layouts  6.89 us
    all_to_all x1, starting transfers between devices, exchange(): return lax.all_to_all(block, AXIS, 0, 0, tiled=True)  2.58 us
    ppermute x2, starting transfers between devices, round_of(): odd = lax.ppermute(odd, AXIS, others)  2.02 us
    ppermute x2, waiting for transfers between devices, round_of(): got = lax.ppermute(sent, AXIS, pairs)  1.85 us
  transfers between devices with their start and end apart: 5, of which 3 were waited for; matrix products, arithmetic and copies ran while one was open for 0% of the time, Pallas kernels for 1%

profile of v5, /device:TPU:0, one launch (start us, length us, event | category | flops | bytes accessed | tf_op | source)
XLA Modules:
  0.0 63.5 jit_solution(2442418474601149382)
XLA Ops:
  0.6 0.0 copy-start.7
  0.6 0.0 copy-start.11
  0.7 0.0 copy-start.5
  0.7 2.7 %shard_map.86 = (f32[4,128,512]{2,1,0:T(8,128)S(1)}, f32[128,512]{1,0:T(8,128)S(1)}, f32[1,128,512]{2,1,0:T(8,128)S(1)}, bf16[512,512]{1,0:T(8,128)(2,1)S(1)}, b...) custom-call(f32[4,128,512]{2,1,0:T(8,128)} %r_ref.5, f32[1,512,512]{2,1,0:T(8,128)} %inv_hbm.1), custom_call_target="tpu_custom_call" | custom-call | flops 805306368 | tf_op jit(solution)/shard_map/pallas_call | solution.py:376
  3.3 0.0 copy-start.10
  3.3 0.0 copy-start
  3.4 0.0 copy-start.3
  3.4 0.0 copy-done.7
  3.4 0.0 copy-done.11
  3.4 0.5 shard_map.87.own_ref
  3.9 0.5 collective-permute-start
  4.4 0.7 %collective-permute-start.1 = (f32[1,128,512]{2,1,0:T(8,128)S(1)}, f32[1,128,512]{2,1,0:T(8,128)S(1)}, u32[]{:S(2)}, u32[]{:S(2)}) collective-permute-start(f32[1,128,512]{2,1,0:T(8,128)S(1)} %get-tuple-element.19), channel_id=1, source_target_pairs={{1,2},{3,4},{5,6},{7,8},{9,10},{11,12},{13,14},{15,16},{17,18},{19... | collective-permute-start | bytes 786440 | tf_op jit(solution)/shard_map/ppermute | solution.py:411
  5.1 0.5 collective-permute-done.got_ref.even_ref
  5.6 16.2 %all_to_all.21 = f32[256,1,128]{2,1,0:T(1,128)S(1)} all-to-all(f32[256,1,128]{2,1,0:T(1,128)S(1)} %bitcast.20), channel_id=1, replica_groups=mesh['sub'=32] {'sub'}, dimensions={0} | all-to-all | bytes 262144 | tf_op jit(solution)/shard_map/all_to_all | solution.py:388
  21.8 0.0 copy-done.10
  21.8 0.2 shard_map.89.coarse_ref
  22.0 0.0 collective-permute-done.1.odd_ref
  22.0 0.0 copy-done.5
  22.0 0.0 copy-done
  22.0 0.0 copy-done.3
  22.0 2.3 %shard_map.90 = (f32[6,4,144,128]{3,2,1,0:T(8,128)S(1)}, f32[4,128,512]{2,1,0:T(8,128)S(1)}, f32[136,512]{1,0:T(8,128)S(1)}, f32[4,128,512]{2,1,0:T(8,128)S(1)}, f32[1,128,512]{2,1,0:T(8,128)S(1)}) custom-call(f32[96,128]{1,0:T(8,128)S(1)} %shard_map.89.coarse_ref, f32[4,128,512]{2,1,0:T(8,128)S(1)} %get-tuple-element.18.local_ref, ...), custom_call_target="tpu_custom_call" | custom-call | flops 1610612736 | tf_op jit(solution)/shard_map/pallas_call | solution.py:376
  24.3 0.0 copy-start.1
  24.3 1.0 %copy-done.1 = f32[4,128,512]{2,1,0:T(8,128)} copy-done((f32[4,128,512]{2,1,0:T(8,128)}, f32[4,128,512]{2,1,0:T(8,128)S(1)}, u32[]{:S(2)}) %copy-start.1) | copy-done | bytes 1048600
  25.3 0.0 copy-start.8
  25.3 1.0 %copy-done.8 = f32[4,128,512]{2,1,0:T(8,128)} copy-done((f32[4,128,512]{2,1,0:T(8,128)}, f32[4,128,512]{2,1,0:T(8,128)S(1)}, u32[]{:S(2)}) %copy-start.8) | copy-done | bytes 1048600
  26.2 0.0 copy-start.12
  26.2 0.2 collective-permute-start.2
  26.5 1.3 %collective-permute-done.2.got_ref.even_ref = f32[136,512]{1,0:T(8,128)S(1)} collective-permute-done((f32[136,512]{1,0:T(8,128)S(1)}, f32[136,512]{1,0:T(8,128)S(1)}, u32[]{:S(2)}, u32[]{:S(2)}) %collective-permute-start.2) | collective-permute-done | bytes 278560 | tf_op jit(solution)/shard_map/ppermute | solution.py:410
  27.8 0.8 %shard_map.91 = f32[288,128]{1,0:T(8,128)} custom-call(f32[136,512]{1,0:T(8,128)S(1)} %collective-permute-done.2.got_ref.even_ref, f32[136,512]{1,0:T(8,128)S(1)} %get-tuple-element.23.own_ref), custom_call_target="tpu_custom_call" | custom-call | flops 50331648 | tf_op jit(solution)/shard_map/pallas_call | solution.py:376
  28.6 0.0 copy-done.12
  28.6 2.6 %all-to-all-start.1 = ((f32[288,1,128]{2,1,0:T(1,128)}), f32[288,1,128]{2,1,0:T(1,128)S(1)}, u32[]{:S(2)}, u32[]{:S(2)}) async-start(f32[288,1,128]{2,1,0:T(1,128)} %bitcast.6), calls=%async_computation.1 | async-start | bytes 294912 | tf_op jit(solution)/shard_map/all_to_all | solution.py:388
  31.2 1.4 %collective-permute-start.3 = (f32[1,128,512]{2,1,0:T(8,128)}, f32[1,128,512]{2,1,0:T(8,128)}, u32[]{:S(2)}, u32[]{:S(2)}) collective-permute-start(f32[1,128,512]{2,1,0:T(8,128)} %copy-done.12), channel_id=1, source_target_pairs={{1,2},{3,4},{5,6},{7,8},{9,10},{11,12},{13,14},{15,16},{17,18},{19... | collective-permute-start | bytes 786440 | tf_op jit(solution)/shard_map/ppermute | solution.py:411
  32.5 7.2 %all-to-all-done.1 = f32[288,1,128]{2,1,0:T(1,128)S(1)} async-done(((f32[288,1,128]{2,1,0:T(1,128)}), f32[288,1,128]{2,1,0:T(1,128)S(1)}, u32[]{:S(2)}, u32[]{:S(2)}) %all-to-all-start.1) | async-done | bytes 147488 | tf_op jit(solution)/shard_map/all_to_all | solution.py:388
  39.7 0.2 shard_map.92.coarse_ref
  39.8 0.0 collective-permute-done.3.odd_ref
  39.9 0.0 copy-start.2
  39.9 1.2 %copy-done.2 = f32[4,128,512]{2,1,0:T(8,128)S(1)} copy-done((f32[4,128,512]{2,1,0:T(8,128)S(1)}, f32[4,128,512]{2,1,0:T(8,128)}, u32[]{:S(2)}) %copy-start.2) | copy-done | bytes 1048600
  41.1 0.0 copy-start.4
  41.1 1.2 %copy-done.4 = f32[4,128,512]{2,1,0:T(8,128)S(1)} copy-done((f32[4,128,512]{2,1,0:T(8,128)S(1)}, f32[4,128,512]{2,1,0:T(8,128)}, u32[]{:S(2)}) %copy-start.4) | copy-done | bytes 1048600
  42.3 0.0 copy-start.6
  42.3 1.2 %copy-done.6 = f32[4,128,512]{2,1,0:T(8,128)S(1)} copy-done((f32[4,128,512]{2,1,0:T(8,128)S(1)}, f32[4,128,512]{2,1,0:T(8,128)}, u32[]{:S(2)}) %copy-start.6) | copy-done | bytes 1048600
  43.5 0.0 copy-start.9
  43.5 1.2 %copy-done.9 = f32[4,128,512]{2,1,0:T(8,128)S(1)} copy-done((f32[4,128,512]{2,1,0:T(8,128)S(1)}, f32[4,128,512]{2,1,0:T(8,128)}, u32[]{:S(2)}) %copy-start.9) | copy-done | bytes 1048600
  44.8 2.4 %shard_map.93 = (f32[6,4,144,128]{3,2,1,0:T(8,128)S(1)}, f32[4,128,512]{2,1,0:T(8,128)S(1)}, f32[32,128]{1,0:T(8,128)S(1)}, f32[32,128]{1,0:T(8,128)S(1)}) custom-call(f32[288,128]{1,0:T(8,128)S(1)} %bitcast.15, f32[96,128]{1,0:T(8,128)S(1)} %shard_map.92.coarse_ref, f32[4,128,512]{2,1,0:T(8,128)S(1)} %copy-done.9, ...), custom_call_target="tpu_custom_call" | custom-call | flops 805306368 | tf_op jit(solution)/shard_map/pallas_call | solution.py:376
  47.2 14.7 %all_to_all.22 = f32[32,1,128]{2,1,0:T(1,128)S(1)} all-to-all(f32[32,1,128]{2,1,0:T(1,128)S(1)} %bitcast.25), channel_id=1, replica_groups=mesh['sub'=32] {'sub'}, dimensions={0} | all-to-all | bytes 32768 | tf_op jit(solution)/shard_map/all_to_all | solution.py:388
  61.9 1.6 %shard_map.94 = (f32[4,128,512]{2,1,0:T(8,128)}, f32[4,128,512]{2,1,0:T(8,128)}) custom-call(f32[32,128]{1,0:T(8,128)S(1)} %bitcast.24, f32[32,128]{1,0:T(8,128)S(1)} %get-tuple-element.29.known_ref, f32[4,128,512]{2,1,0:T(8,128)S(1)} %copy-done, f32[6,4,144,128]{3,2,1,0:T(8,128)S(1)} %get-tuple-element.26.z_ref, f32[4,128,512]{2,1,0:T(8,128)S(1)} %copy-done.2, ...), custom_call_target="tpu_custom_call" | custom-call | flops 100663296 | tf_op jit(solution)/shard_map/pallas_call | solution.py:376
  (1 shorter events, 0.0 us)
Async XLA Ops:
  0.6 2.7 %copy-start.7 = (f32[512,64]{0,1:T(8,128)S(1)}, f32[512,64]{0,1:T(8,128)}, u32[]{:S(2)}) copy-start(f32[512,64]{0,1:T(8,128)} %param.12) | copy-start | bytes 393220
  0.6 2.7 %copy-start.11 = (f32[128,32]{0,1:T(8,128)S(1)}, f32[128,32]{0,1:T(8,128)}, u32[]{:S(2)}) copy-start(f32[128,32]{0,1:T(8,128)} %param.11) | copy-start | bytes 49156
  0.7 21.3 %copy-start.5 = (f32[4,128,512]{2,1,0:T(8,128)S(1)}, f32[4,128,512]{2,1,0:T(8,128)}, u32[]{:S(2)}) copy-start(f32[4,128,512]{2,1,0:T(8,128)} %wind_ref.3) | copy-start | bytes 3145732
  3.3 18.5 %copy-start.10 = (f32[5,32,64]{2,1,0:T(8,128)S(1)}, f32[5,32,64]{2,1,0:T(8,128)}, u32[]{:S(2)}) copy-start(f32[5,32,64]{2,1,0:T(8,128)} %gamma_ref.3) | copy-start | bytes 122884
  3.3 18.6 %copy-start = (f32[4,128,512]{2,1,0:T(8,128)S(1)}, f32[4,128,512]{2,1,0:T(8,128)}, u32[]{:S(2)}) copy-start(f32[4,128,512]{2,1,0:T(8,128)} %r_ref.5) | copy-start | bytes 3145732
  3.4 18.6 %copy-start.3 = (f32[4,128,512]{2,1,0:T(8,128)S(1)}, f32[4,128,512]{2,1,0:T(8,128)}, u32[]{:S(2)}) copy-start(f32[4,128,512]{2,1,0:T(8,128)} %sigma_ref.3) | copy-start | bytes 3145732
  3.9 1.7 %collective-permute-start = (f32[136,512]{1,0:T(8,128)S(1)}, f32[136,512]{1,0:T(8,128)S(1)}, u32[]{:S(2)}, u32[]{:S(2)}) collective-permute-start(f32[136,512]{1,0:T(8,128)S(1)} %shard_map.87.own_ref), channel_id=1, source_target_pairs={{0,1},{1,0},{2,3},{3,2},{4,5},{5,4},{6,7},{7,6},{8,9},{9,8},{10,11... | collective-permute-start | bytes 835592 | tf_op jit(solution)/shard_map/ppermute | solution.py:410
  4.4 17.6 %collective-permute-start.1 = (f32[1,128,512]{2,1,0:T(8,128)S(1)}, f32[1,128,512]{2,1,0:T(8,128)S(1)}, u32[]{:S(2)}, u32[]{:S(2)}) collective-permute-start(f32[1,128,512]{2,1,0:T(8,128)S(1)} %get-tuple-element.19), channel_id=1, source_target_pairs={{1,2},{3,4},{5,6},{7,8},{9,10},{11,12},{13,14},{15,16},{17,18},{19... | collective-permute-start | bytes 786440 | tf_op jit(solution)/shard_map/ppermute | solution.py:411
  24.3 1.0 %copy-start.1 = (f32[4,128,512]{2,1,0:T(8,128)}, f32[4,128,512]{2,1,0:T(8,128)S(1)}, u32[]{:S(2)}) copy-start(f32[4,128,512]{2,1,0:T(8,128)S(1)} %get-tuple-element.27.w_ref) | copy-start | bytes 3145732
  25.3 1.0 %copy-start.8 = (f32[4,128,512]{2,1,0:T(8,128)}, f32[4,128,512]{2,1,0:T(8,128)S(1)}, u32[]{:S(2)}) copy-start(f32[4,128,512]{2,1,0:T(8,128)S(1)} %get-tuple-element.24.local_ref) | copy-start | bytes 3145732
  26.2 2.4 %copy-start.12 = (f32[1,128,512]{2,1,0:T(8,128)}, f32[1,128,512]{2,1,0:T(8,128)S(1)}, u32[]{:S(2)}) copy-start(f32[1,128,512]{2,1,0:T(8,128)S(1)} %get-tuple-element.25) | copy-start | bytes 786436
  26.2 1.6 %collective-permute-start.2 = (f32[136,512]{1,0:T(8,128)S(1)}, f32[136,512]{1,0:T(8,128)S(1)}, u32[]{:S(2)}, u32[]{:S(2)}) collective-permute-start(f32[136,512]{1,0:T(8,128)S(1)} %get-tuple-element.23.own_ref), channel_id=1, source_target_pairs={{0,1},{1,0},{2,3},{3,2},{4,5},{5,4},{6,7},{7,6},{8,9},{9,8},{10,11... | collective-permute-start | bytes 835592 | tf_op jit(solution)/shard_map/ppermute | solution.py:410
  28.6 11.1 %all-to-all-start.1 = ((f32[288,1,128]{2,1,0:T(1,128)}), f32[288,1,128]{2,1,0:T(1,128)S(1)}, u32[]{:S(2)}, u32[]{:S(2)}) async-start(f32[288,1,128]{2,1,0:T(1,128)} %bitcast.6), calls=%async_computation.1 | async-start | bytes 294912 | tf_op jit(solution)/shard_map/all_to_all | solution.py:388
  31.2 8.7 %collective-permute-start.3 = (f32[1,128,512]{2,1,0:T(8,128)}, f32[1,128,512]{2,1,0:T(8,128)}, u32[]{:S(2)}, u32[]{:S(2)}) collective-permute-start(f32[1,128,512]{2,1,0:T(8,128)} %copy-done.12), channel_id=1, source_target_pairs={{1,2},{3,4},{5,6},{7,8},{9,10},{11,12},{13,14},{15,16},{17,18},{19... | collective-permute-start | bytes 786440 | tf_op jit(solution)/shard_map/ppermute | solution.py:411
  39.9 1.2 %copy-start.2 = (f32[4,128,512]{2,1,0:T(8,128)S(1)}, f32[4,128,512]{2,1,0:T(8,128)}, u32[]{:S(2)}) copy-start(f32[4,128,512]{2,1,0:T(8,128)} %copy-done.1) | copy-start | bytes 3145732
  41.1 1.2 %copy-start.4 = (f32[4,128,512]{2,1,0:T(8,128)S(1)}, f32[4,128,512]{2,1,0:T(8,128)}, u32[]{:S(2)}) copy-start(f32[4,128,512]{2,1,0:T(8,128)} %sigma_ref.3) | copy-start | bytes 3145732
  42.3 1.2 %copy-start.6 = (f32[4,128,512]{2,1,0:T(8,128)S(1)}, f32[4,128,512]{2,1,0:T(8,128)}, u32[]{:S(2)}) copy-start(f32[4,128,512]{2,1,0:T(8,128)} %wind_ref.3) | copy-start | bytes 3145732
  43.5 1.2 %copy-start.9 = (f32[4,128,512]{2,1,0:T(8,128)S(1)}, f32[4,128,512]{2,1,0:T(8,128)}, u32[]{:S(2)}) copy-start(f32[4,128,512]{2,1,0:T(8,128)} %copy-done.8) | copy-start | bytes 3145732

commit v6 on v5

--- a/solution.py
+++ b/solution.py
@@ -15,7 +15,7 @@
 NT = (((1,), (1,)), ((), ()))
 TN = (((0,), (0,)), ((), ()))
 CHUNK = 16
-FIRST_LIMIT = 51
+FIRST_LIMIT = 50
 
 
 def halves(x):
@@ -48,8 +48,14 @@
 
 
 def project(summed, by, bz, fold):
-    half = dot3(halves(summed), halves(bz), NT)
-    return pack(dot3(halves(by), halves(half)), fold)
+    high, low = halves(summed)
+    by_high, by_low = halves(by)
+    half = lax.dot_general(
+        jnp.concatenate([by_high, by_low], axis=0), high, NN, preferred_element_type=F32
+    )
+    ky = by.shape[0]
+    half = half[:ky] + (half[ky:] + jnp.dot(by_high, low, preferred_element_type=F32))
+    return pack(dot3(halves(half), halves(bz), NT), fold)
 
 
 def join_kernel(got_ref, own_ref, out_ref, *, rows, width, extra):
@@ -197,7 +203,8 @@
 
 
 def first_kernel(
-    r_hbm, inv_hbm, local_ref, summed_ref, odd_ref, high_ref, low_ref, rr_ref, r_ref, inv_ref, sems
+    r_hbm, inv_hbm, local_ref, summed_ref, odd_ref, high_ref, low_ref, rr_ref, r_ref,
+    inv_ref, sems
 ):
     layers, _, nz = r_ref.shape
     half = nz // 2
@@ -425,10 +432,10 @@
         return block, coarse, got, odd
 
     square = jax.ShapeDtypeStruct((nz, nz), BF16)
-    local, summed, odd, high, low, rr = call(
-        first_kernel, [field, (ny, nz), edge, square, square, (32, LANES)],
+    local, summed, odd, high, low, rr, r = call(
+        first_kernel, [field, (ny, nz), edge, square, square, (32, LANES), field],
         (right_side, local_inverse),
-        [field, (nz, nz), pltpu.SemaphoreType.DMA((layers + 2,))],
+        [(nz, nz), pltpu.SemaphoreType.DMA((layers + 2,))],
         flops=matmul, hbm=(0, 1), limit=FIRST_LIMIT,
     )
     (sent,) = call(
@@ -439,19 +446,19 @@
     z, w, sent, local, odd = call(
         functools.partial(middle_kernel, fold=fold),
         [tiled, field, pair, field, edge],
-        (coarse, local, got, odd, right_side, sigma, wind, by, bz, high, low, rr),
+        (coarse, local, got, odd, r, sigma, wind, by, bz, high, low, rr),
         [(3, ny, nz)], flops=2 * matmul,
     )
     gathered, coarse, got, odd = round_of(sent, odd, 1)
     z2, u, sent, known = call(
         functools.partial(last_kernel, rows=rows),
         [tiled, field, (count, LANES), (32, LANES)],
-        (gathered, coarse, local, got, odd, right_side, z, w, sigma, wind, by, bz),
+        (gathered, coarse, local, got, odd, r, z, w, sigma, wind, by, bz),
         [(3, ny, nz)], flops=matmul,
     )
     sums = exchange(sent)
     return call(
-        finish_kernel, [field, field], (sums, known, right_side, z, w, z2, u),
+        finish_kernel, [field, field], (sums, known, r, z, w, z2, u),
         [field, field, pltpu.SemaphoreType.DMA((2 * layers,))],
         flops=matmul // 8, far_out=True,
     )

time: 63.9 us -> 63.7 us (level)
    unnamed x26 -> x24, local copies, waits for them, and re-layouts: 6.89 us -> 6.97 us
where the time goes in v6:
time: 63.7 us; the launch traced here: 63.3 us
  blocking collectives  30.9 us (49%)
  Pallas kernels  10.3 us (16%)
  waiting for transfers between devices  9.01 us (14%)
  local copies, waits for them, and re-layouts  6.97 us (11%)
  starting transfers between devices  5.35 us (8%)
  between operations  0.75 us (1%)
    all_to_all x2, blocking collectives, exchange(): return lax.all_to_all(block, AXIS, 0, 0, tiled=True)  30.9 us
    pallas_call x9, Pallas kernels, call(): pl.pallas_call(kernel, out_shape=outs, in_specs=[far if i in hbm else vme...  10.3 us
    all_to_all x1, waiting for transfers between devices, exchange(): return lax.all_to_all(block, AXIS, 0, 0, tiled=True)  7.15 us
    unnamed x24, local copies, waits for them, and re-layouts  6.97 us
    all_to_all x1, starting transfers between devices, exchange(): return lax.all_to_all(block, AXIS, 0, 0, tiled=True)  2.58 us
    ppermute x2, starting transfers between devices, round_of(): odd = lax.ppermute(odd, AXIS, others)  2.03 us
    ppermute x2, waiting for transfers between devices, round_of(): got = lax.ppermute(sent, AXIS, pairs)  1.86 us
  transfers between devices with their start and end apart: 5, of which 3 were waited for; matrix products, arithmetic and copies ran while one was open for 0% of the time, Pallas kernels for 1%

profile of v6, /device:TPU:0, one launch (start us, length us, event | category | flops | bytes accessed | tf_op | source)
XLA Modules:
  0.0 63.3 jit_solution(17176719673701307002)
XLA Ops:
  0.6 0.0 copy-start.6
  0.6 0.0 copy-start.10
  0.7 2.6 %shard_map.86 = (f32[4,128,512]{2,1,0:T(8,128)S(1)}, f32[128,512]{1,0:T(8,128)S(1)}, f32[1,128,512]{2,1,0:T(8,128)S(1)}, bf16[512,512]{1,0:T(8,128)(2,1)S(1)}, b...) custom-call(f32[4,128,512]{2,1,0:T(8,128)} %r_hbm.1, f32[1,512,512]{2,1,0:T(8,128)} %inv_hbm.1), custom_call_target="tpu_custom_call" | custom-call | flops 805306368 | tf_op jit(solution)/shard_map/pallas_call | solution.py:383
  3.3 0.0 copy-start.9
  3.3 0.0 copy-start.2
  3.3 0.0 copy-start.4
  3.3 0.0 copy-done.6
  3.3 0.0 copy-done.10
  3.3 0.4 shard_map.87.own_ref
  3.7 0.5 collective-permute-start
  4.3 0.7 %collective-permute-start.1 = (f32[1,128,512]{2,1,0:T(8,128)S(1)}, f32[1,128,512]{2,1,0:T(8,128)S(1)}, u32[]{:S(2)}, u32[]{:S(2)}) collective-permute-start(f32[1,128,512]{2,1,0:T(8,128)S(1)} %get-tuple-element.20), channel_id=1, source_target_pairs={{1,2},{3,4},{5,6},{7,8},{9,10},{11,12},{13,14},{15,16},{17,18},{19... | collective-permute-start | bytes 786440 | tf_op jit(solution)/shard_map/ppermute | solution.py:418
  4.9 0.5 collective-permute-done.got_ref.even_ref
  5.5 16.2 %all_to_all.21 = f32[256,1,128]{2,1,0:T(1,128)S(1)} all-to-all(f32[256,1,128]{2,1,0:T(1,128)S(1)} %bitcast.20), channel_id=1, replica_groups=mesh['sub'=32] {'sub'}, dimensions={0} | all-to-all | bytes 262144 | tf_op jit(solution)/shard_map/all_to_all | solution.py:395
  21.7 0.0 copy-done.9
  21.7 0.2 shard_map.89.coarse_ref
  21.9 0.0 collective-permute-done.1.odd_ref
  21.9 0.0 copy-done.2
  21.9 0.0 copy-done.4
  21.9 2.1 %shard_map.90 = (f32[6,4,144,128]{3,2,1,0:T(8,128)S(1)}, f32[4,128,512]{2,1,0:T(8,128)S(1)}, f32[136,512]{1,0:T(8,128)S(1)}, f32[4,128,512]{2,1,0:T(8,128)S(1)}, f32[1,128,512]{2,1,0:T(8,128)S(1)}) custom-call(f32[96,128]{1,0:T(8,128)S(1)} %shard_map.89.coarse_ref, f32[4,128,512]{2,1,0:T(8,128)S(1)} %get-tuple-element.19.local_ref, ...), custom_call_target="tpu_custom_call" | custom-call | flops 1610612736 | tf_op jit(solution)/shard_map/pallas_call | solution.py:383
  24.0 0.0 copy-start
  24.0 1.1 %copy-done = f32[4,128,512]{2,1,0:T(8,128)} copy-done((f32[4,128,512]{2,1,0:T(8,128)}, f32[4,128,512]{2,1,0:T(8,128)S(1)}, u32[]{:S(2)}) %copy-start) | copy-done | bytes 1048600
  25.1 0.0 copy-start.7
  25.1 1.0 %copy-done.7 = f32[4,128,512]{2,1,0:T(8,128)} copy-done((f32[4,128,512]{2,1,0:T(8,128)}, f32[4,128,512]{2,1,0:T(8,128)S(1)}, u32[]{:S(2)}) %copy-start.7) | copy-done | bytes 1048600
  26.0 0.0 copy-start.11
  26.0 0.2 collective-permute-start.2
  26.2 1.3 %collective-permute-done.2.got_ref.even_ref = f32[136,512]{1,0:T(8,128)S(1)} collective-permute-done((f32[136,512]{1,0:T(8,128)S(1)}, f32[136,512]{1,0:T(8,128)S(1)}, u32[]{:S(2)}, u32[]{:S(2)}) %collective-permute-start.2) | collective-permute-done | bytes 278560 | tf_op jit(solution)/shard_map/ppermute | solution.py:417
  27.6 0.8 %shard_map.91 = f32[288,128]{1,0:T(8,128)} custom-call(f32[136,512]{1,0:T(8,128)S(1)} %collective-permute-done.2.got_ref.even_ref, f32[136,512]{1,0:T(8,128)S(1)} %get-tuple-element.25.own_ref), custom_call_target="tpu_custom_call" | custom-call | flops 50331648 | tf_op jit(solution)/shard_map/pallas_call | solution.py:383
  28.4 0.0 copy-done.11
  28.4 2.6 %all-to-all-start.1 = ((f32[288,1,128]{2,1,0:T(1,128)}), f32[288,1,128]{2,1,0:T(1,128)S(1)}, u32[]{:S(2)}, u32[]{:S(2)}) async-start(f32[288,1,128]{2,1,0:T(1,128)} %bitcast.6), calls=%async_computation.1 | async-start | bytes 294912 | tf_op jit(solution)/shard_map/all_to_all | solution.py:395
  31.0 1.4 %collective-permute-start.3 = (f32[1,128,512]{2,1,0:T(8,128)}, f32[1,128,512]{2,1,0:T(8,128)}, u32[]{:S(2)}, u32[]{:S(2)}) collective-permute-start(f32[1,128,512]{2,1,0:T(8,128)} %copy-done.11), channel_id=1, source_target_pairs={{1,2},{3,4},{5,6},{7,8},{9,10},{11,12},{13,14},{15,16},{17,18},{19... | collective-permute-start | bytes 786440 | tf_op jit(solution)/shard_map/ppermute | solution.py:418
  32.3 7.1 %all-to-all-done.1 = f32[288,1,128]{2,1,0:T(1,128)S(1)} async-done(((f32[288,1,128]{2,1,0:T(1,128)}), f32[288,1,128]{2,1,0:T(1,128)S(1)}, u32[]{:S(2)}, u32[]{:S(2)}) %all-to-all-start.1) | async-done | bytes 147488 | tf_op jit(solution)/shard_map/all_to_all | solution.py:395
  39.5 0.2 shard_map.92.coarse_ref
  39.6 0.0 collective-permute-done.3.odd_ref
  39.6 0.0 copy-start.1
  39.6 1.2 %copy-done.1 = f32[4,128,512]{2,1,0:T(8,128)S(1)} copy-done((f32[4,128,512]{2,1,0:T(8,128)S(1)}, f32[4,128,512]{2,1,0:T(8,128)}, u32[]{:S(2)}) %copy-start.1) | copy-done | bytes 1048600
  40.9 0.0 copy-start.3
  40.9 1.2 %copy-done.3 = f32[4,128,512]{2,1,0:T(8,128)S(1)} copy-done((f32[4,128,512]{2,1,0:T(8,128)S(1)}, f32[4,128,512]{2,1,0:T(8,128)}, u32[]{:S(2)}) %copy-start.3) | copy-done | bytes 1048600
  42.1 0.0 copy-start.5
  42.1 1.2 %copy-done.5 = f32[4,128,512]{2,1,0:T(8,128)S(1)} copy-done((f32[4,128,512]{2,1,0:T(8,128)S(1)}, f32[4,128,512]{2,1,0:T(8,128)}, u32[]{:S(2)}) %copy-start.5) | copy-done | bytes 1048600
  43.3 0.0 copy-start.8
  43.3 1.2 %copy-done.8 = f32[4,128,512]{2,1,0:T(8,128)S(1)} copy-done((f32[4,128,512]{2,1,0:T(8,128)S(1)}, f32[4,128,512]{2,1,0:T(8,128)}, u32[]{:S(2)}) %copy-start.8) | copy-done | bytes 1048600
  44.5 2.4 %shard_map.93 = (f32[6,4,144,128]{3,2,1,0:T(8,128)S(1)}, f32[4,128,512]{2,1,0:T(8,128)S(1)}, f32[32,128]{1,0:T(8,128)S(1)}, f32[32,128]{1,0:T(8,128)S(1)}) custom-call(f32[288,128]{1,0:T(8,128)S(1)} %bitcast.15, f32[96,128]{1,0:T(8,128)S(1)} %shard_map.92.coarse_ref, f32[4,128,512]{2,1,0:T(8,128)S(1)} %copy-done.8, ...), custom_call_target="tpu_custom_call" | custom-call | flops 805306368 | tf_op jit(solution)/shard_map/pallas_call | solution.py:383
  47.0 14.7 %all_to_all.22 = f32[32,1,128]{2,1,0:T(1,128)S(1)} all-to-all(f32[32,1,128]{2,1,0:T(1,128)S(1)} %bitcast.25), channel_id=1, replica_groups=mesh['sub'=32] {'sub'}, dimensions={0} | all-to-all | bytes 32768 | tf_op jit(solution)/shard_map/all_to_all | solution.py:395
  61.7 1.6 %shard_map.94 = (f32[4,128,512]{2,1,0:T(8,128)}, f32[4,128,512]{2,1,0:T(8,128)}) custom-call(f32[32,128]{1,0:T(8,128)S(1)} %bitcast.24, f32[32,128]{1,0:T(8,128)S(1)} %get-tuple-element.31.known_ref, f32[4,128,512]{2,1,0:T(8,128)S(1)} %get-tuple-element.21.r_ref, f32[6,4,144,128]{3,2,1,0:T(8,128)S(1)} %get-tuple-element.28.z_ref, ...), custom_call_target="tpu_custom_call" | custom-call | flops 100663296 | tf_op jit(solution)/shard_map/pallas_call | solution.py:383
  (1 shorter events, 0.0 us)
Async XLA Ops:
  0.6 2.7 %copy-start.6 = (f32[512,64]{0,1:T(8,128)S(1)}, f32[512,64]{0,1:T(8,128)}, u32[]{:S(2)}) copy-start(f32[512,64]{0,1:T(8,128)} %param.12) | copy-start | bytes 393220
  0.6 2.7 %copy-start.10 = (f32[128,32]{0,1:T(8,128)S(1)}, f32[128,32]{0,1:T(8,128)}, u32[]{:S(2)}) copy-start(f32[128,32]{0,1:T(8,128)} %param.11) | copy-start | bytes 49156
  3.3 18.4 %copy-start.9 = (f32[5,32,64]{2,1,0:T(8,128)S(1)}, f32[5,32,64]{2,1,0:T(8,128)}, u32[]{:S(2)}) copy-start(f32[5,32,64]{2,1,0:T(8,128)} %gamma_ref.3) | copy-start | bytes 122884
  3.3 18.6 %copy-start.2 = (f32[4,128,512]{2,1,0:T(8,128)S(1)}, f32[4,128,512]{2,1,0:T(8,128)}, u32[]{:S(2)}) copy-start(f32[4,128,512]{2,1,0:T(8,128)} %sigma_ref.3) | copy-start | bytes 3145732
  3.3 18.6 %copy-start.4 = (f32[4,128,512]{2,1,0:T(8,128)S(1)}, f32[4,128,512]{2,1,0:T(8,128)}, u32[]{:S(2)}) copy-start(f32[4,128,512]{2,1,0:T(8,128)} %wind_ref.3) | copy-start | bytes 3145732
  3.7 1.7 %collective-permute-start = (f32[136,512]{1,0:T(8,128)S(1)}, f32[136,512]{1,0:T(8,128)S(1)}, u32[]{:S(2)}, u32[]{:S(2)}) collective-permute-start(f32[136,512]{1,0:T(8,128)S(1)} %shard_map.87.own_ref), channel_id=1, source_target_pairs={{0,1},{1,0},{2,3},{3,2},{4,5},{5,4},{6,7},{7,6},{8,9},{9,8},{10,11... | collective-permute-start | bytes 835592 | tf_op jit(solution)/shard_map/ppermute | solution.py:417
  4.3 17.6 %collective-permute-start.1 = (f32[1,128,512]{2,1,0:T(8,128)S(1)}, f32[1,128,512]{2,1,0:T(8,128)S(1)}, u32[]{:S(2)}, u32[]{:S(2)}) collective-permute-start(f32[1,128,512]{2,1,0:T(8,128)S(1)} %get-tuple-element.20), channel_id=1, source_target_pairs={{1,2},{3,4},{5,6},{7,8},{9,10},{11,12},{13,14},{15,16},{17,18},{19... | collective-permute-start | bytes 786440 | tf_op jit(solution)/shard_map/ppermute | solution.py:418
  24.0 1.1 %copy-start = (f32[4,128,512]{2,1,0:T(8,128)}, f32[4,128,512]{2,1,0:T(8,128)S(1)}, u32[]{:S(2)}) copy-start(f32[4,128,512]{2,1,0:T(8,128)S(1)} %get-tuple-element.29.w_ref) | copy-start | bytes 3145732
  25.1 1.0 %copy-start.7 = (f32[4,128,512]{2,1,0:T(8,128)}, f32[4,128,512]{2,1,0:T(8,128)S(1)}, u32[]{:S(2)}) copy-start(f32[4,128,512]{2,1,0:T(8,128)S(1)} %get-tuple-element.26.local_ref) | copy-start | bytes 3145732
  26.0 2.4 %copy-start.11 = (f32[1,128,512]{2,1,0:T(8,128)}, f32[1,128,512]{2,1,0:T(8,128)S(1)}, u32[]{:S(2)}) copy-start(f32[1,128,512]{2,1,0:T(8,128)S(1)} %get-tuple-element.27) | copy-start | bytes 786436
  26.0 1.6 %collective-permute-start.2 = (f32[136,512]{1,0:T(8,128)S(1)}, f32[136,512]{1,0:T(8,128)S(1)}, u32[]{:S(2)}, u32[]{:S(2)}) collective-permute-start(f32[136,512]{1,0:T(8,128)S(1)} %get-tuple-element.25.own_ref), channel_id=1, source_target_pairs={{0,1},{1,0},{2,3},{3,2},{4,5},{5,4},{6,7},{7,6},{8,9},{9,8},{10,11... | collective-permute-start | bytes 835592 | tf_op jit(solution)/shard_map/ppermute | solution.py:417
  28.4 11.1 %all-to-all-start.1 = ((f32[288,1,128]{2,1,0:T(1,128)}), f32[288,1,128]{2,1,0:T(1,128)S(1)}, u32[]{:S(2)}, u32[]{:S(2)}) async-start(f32[288,1,128]{2,1,0:T(1,128)} %bitcast.6), calls=%async_computation.1 | async-start | bytes 294912 | tf_op jit(solution)/shard_map/all_to_all | solution.py:395
  31.0 8.7 %collective-permute-start.3 = (f32[1,128,512]{2,1,0:T(8,128)}, f32[1,128,512]{2,1,0:T(8,128)}, u32[]{:S(2)}, u32[]{:S(2)}) collective-permute-start(f32[1,128,512]{2,1,0:T(8,128)} %copy-done.11), channel_id=1, source_target_pairs={{1,2},{3,4},{5,6},{7,8},{9,10},{11,12},{13,14},{15,16},{17,18},{19... | collective-permute-start | bytes 786440 | tf_op jit(solution)/shard_map/ppermute | solution.py:418
  39.6 1.2 %copy-start.1 = (f32[4,128,512]{2,1,0:T(8,128)S(1)}, f32[4,128,512]{2,1,0:T(8,128)}, u32[]{:S(2)}) copy-start(f32[4,128,512]{2,1,0:T(8,128)} %copy-done) | copy-start | bytes 3145732
  40.9 1.2 %copy-start.3 = (f32[4,128,512]{2,1,0:T(8,128)S(1)}, f32[4,128,512]{2,1,0:T(8,128)}, u32[]{:S(2)}) copy-start(f32[4,128,512]{2,1,0:T(8,128)} %sigma_ref.3) | copy-start | bytes 3145732
  42.1 1.2 %copy-start.5 = (f32[4,128,512]{2,1,0:T(8,128)S(1)}, f32[4,128,512]{2,1,0:T(8,128)}, u32[]{:S(2)}) copy-start(f32[4,128,512]{2,1,0:T(8,128)} %wind_ref.3) | copy-start | bytes 3145732
  43.3 1.2 %copy-start.8 = (f32[4,128,512]{2,1,0:T(8,128)S(1)}, f32[4,128,512]{2,1,0:T(8,128)}, u32[]{:S(2)}) copy-start(f32[4,128,512]{2,1,0:T(8,128)} %copy-done.7) | copy-start | bytes 3145732

commit v7 on v6

--- a/solution.py
+++ b/solution.py
@@ -15,6 +15,7 @@
 NT = (((1,), (1,)), ((), ()))
 TN = (((0,), (0,)), ((), ()))
 CHUNK = 16
+STEP = 2
 FIRST_LIMIT = 50
 
 
@@ -206,7 +207,7 @@
     r_hbm, inv_hbm, local_ref, summed_ref, odd_ref, high_ref, low_ref, rr_ref, r_ref,
     inv_ref, sems
 ):
-    layers, _, nz = r_ref.shape
+    layers, ny, nz = r_ref.shape
     half = nz // 2
     moves = [(inv_hbm.at[0, :half], inv_ref.at[:half])]
     moves += [(r_hbm.at[x], r_ref.at[x]) for x in range(layers)]
@@ -218,19 +219,23 @@
     upper = halves(inv_ref[:half])
     high_ref[:half], low_ref[:half] = upper
     total = jnp.zeros((8, LANES), F32)
-    for x in range(layers):
-        loads[x + 1].wait()
-        local_ref[x] = dot3(halves(r_ref[x, :, :half]), upper)
-        for j in range(tiles_of(r_ref)):
-            r = r_ref[x, :, columns(j)]
-            total = total + rows_sum(r * r)
-            summed_ref[:, columns(j)] = r if x == 0 else summed_ref[:, columns(j)] + r
+    for x in range(0, layers, STEP):
+        for load in loads[x + 1 : x + 1 + STEP]:
+            load.wait()
+        lines = r_ref[x : x + STEP, :, :half].reshape(STEP * ny, half)
+        local_ref[x : x + STEP] = dot3(halves(lines), upper).reshape(STEP, ny, nz)
+        for y in range(x, x + STEP):
+            for j in range(tiles_of(r_ref)):
+                r = r_ref[y, :, columns(j)]
+                total = total + rows_sum(r * r)
+                summed_ref[:, columns(j)] = r if y == 0 else summed_ref[:, columns(j)] + r
     rr_ref[:8] = total
     loads[layers + 1].wait()
     lower = halves(inv_ref[half:])
     high_ref[half:], low_ref[half:] = lower
-    for x in range(layers):
-        local_ref[x] += dot3(halves(r_ref[x, :, half:]), lower)
+    for x in range(0, layers, STEP):
+        lines = r_ref[x : x + STEP, :, half:].reshape(STEP * ny, half)
+        local_ref[x : x + STEP] += dot3(halves(lines), lower).reshape(STEP, ny, nz)
     odd_ref[0] = local_ref[jnp.where(even_here(), 0, layers - 1)]
 
 

time: 63.7 us -> 63.6 us (level)
  no operation moved by 1% of the time
where the time goes in v7:
time: 63.6 us; the launch traced here: 63.2 us
  blocking collectives  30.9 us (49%)
  Pallas kernels  10.2 us (16%)
  waiting for transfers between devices  9.01 us (14%)
  local copies, waits for them, and re-layouts  6.97 us (11%)
  starting transfers between devices  5.35 us (8%)
  between operations  0.75 us (1%)
    all_to_all x2, blocking collectives, exchange(): return lax.all_to_all(block, AXIS, 0, 0, tiled=True)  30.9 us
    pallas_call x9, Pallas kernels, call(): pl.pallas_call(kernel, out_shape=outs, in_specs=[far if i in hbm else vme...  10.2 us
    all_to_all x1, waiting for transfers between devices, exchange(): return lax.all_to_all(block, AXIS, 0, 0, tiled=True)  7.15 us
    unnamed x24, local copies, waits for them, and re-layouts  6.97 us
    all_to_all x1, starting transfers between devices, exchange(): return lax.all_to_all(block, AXIS, 0, 0, tiled=True)  2.58 us
    ppermute x2, starting transfers between devices, round_of(): odd = lax.ppermute(odd, AXIS, others)  2.03 us
    ppermute x2, waiting for transfers between devices, round_of(): got = lax.ppermute(sent, AXIS, pairs)  1.86 us
  transfers between devices with their start and end apart: 5, of which 3 were waited for; matrix products, arithmetic and copies ran while one was open for 0% of the time, Pallas kernels for 1%

profile of v7, /device:TPU:0, one launch (start us, length us, event | category | flops | bytes accessed | tf_op | source)
XLA Modules:
  0.0 63.2 jit_solution(783878525889051243)
XLA Ops:
  0.6 0.0 copy-start.6
  0.6 0.0 copy-start.10
  0.7 2.5 %shard_map.86 = (f32[4,128,512]{2,1,0:T(8,128)S(1)}, f32[128,512]{1,0:T(8,128)S(1)}, f32[1,128,512]{2,1,0:T(8,128)S(1)}, bf16[512,512]{1,0:T(8,128)(2,1)S(1)}, b...) custom-call(f32[4,128,512]{2,1,0:T(8,128)} %r_hbm.1, f32[1,512,512]{2,1,0:T(8,128)} %inv_hbm.1), custom_call_target="tpu_custom_call" | custom-call | flops 805306368 | tf_op jit(solution)/shard_map/pallas_call | solution.py:388
  3.2 0.0 copy-start.9
  3.2 0.0 copy-start.2
  3.2 0.0 copy-start.4
  3.2 0.0 copy-done.6
  3.2 0.0 copy-done.10
  3.2 0.4 shard_map.87.own_ref
  3.6 0.5 collective-permute-start
  4.2 0.7 %collective-permute-start.1 = (f32[1,128,512]{2,1,0:T(8,128)S(1)}, f32[1,128,512]{2,1,0:T(8,128)S(1)}, u32[]{:S(2)}, u32[]{:S(2)}) collective-permute-start(f32[1,128,512]{2,1,0:T(8,128)S(1)} %get-tuple-element.20), channel_id=1, source_target_pairs={{1,2},{3,4},{5,6},{7,8},{9,10},{11,12},{13,14},{15,16},{17,18},{19... | collective-permute-start | bytes 786440 | tf_op jit(solution)/shard_map/ppermute | solution.py:423
  4.8 0.5 collective-permute-done.got_ref.even_ref
  5.4 16.2 %all_to_all.21 = f32[256,1,128]{2,1,0:T(1,128)S(1)} all-to-all(f32[256,1,128]{2,1,0:T(1,128)S(1)} %bitcast.20), channel_id=1, replica_groups=mesh['sub'=32] {'sub'}, dimensions={0} | all-to-all | bytes 262144 | tf_op jit(solution)/shard_map/all_to_all | solution.py:400
  21.6 0.0 copy-done.9
  21.6 0.2 shard_map.89.coarse_ref
  21.8 0.0 collective-permute-done.1.odd_ref
  21.8 0.0 copy-done.2
  21.8 0.0 copy-done.4
  21.8 2.1 %shard_map.90 = (f32[6,4,144,128]{3,2,1,0:T(8,128)S(1)}, f32[4,128,512]{2,1,0:T(8,128)S(1)}, f32[136,512]{1,0:T(8,128)S(1)}, f32[4,128,512]{2,1,0:T(8,128)S(1)}, f32[1,128,512]{2,1,0:T(8,128)S(1)}) custom-call(f32[96,128]{1,0:T(8,128)S(1)} %shard_map.89.coarse_ref, f32[4,128,512]{2,1,0:T(8,128)S(1)} %get-tuple-element.19.local_ref, ...), custom_call_target="tpu_custom_call" | custom-call | flops 1610612736 | tf_op jit(solution)/shard_map/pallas_call | solution.py:388
  23.9 0.0 copy-start
  23.9 1.1 %copy-done = f32[4,128,512]{2,1,0:T(8,128)} copy-done((f32[4,128,512]{2,1,0:T(8,128)}, f32[4,128,512]{2,1,0:T(8,128)S(1)}, u32[]{:S(2)}) %copy-start) | copy-done | bytes 1048600
  25.0 0.0 copy-start.7
  25.0 1.0 %copy-done.7 = f32[4,128,512]{2,1,0:T(8,128)} copy-done((f32[4,128,512]{2,1,0:T(8,128)}, f32[4,128,512]{2,1,0:T(8,128)S(1)}, u32[]{:S(2)}) %copy-start.7) | copy-done | bytes 1048600
  25.9 0.0 copy-start.11
  25.9 0.2 collective-permute-start.2
  26.1 1.3 %collective-permute-done.2.got_ref.even_ref = f32[136,512]{1,0:T(8,128)S(1)} collective-permute-done((f32[136,512]{1,0:T(8,128)S(1)}, f32[136,512]{1,0:T(8,128)S(1)}, u32[]{:S(2)}, u32[]{:S(2)}) %collective-permute-start.2) | collective-permute-done | bytes 278560 | tf_op jit(solution)/shard_map/ppermute | solution.py:422
  27.5 0.8 %shard_map.91 = f32[288,128]{1,0:T(8,128)} custom-call(f32[136,512]{1,0:T(8,128)S(1)} %collective-permute-done.2.got_ref.even_ref, f32[136,512]{1,0:T(8,128)S(1)} %get-tuple-element.25.own_ref), custom_call_target="tpu_custom_call" | custom-call | flops 50331648 | tf_op jit(solution)/shard_map/pallas_call | solution.py:388
  28.3 0.0 copy-done.11
  28.3 2.6 %all-to-all-start.1 = ((f32[288,1,128]{2,1,0:T(1,128)}), f32[288,1,128]{2,1,0:T(1,128)S(1)}, u32[]{:S(2)}, u32[]{:S(2)}) async-start(f32[288,1,128]{2,1,0:T(1,128)} %bitcast.6), calls=%async_computation.1 | async-start | bytes 294912 | tf_op jit(solution)/shard_map/all_to_all | solution.py:400
  30.9 1.4 %collective-permute-start.3 = (f32[1,128,512]{2,1,0:T(8,128)}, f32[1,128,512]{2,1,0:T(8,128)}, u32[]{:S(2)}, u32[]{:S(2)}) collective-permute-start(f32[1,128,512]{2,1,0:T(8,128)} %copy-done.11), channel_id=1, source_target_pairs={{1,2},{3,4},{5,6},{7,8},{9,10},{11,12},{13,14},{15,16},{17,18},{19... | collective-permute-start | bytes 786440 | tf_op jit(solution)/shard_map/ppermute | solution.py:423
  32.2 7.1 %all-to-all-done.1 = f32[288,1,128]{2,1,0:T(1,128)S(1)} async-done(((f32[288,1,128]{2,1,0:T(1,128)}), f32[288,1,128]{2,1,0:T(1,128)S(1)}, u32[]{:S(2)}, u32[]{:S(2)}) %all-to-all-start.1) | async-done | bytes 147488 | tf_op jit(solution)/shard_map/all_to_all | solution.py:400
  39.4 0.2 shard_map.92.coarse_ref
  39.5 0.0 collective-permute-done.3.odd_ref
  39.5 0.0 copy-start.1
  39.5 1.2 %copy-done.1 = f32[4,128,512]{2,1,0:T(8,128)S(1)} copy-done((f32[4,128,512]{2,1,0:T(8,128)S(1)}, f32[4,128,512]{2,1,0:T(8,128)}, u32[]{:S(2)}) %copy-start.1) | copy-done | bytes 1048600
  40.8 0.0 copy-start.3
  40.8 1.2 %copy-done.3 = f32[4,128,512]{2,1,0:T(8,128)S(1)} copy-done((f32[4,128,512]{2,1,0:T(8,128)S(1)}, f32[4,128,512]{2,1,0:T(8,128)}, u32[]{:S(2)}) %copy-start.3) | copy-done | bytes 1048600
  42.0 0.0 copy-start.5
  42.0 1.2 %copy-done.5 = f32[4,128,512]{2,1,0:T(8,128)S(1)} copy-done((f32[4,128,512]{2,1,0:T(8,128)S(1)}, f32[4,128,512]{2,1,0:T(8,128)}, u32[]{:S(2)}) %copy-start.5) | copy-done | bytes 1048600
  43.2 0.0 copy-start.8
  43.2 1.2 %copy-done.8 = f32[4,128,512]{2,1,0:T(8,128)S(1)} copy-done((f32[4,128,512]{2,1,0:T(8,128)S(1)}, f32[4,128,512]{2,1,0:T(8,128)}, u32[]{:S(2)}) %copy-start.8) | copy-done | bytes 1048600
  44.4 2.4 %shard_map.93 = (f32[6,4,144,128]{3,2,1,0:T(8,128)S(1)}, f32[4,128,512]{2,1,0:T(8,128)S(1)}, f32[32,128]{1,0:T(8,128)S(1)}, f32[32,128]{1,0:T(8,128)S(1)}) custom-call(f32[288,128]{1,0:T(8,128)S(1)} %bitcast.15, f32[96,128]{1,0:T(8,128)S(1)} %shard_map.92.coarse_ref, f32[4,128,512]{2,1,0:T(8,128)S(1)} %copy-done.8, ...), custom_call_target="tpu_custom_call" | custom-call | flops 805306368 | tf_op jit(solution)/shard_map/pallas_call | solution.py:388
  46.9 14.7 %all_to_all.22 = f32[32,1,128]{2,1,0:T(1,128)S(1)} all-to-all(f32[32,1,128]{2,1,0:T(1,128)S(1)} %bitcast.25), channel_id=1, replica_groups=mesh['sub'=32] {'sub'}, dimensions={0} | all-to-all | bytes 32768 | tf_op jit(solution)/shard_map/all_to_all | solution.py:400
  61.6 1.6 %shard_map.94 = (f32[4,128,512]{2,1,0:T(8,128)}, f32[4,128,512]{2,1,0:T(8,128)}) custom-call(f32[32,128]{1,0:T(8,128)S(1)} %bitcast.24, f32[32,128]{1,0:T(8,128)S(1)} %get-tuple-element.31.known_ref, f32[4,128,512]{2,1,0:T(8,128)S(1)} %get-tuple-element.21.r_ref, f32[6,4,144,128]{3,2,1,0:T(8,128)S(1)} %get-tuple-element.28.z_ref, ...), custom_call_target="tpu_custom_call" | custom-call | flops 100663296 | tf_op jit(solution)/shard_map/pallas_call | solution.py:388
  (1 shorter events, 0.0 us)
Async XLA Ops:
  0.6 2.6 %copy-start.6 = (f32[512,64]{0,1:T(8,128)S(1)}, f32[512,64]{0,1:T(8,128)}, u32[]{:S(2)}) copy-start(f32[512,64]{0,1:T(8,128)} %param.12) | copy-start | bytes 393220
  0.6 2.6 %copy-start.10 = (f32[128,32]{0,1:T(8,128)S(1)}, f32[128,32]{0,1:T(8,128)}, u32[]{:S(2)}) copy-start(f32[128,32]{0,1:T(8,128)} %param.11) | copy-start | bytes 49156
  3.2 18.4 %copy-start.9 = (f32[5,32,64]{2,1,0:T(8,128)S(1)}, f32[5,32,64]{2,1,0:T(8,128)}, u32[]{:S(2)}) copy-start(f32[5,32,64]{2,1,0:T(8,128)} %gamma_ref.3) | copy-start | bytes 122884
  3.2 18.6 %copy-start.2 = (f32[4,128,512]{2,1,0:T(8,128)S(1)}, f32[4,128,512]{2,1,0:T(8,128)}, u32[]{:S(2)}) copy-start(f32[4,128,512]{2,1,0:T(8,128)} %sigma_ref.3) | copy-start | bytes 3145732
  3.2 18.6 %copy-start.4 = (f32[4,128,512]{2,1,0:T(8,128)S(1)}, f32[4,128,512]{2,1,0:T(8,128)}, u32[]{:S(2)}) copy-start(f32[4,128,512]{2,1,0:T(8,128)} %wind_ref.3) | copy-start | bytes 3145732
  3.6 1.7 %collective-permute-start = (f32[136,512]{1,0:T(8,128)S(1)}, f32[136,512]{1,0:T(8,128)S(1)}, u32[]{:S(2)}, u32[]{:S(2)}) collective-permute-start(f32[136,512]{1,0:T(8,128)S(1)} %shard_map.87.own_ref), channel_id=1, source_target_pairs={{0,1},{1,0},{2,3},{3,2},{4,5},{5,4},{6,7},{7,6},{8,9},{9,8},{10,11... | collective-permute-start | bytes 835592 | tf_op jit(solution)/shard_map/ppermute | solution.py:422
  4.2 17.6 %collective-permute-start.1 = (f32[1,128,512]{2,1,0:T(8,128)S(1)}, f32[1,128,512]{2,1,0:T(8,128)S(1)}, u32[]{:S(2)}, u32[]{:S(2)}) collective-permute-start(f32[1,128,512]{2,1,0:T(8,128)S(1)} %get-tuple-element.20), channel_id=1, source_target_pairs={{1,2},{3,4},{5,6},{7,8},{9,10},{11,12},{13,14},{15,16},{17,18},{19... | collective-permute-start | bytes 786440 | tf_op jit(solution)/shard_map/ppermute | solution.py:423
  23.9 1.1 %copy-start = (f32[4,128,512]{2,1,0:T(8,128)}, f32[4,128,512]{2,1,0:T(8,128)S(1)}, u32[]{:S(2)}) copy-start(f32[4,128,512]{2,1,0:T(8,128)S(1)} %get-tuple-element.29.w_ref) | copy-start | bytes 3145732
  25.0 1.0 %copy-start.7 = (f32[4,128,512]{2,1,0:T(8,128)}, f32[4,128,512]{2,1,0:T(8,128)S(1)}, u32[]{:S(2)}) copy-start(f32[4,128,512]{2,1,0:T(8,128)S(1)} %get-tuple-element.26.local_ref) | copy-start | bytes 3145732
  25.9 2.4 %copy-start.11 = (f32[1,128,512]{2,1,0:T(8,128)}, f32[1,128,512]{2,1,0:T(8,128)S(1)}, u32[]{:S(2)}) copy-start(f32[1,128,512]{2,1,0:T(8,128)S(1)} %get-tuple-element.27) | copy-start | bytes 786436
  25.9 1.6 %collective-permute-start.2 = (f32[136,512]{1,0:T(8,128)S(1)}, f32[136,512]{1,0:T(8,128)S(1)}, u32[]{:S(2)}, u32[]{:S(2)}) collective-permute-start(f32[136,512]{1,0:T(8,128)S(1)} %get-tuple-element.25.own_ref), channel_id=1, source_target_pairs={{0,1},{1,0},{2,3},{3,2},{4,5},{5,4},{6,7},{7,6},{8,9},{9,8},{10,11... | collective-permute-start | bytes 835592 | tf_op jit(solution)/shard_map/ppermute | solution.py:422
  28.3 11.1 %all-to-all-start.1 = ((f32[288,1,128]{2,1,0:T(1,128)}), f32[288,1,128]{2,1,0:T(1,128)S(1)}, u32[]{:S(2)}, u32[]{:S(2)}) async-start(f32[288,1,128]{2,1,0:T(1,128)} %bitcast.6), calls=%async_computation.1 | async-start | bytes 294912 | tf_op jit(solution)/shard_map/all_to_all | solution.py:400
  30.9 8.7 %collective-permute-start.3 = (f32[1,128,512]{2,1,0:T(8,128)}, f32[1,128,512]{2,1,0:T(8,128)}, u32[]{:S(2)}, u32[]{:S(2)}) collective-permute-start(f32[1,128,512]{2,1,0:T(8,128)} %copy-done.11), channel_id=1, source_target_pairs={{1,2},{3,4},{5,6},{7,8},{9,10},{11,12},{13,14},{15,16},{17,18},{19... | collective-permute-start | bytes 786440 | tf_op jit(solution)/shard_map/ppermute | solution.py:423
  39.5 1.2 %copy-start.1 = (f32[4,128,512]{2,1,0:T(8,128)S(1)}, f32[4,128,512]{2,1,0:T(8,128)}, u32[]{:S(2)}) copy-start(f32[4,128,512]{2,1,0:T(8,128)} %copy-done) | copy-start | bytes 3145732
  40.8 1.2 %copy-start.3 = (f32[4,128,512]{2,1,0:T(8,128)S(1)}, f32[4,128,512]{2,1,0:T(8,128)}, u32[]{:S(2)}) copy-start(f32[4,128,512]{2,1,0:T(8,128)} %sigma_ref.3) | copy-start | bytes 3145732
  42.0 1.2 %copy-start.5 = (f32[4,128,512]{2,1,0:T(8,128)S(1)}, f32[4,128,512]{2,1,0:T(8,128)}, u32[]{:S(2)}) copy-start(f32[4,128,512]{2,1,0:T(8,128)} %wind_ref.3) | copy-start | bytes 3145732
  43.2 1.2 %copy-start.8 = (f32[4,128,512]{2,1,0:T(8,128)S(1)}, f32[4,128,512]{2,1,0:T(8,128)}, u32[]{:S(2)}) copy-start(f32[4,128,512]{2,1,0:T(8,128)} %copy-done.7) | copy-start | bytes 3145732
